TPU v7x, 32 devices: a whole 2x2x4 slice. The times are simulated.
32 devices in a mesh: dp: 32 (over z, y, x, core).
Axes of the slice: x: 2, y: 2, z: 4, core: 2. Of those that a mesh axis runs over, the one named last changes fastest.
Arguments:
- w_in0: float32 [128, 64], replicated
- w_short: float32 [128, 256], replicated
- w_in: float32 [17, 256, 64], replicated
- w_mid: float32 [18, 3, 3, 64, 64], replicated
- w_out: float32 [18, 64, 256], replicated
- w_fc: float32 [256, 100], replicated
- w_bn: float32 [14336], replicated
- w_bias: float32 [100], replicated
- g_in0: float32 [32, 128, 64], P('dp')
- g_short: float32 [32, 128, 256], P('dp')
- g_in: float32 [32, 17, 256, 64], P('dp')
- g_mid: float32 [32, 18, 3, 3, 64, 64], P('dp')
- g_out: float32 [32, 18, 64, 256], P('dp')
- g_bn: float32 [32, 14336], P('dp')
- pooled: bfloat16 [32768, 256], P('dp')
- dlogits: bfloat16 [32768, 100], P('dp')
- v_in0: float32 [8192], P('dp')
- v_short: float32 [32768], P('dp')
- v_in: float32 [17, 16384], P(None, 'dp')
- v_mid: float32 [18, 36864], P(None, 'dp')
- v_out: float32 [18, 16384], P(None, 'dp')
- v_fc: float32 [25600], P('dp')
- v_bn: float32 [14336], P('dp')
- v_bias: float32 [128], P('dp')
- learn_rate: float32 [], replicated
Outputs:
- output 1: float32 [128, 64], replicated
- output 2: float32 [128, 256], replicated
- output 3: float32 [17, 256, 64], replicated
- output 4: float32 [18, 3, 3, 64, 64], replicated
- output 5: float32 [18, 64, 256], replicated
- output 6: float32 [256, 100], replicated
- output 7: float32 [14336], replicated
- output 8: float32 [100], replicated
- output 9: bfloat16 [128, 64], replicated
- output 10: bfloat16 [128, 256], replicated
- output 11: bfloat16 [17, 256, 64], replicated
- output 12: bfloat16 [18, 3, 3, 64, 64], replicated
- output 13: bfloat16 [18, 64, 256], replicated
- output 14: bfloat16 [256, 100], replicated
- output 15: float32 [8192], P('dp')
- output 16: float32 [32768], P('dp')
- output 17: float32 [17, 16384], P(None, 'dp')
- output 18: float32 [18, 36864], P(None, 'dp')
- output 19: float32 [18, 16384], P(None, 'dp')
- output 20: float32 [25600], P('dp')
- output 21: float32 [14336], P('dp')
- output 22: float32 [128], P('dp')
All inputs are finite; a program needn't handle non-finite values.
Results may differ from a plain program's by a relative error of at most 0.001.
Values sent between devices are 32-bit elements.
A program may use at most 1 GiB of HBM per device.

v0:
```python
import jax
import jax.numpy as jnp
from jax import lax
from jax.sharding import PartitionSpec as P

MOMENTUM = 0.9
TRUST_COEF = 0.001
DECAY = 0.0001


def trust_factor(sq_w, sq_g):
    w_norm = jnp.sqrt(sq_w)
    g_norm = jnp.sqrt(sq_g)
    return jnp.where((w_norm > 0) & (g_norm > 0), TRUST_COEF * w_norm / (g_norm + DECAY * w_norm), 1.0)


def solution(mesh):
    n_dev = mesh.shape['dp']
    spec_full = P()
    spec_lead = P('dp')
    spec_cols = P(None, 'dp')
    moment_specs = (spec_lead, spec_lead, spec_cols, spec_cols, spec_cols, spec_lead, spec_lead, spec_lead)
    in_specs = (spec_full,) * 8 + (spec_lead,) * 8 + moment_specs + (spec_full,)
    out_specs = (spec_full,) * 14 + moment_specs

    def body(w_in0, w_short, w_in, w_mid, w_out, w_fc, w_bn, w_bias,
             g_in0, g_short, g_in, g_mid, g_out, g_bn, pooled, dlogits,
             v_in0, v_short, v_in, v_mid, v_out, v_fc, v_bn, v_bias, learn_rate):
        rank = lax.axis_index('dp')
        rows = pooled.shape[0] * n_dev
        classes = w_bias.shape[0]
        bias_width = v_bias.shape[0]
        bias_pad = bias_width * n_dev
        bn_width = v_bn.shape[0]
        fc_local = lax.dot_general(pooled, dlogits, (((0,), (0,)), ((), ())),
                                   preferred_element_type=jnp.float32)
        bias_local = jnp.sum(dlogits, axis=0, dtype=jnp.float32)
        weights = [w_in0, w_short, w_in, w_mid, w_out, w_fc]
        moments = [v_in0, v_short, v_in, v_mid, v_out, v_fc]
        local_grads = [g_in0, g_short, g_in, g_mid, g_out, fc_local]
        divisors = [n_dev] * 5 + [rows]
        w_parts = []
        g_parts = []
        squares = []
        for weight, moment, gradient, divisor in zip(weights, moments, local_grads, divisors):
            moment_2d = moment.reshape(-1, moment.shape[-1])
            count, width = moment_2d.shape
            w_flat = weight.reshape(count, -1)
            w_part = lax.dynamic_slice_in_dim(w_flat, rank * width, width, axis=1)
            g_part = lax.psum_scatter(gradient.reshape(count, -1), 'dp', scatter_dimension=1, tiled=True) / divisor
            w_parts.append(w_part)
            g_parts.append(g_part)
            squares.append(jnp.sum(w_part * w_part, axis=1))
            squares.append(jnp.sum(g_part * g_part, axis=1))
        bn_grad = lax.psum_scatter(g_bn.reshape(-1), 'dp', scatter_dimension=0, tiled=True) / n_dev
        bias_grad = lax.psum_scatter(jnp.pad(bias_local, (0, bias_pad - classes)), 'dp',
                                     scatter_dimension=0, tiled=True) / rows
        sq_total = lax.psum(jnp.concatenate(squares), 'dp')
        offset = 0
        kernels_new = []
        kernels_bf = []
        moments_new = []
        for weight, moment, w_part, g_part in zip(weights, moments, w_parts, g_parts):
            count = w_part.shape[0]
            trust = trust_factor(sq_total[offset:offset + count], sq_total[offset + count:offset + 2 * count])[:, None]
            offset += 2 * count
            moment_next = MOMENTUM * moment.reshape(w_part.shape) + learn_rate * trust * (g_part + DECAY * w_part)
            w_full = lax.all_gather(w_part - moment_next, 'dp', axis=1, tiled=True).reshape(weight.shape)
            kernels_new.append(w_full)
            kernels_bf.append(w_full.astype(jnp.bfloat16))
            moments_new.append(moment_next.reshape(moment.shape))
        bn_moment = MOMENTUM * v_bn + learn_rate * bn_grad
        bn_part = lax.dynamic_slice_in_dim(w_bn, rank * bn_width, bn_width) - bn_moment
        bn_full = lax.all_gather(bn_part, 'dp', axis=0, tiled=True)
        bias_moment = MOMENTUM * v_bias + learn_rate * bias_grad
        w_bias_pad = jnp.pad(w_bias, (0, bias_pad - classes))
        bias_part = lax.dynamic_slice_in_dim(w_bias_pad, rank * bias_width, bias_width) - bias_moment
        bias_full = lax.all_gather(bias_part, 'dp', axis=0, tiled=True)[:classes]
        return (tuple(kernels_new) + (bn_full, bias_full) + tuple(kernels_bf)
                + tuple(moments_new) + (bn_moment, bias_moment))

    return jax.shard_map(body, mesh=mesh, in_specs=in_specs, out_specs=out_specs, check_vma=False)
```

profile of v0, /device:TPU:0, one launch (start us, length us, event | category | flops | bytes accessed | tf_op | source)
XLA Modules:
  0.0 1249.5 jit_solution(4643942059519128717)
XLA Ops:
  7.3 0.9 copy.62
  8.2 5.5 reshape.169
  13.8 0.8 copy-done.4
  15.0 6.3 reshape.171
  21.3 0.8 copy-done.7
  22.3 8.2 copy.82
  30.5 11.2 bitcast_bitcast_fusion
  41.8 1.8 copy.64
  43.6 1.9 reshape.139
  45.6 1.2 copy-done.2
  47.0 2.1 copy.84
  49.2 5.6 reshape.141
  54.9 0.7 copy-done.14
  56.6 1.8 copy.63
  58.4 1.9 reshape.138
  60.3 5.7 reshape.140
  66.3 0.9 copy.83
  68.3 0.7 multiply_reduce_fusion.9
  69.6 0.9 multiply_reduce_fusion.5
  70.6 1.0 multiply_reduce_fusion.1
  71.7 43.0 %all-reduce.8 = (f32[14336]{0:T(1024)S(1)}, f32[128]{0:T(128)S(1)}) all-reduce(f32[14336]{0:T(1024)S(1)} %bitcast.73, f32[128]{0:T(128)S(1)} %pad.8), channel_id=8, replica_groups=mesh['dp'=32] {'dp'}, use_global_device_ids=true, to_apply=%region_19.0.clone | all-reduce | flops 14464 | bytes 115712
  115.3 1.4 subtract_dynamic-update-slice_fusion
  116.8 42.3 %reduce-scatter.19.cloned.1.call-done = f32[256,1]{1,0:T(8,128)} async-done(((f32[8192,1]{1,0:T(8,128)}), f32[256,1]{1,0:T(8,128)}) %reduce-scatter.19.cloned.1.call-update) | async-done | bytes 1040
  159.0 1.0 copy.75
  160.6 153.3 %reduce-scatter.23.cloned.1.call-done = f32[800,1]{1,0:T(8,128)} async-done(((f32[25600,1]{1,0:T(8,128)}), f32[800,1]{1,0:T(8,128)}) %reduce-scatter.23.cloned.1.call-update) | async-done | bytes 3216
  313.9 1.2 copy.79
  315.1 0.6 multiply_reduce_fusion.8
  315.7 181.7 %reduce-scatter.21.cloned.1.call-done = f32[1024,1]{1,0:T(8,128)} async-done(((f32[32768,1]{1,0:T(8,128)}), f32[1024,1]{1,0:T(8,128)}) %reduce-scatter.21.cloned.1.call-update) | async-done | bytes 4112
  497.5 1.2 copy.77
  499.3 139.6 %reduce-scatter.13.cloned.1.call-done = f32[17,512]{1,0:T(8,128)} async-done(((f32[17,16384]{1,0:T(8,128)}), f32[17,512]{1,0:T(8,128)}) %reduce-scatter.13.cloned.1.call-update) | async-done | bytes 34832 | tf_op jit(solution)/shard_map/reduce_scatter | solution.py:50
  639.0 0.9 multiply_reduce_fusion.4
  639.9 134.6 %reduce-scatter.17.cloned.1.call-done = f32[18,512]{1,0:T(8,128)} async-done(((f32[18,16384]{1,0:T(8,128)}), f32[18,512]{1,0:T(8,128)}) %reduce-scatter.17.cloned.1.call-update) | async-done | bytes 36880 | tf_op jit(solution)/shard_map/reduce_scatter | solution.py:50
  774.5 0.9 multiply_reduce_fusion.2
  775.4 103.7 %reduce-scatter.15.cloned.1.call-done = f32[18,1152]{1,0:T(8,128)} async-done(((f32[18,36864]{1,0:T(8,128)}), f32[18,1152]{1,0:T(8,128)}) %reduce-scatter.15.cloned.1.call-update) | async-done | bytes 82960 | tf_op jit(solution)/shard_map/reduce_scatter | solution.py:50
  879.1 1.0 multiply_reduce_fusion
  880.1 4.0 concatenate.3
  884.0 41.0 %all-reduce.7 = (f32[112]{0:T(128)S(1)}, f32[14336]{0:T(1024)}, f32[128]{0:T(128)}) all-reduce(f32[112]{0:T(128)S(1)} %concatenate.3, f32[14336]{0:T(1024)S(1)} %get-tuple-element.87, f32[128]{0:T(128)S(1)} %get-tuple-element.85), channel_id=1, replica_groups=mesh['dp'=32] {'dp'}, use_global_device_ids=true, to_apply=%region_18.0 | all-reduce | flops 14576 | bytes 116608 | tf_op jit(solution)/shard_map/psum | solution.py:58
  927.2 0.7 fusion.7
  928.2 0.6 copy-done.6
  928.9 1.5 dynamic-slice_subtract_fusion.2
  930.7 1.5 dynamic-slice_subtract_fusion.1
  932.3 1.7 dynamic-slice_subtract_fusion
  936.8 39.6 %all_gather.24 = f32[1,8192]{1,0:T(1,128)S(1)} all-gather(f32[1,256]{1,0:T(1,128)S(1)} %get-tuple-element.83), channel_id=1, replica_groups=mesh['dp'=32] {'dp'}, dimensions={1}, use_global_device_ids=true | all-gather | bytes 33792 | tf_op jit(solution)/shard_map/all_gather | solution.py:68
  976.9 0.7 reduce.15
  977.7 0.7 copy.67
  979.8 37.0 %all_gather.25 = f32[1,32768]{1,0:T(1,128)S(1)} all-gather(f32[1,1024]{1,0:T(1,128)S(1)} %get-tuple-element.81), channel_id=1, replica_groups=mesh['dp'=32] {'dp'}, dimensions={1}, use_global_device_ids=true | all-gather | bytes 135168 | tf_op jit(solution)/shard_map/all_gather | solution.py:68
  1016.8 0.9 reduce.16
  1017.8 0.7 copy.70
  1018.5 0.6 convert_element_type.26
  1019.1 36.4 %all-reduce.11.cloned.1.call-done = f32[25600]{0:T(1024)} async-done(((f32[25600]{0:T(1024)}), f32[25600]{0:T(1024)}) %all-reduce.11.cloned.1.call-update) | async-done | bytes 102416
  1055.5 1.1 reshape.151
  1056.6 0.7 copy.69
  1057.4 0.7 copy.72
  1058.2 54.6 %all-gather.4.cloned.1.call-done = f32[17,16384]{1,0:T(8,128)} async-done(((f32[17,512]{1,0:T(8,128)}), f32[17,16384]{1,0:T(8,128)}) %all-gather.4.cloned.1.call-update) | async-done | bytes 1114128 | tf_op jit(solution)/shard_map/all_gather | solution.py:68
  1112.7 2.2 reshape.148
  1115.0 1.7 copy.68
  1116.6 1.2 convert_element_type.27
  1117.8 2.2 copy.71
  1120.0 49.8 %all-gather.8.cloned.1.call-done = f32[18,16384]{1,0:T(8,128)} async-done(((f32[18,512]{1,0:T(8,128)}), f32[18,16384]{1,0:T(8,128)}) %all-gather.8.cloned.1.call-update) | async-done | bytes 1179664 | tf_op jit(solution)/shard_map/all_gather | solution.py:68
  1169.8 1.9 copy.85
  1171.8 1.4 fusion.8
  1173.1 59.4 %all-gather.6.cloned.1.call-done = f32[18,36864]{1,0:T(8,128)} async-done(((f32[18,1152]{1,0:T(8,128)}), f32[18,36864]{1,0:T(8,128)}) %all-gather.6.cloned.1.call-update) | async-done | bytes 2654224 | tf_op jit(solution)/shard_map/all_gather | solution.py:68
  1232.6 5.4 reshape.149
  1238.0 4.7 convert_element_type.28
  (91 shorter events, 8.4 us)
Async XLA Ops:
  7.2 6.6 copy-start
  7.2 151.8 %reduce-scatter.19.cloned.1.call-start = ((), (), s32[]{:S(2)}) async-start(), calls=%async_computation.13 | async-start | bytes 4325376
  13.7 0.9 copy-start.4
  13.7 300.2 %reduce-scatter.23.cloned.1.call-start = ((), (), s32[]{:S(2)}) async-start(), calls=%async_computation.15 | async-start | bytes 13516800
  21.2 0.9 copy-start.7
  21.2 476.2 %reduce-scatter.21.cloned.1.call-start = ((), (), s32[]{:S(2)}) async-start(), calls=%async_computation.14 | async-start | bytes 17301504
  41.8 597.2 %reduce-scatter.13.cloned.1.call-start = ((), (), s32[]{:S(2)}) async-start(), calls=%async_computation.6 | async-start | bytes 1622016 | tf_op jit(solution)/shard_map/reduce_scatter | solution.py:50
  45.6 1.3 copy-start.2
  45.6 728.9 %reduce-scatter.17.cloned.1.call-start = ((), (), s32[]{:S(2)}) async-start(), calls=%async_computation.8 | async-start | bytes 1622016 | tf_op jit(solution)/shard_map/reduce_scatter | solution.py:50
  49.1 829.9 %reduce-scatter.15.cloned.1.call-start = ((), (), s32[]{:S(2)}) async-start(), calls=%async_computation.7 | async-start | bytes 3649536 | tf_op jit(solution)/shard_map/reduce_scatter | solution.py:50
  54.8 0.8 copy-start.14
  54.8 1.6 copy-start.8
  54.8 1000.7 %all-reduce.11.cloned.1.call-start = ((), (), s32[]{:S(2)}) async-start(), calls=%async_computation.12 | async-start | bytes 204800
  60.3 5.7 copy-start.3
  66.2 1.0 copy-start.10
  66.2 5.5 copy-start.11
  66.2 48.5 %copy-start.19 = (f32[100]{0:T(128)S(1)}, f32[100]{0:T(128)}, u32[]{:S(2)}) copy-start(f32[100]{0:T(128)} %param.32) | copy-start | bytes 1204
  66.2 48.5 %copy-start.20 = (f32[4]{0:T(128)S(1)}, f32[4]{0:T(128)}, u32[]{:S(2)}) copy-start(f32[4]{0:T(128)} %param.48) | copy-start | bytes 52
  66.3 49.1 %copy-start.17 = (f32[448]{0:T(512)S(1)}, f32[448]{0:T(512)}, u32[]{:S(2)}) copy-start(f32[448]{0:T(512)} %param.47) | copy-start | bytes 5380
  66.3 50.5 %copy-start.15 = (f32[800]{0:T(1024)S(1)}, f32[800]{0:T(1024)}, u32[]{:S(2)}) copy-start(f32[800]{0:T(1024)} %param.46) | copy-start | bytes 9604
  67.2 861.7 %copy-start.12 = (f32[17,512]{1,0:T(8,128)S(1)}, f32[17,512]{1,0:T(8,128)}, u32[]{:S(2)}) copy-start(f32[17,512]{1,0:T(8,128)} %param.43) | copy-start | bytes 104452
  67.2 863.4 %copy-start.13 = (f32[18,512]{1,0:T(8,128)S(1)}, f32[18,512]{1,0:T(8,128)}, u32[]{:S(2)}) copy-start(f32[18,512]{1,0:T(8,128)} %param.45) | copy-start | bytes 110596
  67.3 864.9 %copy-start.9 = (f32[18,1152]{1,0:T(8,128)S(1)}, f32[18,1152]{1,0:T(8,128)}, u32[]{:S(2)}) copy-start(f32[18,1152]{1,0:T(8,128)} %param.44) | copy-start | bytes 248836
  71.7 862.4 %copy-start.18 = (f32[256]{0:T(256)S(1)}, f32[256]{0:T(256)}, u32[]{:S(2)}) copy-start(f32[256]{0:T(256)} %param.41) | copy-start | bytes 3076
  71.7 862.4 %copy-start.16 = (f32[1024]{0:T(1024)S(1)}, f32[1024]{0:T(1024)}, u32[]{:S(2)}) copy-start(f32[1024]{0:T(1024)} %param.42) | copy-start | bytes 12292
  928.2 0.6 copy-start.6
  928.9 183.9 %all-gather.4.cloned.1.call-start = ((), (), s32[]{:S(2)}) async-start(), calls=%async_computation.9 | async-start | bytes 1622016 | tf_op jit(solution)/shard_map/all_gather | solution.py:68
  930.5 239.3 %all-gather.8.cloned.1.call-start = ((), (), s32[]{:S(2)}) async-start(), calls=%async_computation.11 | async-start | bytes 1622016 | tf_op jit(solution)/shard_map/all_gather | solution.py:68
  932.2 300.3 %all-gather.6.cloned.1.call-start = ((), (), s32[]{:S(2)}) async-start(), calls=%async_computation.10 | async-start | bytes 3649536 | tf_op jit(solution)/shard_map/all_gather | solution.py:68
  1017.8 97.2 %copy-start.5 = (f32[128,256]{1,0:T(8,128)}, f32[128,256]{1,0:T(8,128)S(1)}, u32[]{:S(2)}) copy-start(f32[128,256]{1,0:T(8,128)S(1)} %reshape.147) | copy-start | bytes 393220
  1238.0 4.7 copy-start.1
Sparse Core Ops, SparseCore 0:
  13.8 145.1 reduce-scatter.18
  161.3 152.5 reduce-scatter.22
  316.2 181.1 reduce-scatter.20
  499.6 139.3 reduce-scatter.12
  641.0 133.3 reduce-scatter.16
  779.7 99.2 reduce-scatter.14
  929.0 126.4 all-reduce.10
  1059.0 53.7 all-gather.3
  1116.2 53.5 all-gather.7
  1173.2 59.3 all-gather.5
where the time goes:
time: 1250 us
  waiting for transfers between devices  956 us (76%)
  blocking collectives  161 us (13%)
  local copies, waits for them, and re-layouts  85.7 us (7%)
  other arithmetic  27.3 us (2%)
  between operations  19.6 us (2%)
    unnamed x14, waiting for transfers between devices  414 us
    reduce_scatter x3, waiting for transfers between devices, body(): lax.psum_scatter(gradient.reshape(count, -1), 'dp', scatter_dimension=1,...  378 us
    all_gather x3, waiting for transfers between devices, body(): lax.all_gather(w_part - moment_next, 'dp', axis=1, tiled=True)  164 us
    all_gather x2, blocking collectives, body(): lax.all_gather(w_part - moment_next, 'dp', axis=1, tiled=True)  76.6 us
    unnamed x69, local copies, waits for them, and re-layouts  44.5 us
    unnamed x1, blocking collectives  43 us
    psum x1, blocking collectives, body(): sq_total = lax.psum(jnp.concatenate(squares), 'dp')  41 us
  transfers between devices with their start and end apart: 10, of which 10 were waited for; matrix products, arithmetic and copies ran while one was open for 7% of the time, Pallas kernels for 0%

commit v1 on v0

v1 whole, which is shorter than its diff:
```python
import functools
import jax
import jax.numpy as jnp
from jax import lax
from jax.experimental import pallas as pl
from jax.experimental.pallas import tpu as pltpu
from jax.sharding import PartitionSpec as P

MOMENTUM = 0.9
TRUST_COEF = 0.001
DECAY = 0.0001
N_DEV = 32
LANES = 128
MID, IN0, IN, OUT, SHORT, FC, BN, BIAS, ROWS = 0, 162, 164, 232, 304, 312, 320, 324, 328
N_MID, N_IN, N_OUT = 18, 17, 18
CLASSES = 100
ID_IN0, ID_IN, ID_OUT, ID_SHORT, ID_FC, ID_PLAIN = 18, 19, 36, 54, 55, 56
F32 = jnp.float32
VMEM = pltpu.VMEM


def tensor_of_row(row):
    out = jnp.where(row < IN0, row // 9, ID_IN0)
    out = jnp.where(row >= IN, ID_IN + (row - IN) // 4, out)
    out = jnp.where(row >= OUT, ID_OUT + (row - OUT) // 4, out)
    out = jnp.where(row >= SHORT, ID_SHORT + (row - SHORT) // 8, out)
    return jnp.where(row >= BN, ID_PLAIN, out)


def left(a, b):
    return jnp.concatenate([a[:, :64], b[:, :64]], axis=1)


def right(a, b):
    return jnp.concatenate([a[:, 64:], b[:, 64:]], axis=1)


def across(piece8, row):
    return pl.ds(piece8 * 8 * ROWS + row, 8, stride=ROWS)


def pack_kernel(g_mid, g_in, g_in0, g_out, g_short, g_bn, pooled, dlog_t,
                w_mid, w_in, w_in0, w_out, w_short, w_fc, w_bn, w_bias, v_mid, v_in, v_out, v_small,
                packed, w_own, v_own,
                s_mid, s_in, s_in0, s_out, s_short, s_bn, s_x, s_d, xt, fct,
                o_mid, o_in, o_in0, o_out, o_short, o_fc, o_bn, ot, sems):
    rank = lax.axis_index('dp')
    copies = []

    def fetch(src, dst):
        copy = pltpu.make_async_copy(src, dst, sems.at[len(copies)])
        copy.start()
        copies.append(copy)
        return copy

    c_mid = fetch(g_mid, s_mid)
    c_in = fetch(g_in, s_in)
    c_in0 = fetch(g_in0, s_in0)
    c_out = [fetch(g_out.at[:, :, pl.ds(128 * h, 128)], s_out.at[h]) for h in range(2)]
    c_short = [fetch(g_short.at[:, pl.ds(128 * h, 128)], s_short.at[h]) for h in range(2)]
    c_bn = fetch(g_bn, s_bn)
    c_fc = [fetch(pooled, s_x), fetch(dlog_t, s_d)]
    mid_at = pl.multiple_of((18 * rank) // 8 * 8, 8)
    mid_off = 18 * rank - mid_at
    out_at = pl.multiple_of((2 * rank) // 8 * 8, 8)
    out_off = 2 * lax.rem(rank, 4)
    short_at = pl.multiple_of((4 * rank) // 8 * 8, 8)
    short_off = 4 * lax.rem(rank, 2)
    col_at = pl.multiple_of((rank // 16) * 128, 128)
    col_off = pl.multiple_of(lax.rem(rank, 16) * 8, 8)
    c_own = [
        fetch(w_mid.at[:, pl.ds(mid_at, 24), :], o_mid),
        fetch(w_in.at[:, :, pl.ds(col_at, 128)], o_in),
        fetch(w_in0, o_in0),
        fetch(w_out.at[:, pl.ds(out_at, 8), pl.ds(0, 128)], o_out.at[0]),
        fetch(w_out.at[:, pl.ds(out_at, 8), pl.ds(128, 128)], o_out.at[1]),
        fetch(w_short.at[pl.ds(short_at, 8), pl.ds(0, 128)], o_short.at[0]),
        fetch(w_short.at[pl.ds(short_at, 8), pl.ds(128, 128)], o_short.at[1]),
        fetch(w_fc.at[:, pl.ds(col_at, 128)], o_fc),
        fetch(w_bn, o_bn),
    ]

    for ref, base, tiles, count in ((v_mid, MID, 9, N_MID), (v_in, IN, 4, N_IN), (v_out, OUT, 4, N_OUT)):
        for m in range(tiles):
            for t in range(0, count, 8):
                size = min(8, count - t)
                v_own[pl.ds(base + tiles * t + m, size, stride=tiles), :] = ref[t:t + size, 128 * m:128 * m + 128]
    v_own[IN0:IN0 + 2, :] = v_small[0:2, :]
    v_own[SHORT:SHORT + 24, :] = v_small[8:32, :]

    c_mid.wait()

    def mid_body(t, carry):
        for a in range(4):
            for k in range(9):
                even = s_mid[t, pl.ds(144 * a + 2 * k, 8, stride=18), :]
                odd = s_mid[t, pl.ds(144 * a + 2 * k + 1, 8, stride=18), :]
                packed[across(a, MID + 9 * t + k), :] = jnp.concatenate([even, odd], axis=1)
        return carry

    lax.fori_loop(0, N_MID, mid_body, 0)
    c_in.wait()
    c_in0.wait()

    def in_rows(t, other):
        for a in range(4):
            for k in range(4):
                even = xt[pl.ds(64 * a + 2 * k, 8, stride=8), :]
                odd = xt[pl.ds(64 * a + 2 * k + 1, 8, stride=8), :]
                packed[across(a, IN + 4 * t + k), :] = left(even, odd)
                if other is not None:
                    packed[across(a, IN + 4 * other + k), :] = right(even, odd)

    def in_body(t, carry):
        both = jnp.concatenate([s_in[t], s_in[t + 8]], axis=0)
        for h in range(2):
            xt[128 * h:128 * h + 128, :] = both[:, 128 * h:128 * h + 128].T
        in_rows(t, t + 8)
        return carry

    lax.fori_loop(0, 8, in_body, 0)
    last = jnp.concatenate([s_in[16], jnp.concatenate([s_in0[...], s_in0[...]], axis=1)], axis=0)
    for h in range(2):
        xt[128 * h:128 * h + 128, :] = last[:, 128 * h:128 * h + 128].T
    in_rows(16, None)
    for a in range(4):
        for k in range(2):
            even = xt[pl.ds(32 * a + 2 * k, 8, stride=4), :]
            odd = xt[pl.ds(32 * a + 2 * k + 1, 8, stride=4), :]
            packed[across(a, IN0 + k), :] = right(even, odd)
    for copy in c_out + c_short:
        copy.wait()

    def out_body(t, carry):
        for a in range(4):
            for p in range(2):
                for h in range(2):
                    packed[across(a, OUT + 4 * t + 2 * p + h), :] = s_out[h, t, pl.ds(16 * a + p, 8, stride=2), :]
        return carry

    lax.fori_loop(0, N_OUT, out_body, 0)
    for a in range(4):
        for p in range(4):
            for h in range(2):
                packed[across(a, SHORT + 2 * p + h), :] = s_short[h, pl.ds(32 * a + p, 8, stride=4), :]
    for i in range(N_DEV):
        packed[i * ROWS + BN:i * ROWS + ROWS, :] = jnp.zeros((8, LANES), F32)
    c_bn.wait()
    for b in range(2):
        for k in range(4):
            for half in range(2):
                packed[pl.ds((16 * b + half) * ROWS + BN + k, 8, stride=2 * ROWS), :] = (
                    s_bn[pl.ds(56 * b + 3 * half + k, 8, stride=7), :])
    for copy in c_fc:
        copy.wait()
    scale = 1.0 / s_x.shape[0]
    fct[...] = jnp.zeros_like(fct)
    fct[0:CLASSES, :] = jnp.dot(s_d[...], s_x[...], preferred_element_type=F32) * scale
    bias = lax.dot_general(jnp.ones((8, s_d.shape[1]), jnp.bfloat16), s_d[...], (((1,), (1,)), ((), ())),
                           preferred_element_type=F32) * scale
    bias = jnp.concatenate([bias, jnp.zeros((8, LANES - CLASSES), F32)], axis=1)
    for a in range(4):
        packed[across(a, BIAS), :] = bias
    for h in range(2):
        cols = fct[:, 128 * h:128 * h + 128].T
        for j in range(16):
            at = (16 * h + j) * ROWS + FC
            packed[at:at + 8, :] = cols[8 * j:8 * j + 8, :]

    for copy in c_own:
        copy.wait()
    for t in range(N_MID):
        even = o_mid[t, pl.ds(mid_off, 9, stride=2), :]
        odd = o_mid[t, pl.ds(mid_off + 1, 9, stride=2), :]
        w_own[MID + 9 * t:MID + 9 * t + 9, :] = jnp.concatenate([even, odd], axis=1)
    for t in range(9):
        other = o_in[t + 8] if t < 8 else o_in0[...]
        ot[...] = jnp.concatenate([o_in[2 * 8 if t == 8 else t], other], axis=0).T
        even = ot[pl.ds(col_off, 4, stride=2), :]
        odd = ot[pl.ds(col_off + 1, 4, stride=2), :]
        here = 16 if t == 8 else t
        w_own[IN + 4 * here:IN + 4 * here + 4, :] = left(even, odd)
        if t < 8:
            w_own[IN + 4 * (t + 8):IN + 4 * (t + 8) + 4, :] = right(even, odd)
    even = ot[pl.ds(4 * rank, 2, stride=2), :]
    odd = ot[pl.ds(4 * rank + 1, 2, stride=2), :]
    w_own[IN0:IN0 + 2, :] = right(even, odd)
    for p in range(2):
        for h in range(2):
            for t in range(N_OUT):
                w_own[OUT + 4 * t + 2 * p + h:OUT + 4 * t + 2 * p + h + 1, :] = o_out[h, t, pl.ds(out_off + p, 1), :]
    for p in range(4):
        for h in range(2):
            w_own[SHORT + 2 * p + h:SHORT + 2 * p + h + 1, :] = o_short[h, pl.ds(short_off + p, 1), :]
    fct[0:CLASSES, 0:LANES] = o_fc[...]
    ot[...] = fct[:, 0:LANES].T
    w_own[FC:FC + 8, :] = jnp.where(lax.broadcasted_iota(jnp.int32, (8, LANES), 1) < CLASSES,
                                    ot[pl.ds(col_off, 8), :], 0.0)
    w_own[BN:ROWS, :] = jnp.zeros((8, LANES), F32)
    bn_at = 7 * (rank // 2) + 3 * lax.rem(rank, 2)
    for k in range(4):
        w_own[BN + k:BN + k + 1, :] = o_bn[pl.ds(bn_at + k, 1), :]
    lane = lax.broadcasted_iota(jnp.int32, (1, LANES), 1)
    w_own[BIAS:BIAS + 1, :] = jnp.where((lane >= 4 * rank) & (lane < 4 * rank + 4), w_bias[...], 0.0)


def pack_grads(ops):
    any_ = pl.BlockSpec(memory_space=pl.ANY)
    vm = pl.BlockSpec(memory_space=VMEM)
    return pl.pallas_call(
        pack_kernel,
        out_shape=(jax.ShapeDtypeStruct((N_DEV * ROWS, LANES), F32), jax.ShapeDtypeStruct((ROWS, LANES), F32),
                   jax.ShapeDtypeStruct((ROWS, LANES), F32)),
        in_specs=[any_] * 15 + [vm] * 5,
        out_specs=(vm, vm, vm),
        scratch_shapes=[
            VMEM((N_MID, 576, 64), F32), VMEM((N_IN, 64, 256), F32), VMEM((64, 128), F32),
            VMEM((2, N_OUT, 64, 128), F32), VMEM((2, 128, 128), F32), VMEM((112, 128), F32),
            VMEM((1024, 256), jnp.bfloat16), VMEM((CLASSES, 1024), jnp.bfloat16),
            VMEM((256, 128), F32), VMEM((128, 256), F32),
            VMEM((N_MID, 24, 64), F32), VMEM((N_IN, 64, 128), F32), VMEM((64, 128), F32),
            VMEM((2, N_OUT, 8, 128), F32), VMEM((2, 8, 128), F32), VMEM((CLASSES, 128), F32),
            VMEM((112, 128), F32), VMEM((128, 128), F32),
            pltpu.SemaphoreType.DMA((24,)),
        ],
        compiler_params=pltpu.CompilerParams(vmem_limit_bytes=40 * 2**20),
    )(*ops)


def unpack_kernel(packed, v_own, n_mid, n_in, n_in0, n_out, n_short, n_fc, n_bn, n_bias,
                  b_mid, b_in, b_in0, b_out, b_short, b_fc, v_mid, v_in, v_out, v_small,
                  s_mid, s_in, s_out, s_short, s_in0, s_fc, t_mid, t_in, t_out, t_short, t_in0, t_fc, xt, sems):
    bf = jnp.bfloat16

    def put(src, dst, k):
        pltpu.make_async_copy(src, dst, sems.at[k]).start()

    def mid_body(t, carry):
        for a in range(4):
            for k in range(9):
                x = packed[across(a, MID + 9 * t + k), :]
                s_mid[t, pl.ds(144 * a + 2 * k, 8, stride=18), :] = x[:, :64]
                s_mid[t, pl.ds(144 * a + 2 * k + 1, 8, stride=18), :] = x[:, 64:]
        put(s_mid.at[t], n_mid.at[t], 0)
        t_mid[t] = s_mid[t].astype(bf)
        put(t_mid.at[t], b_mid.at[t], 1)
        return carry

    lax.fori_loop(0, N_MID, mid_body, 0)

    def in_rows(t, other):
        for a in range(4):
            for k in range(4):
                x = packed[across(a, IN + 4 * t + k), :]
                y = packed[across(a, IN + 4 * other + k), :] if other is not None else x
                xt[pl.ds(64 * a + 2 * k, 8, stride=8), :] = left(x, y)
                xt[pl.ds(64 * a + 2 * k + 1, 8, stride=8), :] = right(x, y)

    def in_body(t, carry):
        in_rows(t, t + 8)
        for h in range(2):
            cols = xt[128 * h:128 * h + 128, :].T
            s_in[t, :, 128 * h:128 * h + 128] = cols[:64]
            s_in[t + 8, :, 128 * h:128 * h + 128] = cols[64:]
            t_in[t, :, 128 * h:128 * h + 128] = cols[:64].astype(bf)
            t_in[t + 8, :, 128 * h:128 * h + 128] = cols[64:].astype(bf)
        for u in (t, t + 8):
            put(s_in.at[u], n_in.at[u], 2)
            put(t_in.at[u], b_in.at[u], 3)
        return carry

    lax.fori_loop(0, 8, in_body, 0)
    in_rows(16, None)
    for h in range(2):
        cols = xt[128 * h:128 * h + 128, :].T
        s_in[16, :, 128 * h:128 * h + 128] = cols[:64]
        t_in[16, :, 128 * h:128 * h + 128] = cols[:64].astype(bf)
    put(s_in.at[16], n_in.at[16], 2)
    put(t_in.at[16], b_in.at[16], 3)
    for a in range(4):
        for k in range(2):
            x = packed[across(a, IN0 + k), :]
            xt[pl.ds(32 * a + 2 * k, 8, stride=4), :] = x
            xt[pl.ds(32 * a + 2 * k + 1, 8, stride=4), :] = right(x, x)
    cols = xt[0:128, :].T
    s_in0[...] = cols[:64]
    t_in0[...] = cols[:64].astype(bf)
    put(s_in0, n_in0, 4)
    put(t_in0, b_in0, 5)

    def out_body(t, carry):
        for a in range(4):
            for p in range(2):
                for h in range(2):
                    s_out[h, t, pl.ds(16 * a + p, 8, stride=2), :] = packed[across(a, OUT + 4 * t + 2 * p + h), :]
        for h in range(2):
            t_out[h, t] = s_out[h, t].astype(bf)
            put(s_out.at[h, t], n_out.at[t, :, pl.ds(128 * h, 128)], 6)
            put(t_out.at[h, t], b_out.at[t, :, pl.ds(128 * h, 128)], 7)
        return carry

    lax.fori_loop(0, N_OUT, out_body, 0)
    for h in range(2):
        for a in range(4):
            for p in range(4):
                s_short[h, pl.ds(32 * a + p, 8, stride=4), :] = packed[across(a, SHORT + 2 * p + h), :]
        t_short[h] = s_short[h].astype(bf)
        put(s_short.at[h], n_short.at[:, pl.ds(128 * h, 128)], 8)
        put(t_short.at[h], b_short.at[:, pl.ds(128 * h, 128)], 9)
    for i in range(N_DEV):
        xt[8 * i:8 * i + 8, :] = packed[i * ROWS + FC:i * ROWS + FC + 8, :]
    for h in range(2):
        cols = xt[128 * h:128 * h + 128, :].T
        s_fc[:, 128 * h:128 * h + 128] = cols[:CLASSES]
        t_fc[:, 128 * h:128 * h + 128] = cols[:CLASSES].astype(bf)
    put(s_fc, n_fc, 10)
    put(t_fc, b_fc, 11)

    lane = lax.broadcasted_iota(jnp.int32, (8, LANES), 1)
    for b in range(2):
        def even(k):
            return packed[pl.ds(16 * b * ROWS + BN + k, 8, stride=2 * ROWS), :]

        def odd(k):
            return packed[pl.ds((16 * b + 1) * ROWS + BN + k, 8, stride=2 * ROWS), :]

        for k in range(3):
            n_bn[pl.ds(56 * b + k, 8, stride=7), :] = even(k)
            n_bn[pl.ds(56 * b + 4 + k, 8, stride=7), :] = odd(1 + k)
        n_bn[pl.ds(56 * b + 3, 8, stride=7), :] = jnp.where(lane < 64, even(3), odd(0))
    total = packed[across(0, BIAS), :]
    for a in range(1, 4):
        total = total + packed[across(a, BIAS), :]
    n_bias[...] = jnp.sum(total, axis=0, keepdims=True)

    for ref, base, tiles, count in ((v_mid, MID, 9, N_MID), (v_in, IN, 4, N_IN), (v_out, OUT, 4, N_OUT)):
        for m in range(tiles):
            for t in range(0, count, 8):
                size = min(8, count - t)
                ref[t:t + size, 128 * m:128 * m + 128] = v_own[pl.ds(base + tiles * t + m, size, stride=tiles), :]
    v_small[0:2, :] = v_own[IN0:IN0 + 2, :]
    v_small[8:32, :] = v_own[SHORT:SHORT + 24, :]

    for k, (src, dst) in enumerate(((s_mid, n_mid), (t_mid, b_mid), (s_in, n_in), (t_in, b_in), (s_in0, n_in0),
                                    (t_in0, b_in0))):
        pltpu.make_async_copy(src, dst, sems.at[k]).wait()
    for h in range(2):
        half = pl.ds(128 * h, 128)
        for k, (src, dst) in enumerate(((s_out, n_out.at[:, :, half]), (t_out, b_out.at[:, :, half]),
                                        (s_short, n_short.at[:, half]), (t_short, b_short.at[:, half]))):
            pltpu.make_async_copy(src.at[h], dst, sems.at[6 + k]).wait()
    pltpu.make_async_copy(s_fc, n_fc, sems.at[10]).wait()
    pltpu.make_async_copy(t_fc, b_fc, sems.at[11]).wait()


def unpack_weights(packed, v_own):
    any_ = pl.BlockSpec(memory_space=pl.ANY)
    vm = pl.BlockSpec(memory_space=VMEM)
    bf = jnp.bfloat16
    kernels = ((N_MID, 576, 64), (N_IN, 64, 256), (64, 128), (N_OUT, 64, 256), (128, 256), (CLASSES, 256))
    shapes = [(s, F32) for s in kernels] + [((112, 128), F32), ((1, 128), F32)] + [(s, bf) for s in kernels]
    shapes += [((N_MID, 1152), F32), ((N_IN, 512), F32), ((N_OUT, 512), F32), ((32, LANES), F32)]
    scratch = ((N_MID, 576, 64), (N_IN, 64, 256), (2, N_OUT, 64, 128), (2, 128, 128), (64, 128), (CLASSES, 256))
    return pl.pallas_call(
        unpack_kernel,
        out_shape=[jax.ShapeDtypeStruct(s, d) for s, d in shapes],
        in_specs=[vm, vm],
        out_specs=[any_] * 6 + [vm] * 2 + [any_] * 6 + [vm] * 4,
        scratch_shapes=[VMEM(s, F32) for s in scratch] + [VMEM(s, bf) for s in scratch]
        + [VMEM((256, 128), F32), pltpu.SemaphoreType.DMA((12,))],
        compiler_params=pltpu.CompilerParams(vmem_limit_bytes=40 * 2**20),
    )(packed, v_own)


def exchange(packed, w_own, v_own, learn_rate):
    rank = lax.axis_index('dp')
    grad = lax.psum_scatter(packed.reshape(N_DEV, ROWS, LANES), 'dp', scatter_dimension=0, tiled=True)[0] / N_DEV
    ids = tensor_of_row(jnp.arange(ROWS))
    member = ids[:, None] == jnp.arange(64)[None, :]
    sums = jnp.stack([jnp.sum(grad * grad, axis=1), jnp.sum(w_own * w_own, axis=1)])
    partial = jnp.sum(jnp.where(member[None], sums[:, :, None], 0.0), axis=1)
    total = lax.psum(partial, 'dp')
    g_norm = jnp.sqrt(total[0])
    w_norm = jnp.sqrt(total[1])
    trust = jnp.where((w_norm > 0) & (g_norm > 0), TRUST_COEF * w_norm / (g_norm + DECAY * w_norm), 1.0)
    trust = jnp.sum(jnp.where(member, trust[None], 0.0), axis=1)
    plain = ids == ID_PLAIN
    trust = jnp.where(plain, 1.0, trust)[:, None]
    decay = jnp.where(plain, 0.0, DECAY)[:, None]
    v_next = MOMENTUM * v_own + learn_rate * trust * (grad + decay * w_own)
    lane = jnp.arange(LANES)
    mine = (jnp.arange(ROWS)[:, None] != BIAS) | ((lane >= 4 * rank) & (lane < 4 * rank + 4))[None]
    w_next = jnp.where(mine, w_own - v_next, 0.0)
    gathered = lax.all_gather(w_next, 'dp', axis=0, tiled=True)
    return gathered, v_next


def solution(mesh):
    spec_full = P()
    spec_lead = P('dp')
    spec_cols = P(None, 'dp')
    moment_specs = (spec_lead, spec_lead, spec_cols, spec_cols, spec_cols, spec_lead, spec_lead, spec_lead)
    in_specs = (spec_full,) * 8 + (spec_lead,) * 8 + moment_specs + (spec_full,)
    out_specs = (spec_full,) * 14 + moment_specs

    def body(w_in0, w_short, w_in, w_mid, w_out, w_fc, w_bn, w_bias,
             g_in0, g_short, g_in, g_mid, g_out, g_bn, pooled, dlogits,
             v_in0, v_short, v_in, v_mid, v_out, v_fc, v_bn, v_bias, learn_rate):
        rank = lax.axis_index('dp')
        odd = rank % 2 == 1
        lane = jnp.arange(LANES)
        v_bn_rows = jnp.where(odd, jnp.pad(v_bn, (64, 0)), jnp.pad(v_bn, (0, 64))).reshape(4, LANES)
        v_bias_row = lax.dynamic_update_slice(jnp.zeros((1, LANES), F32), v_bias[None], (0, 4 * rank))
        v_small = jnp.concatenate([
            jnp.pad(v_in0.reshape(2, LANES), ((0, 6), (0, 0))), v_short.reshape(8, LANES),
            jnp.pad(v_fc.reshape(8, CLASSES), ((0, 0), (0, LANES - CLASSES))),
            v_bn_rows, v_bias_row, jnp.zeros((3, LANES), F32)])
        packed, w_own, v_own = pack_grads((
            g_mid.reshape(N_MID, 576, 64), jnp.swapaxes(g_in[0], 1, 2), g_in0[0].T, g_out[0], g_short[0],
            g_bn.reshape(112, LANES), pooled, dlogits.T,
            w_mid.reshape(N_MID, 576, 64), jnp.swapaxes(w_in, 1, 2), w_in0.T, w_out, w_short, w_fc.T,
            w_bn.reshape(112, LANES), jnp.pad(w_bias, (0, LANES - CLASSES))[None], v_mid, v_in, v_out, v_small))
        gathered, v_next = exchange(packed, w_own, v_own, learn_rate)
        (n_mid, n_in, n_in0, n_out, n_short, n_fc, n_bn, n_bias, b_mid, b_in, b_in0, b_out, b_short, b_fc,
         m_mid, m_in, m_out, m_small) = unpack_weights(gathered, v_next)
        m_bn = m_small[24:28].reshape(-1)
        m_bn = jnp.where(odd, m_bn[64:], m_bn[:448])
        m_bias = lax.dynamic_slice(m_small, (28, 4 * rank), (1, 4))[0]
        return (n_in0.T, n_short, jnp.swapaxes(n_in, 1, 2), n_mid.reshape(w_mid.shape), n_out, n_fc.T,
                n_bn.reshape(-1), n_bias[0, :CLASSES],
                b_in0.T, b_short, jnp.swapaxes(b_in, 1, 2), b_mid.reshape(w_mid.shape), b_out, b_fc.T,
                m_small[0:2].reshape(-1), m_small[8:16].reshape(-1), m_in, m_mid, m_out,
                m_small[16:24, :CLASSES].reshape(-1), m_bn, m_bias)

    return jax.shard_map(body, mesh=mesh, in_specs=in_specs, out_specs=out_specs, check_vma=False)
```

time: 1250 us -> 312 us (0.25)
  waiting for transfers between devices: 956 us -> 213 us
  blocking collectives: 161 us -> 36.8 us
  local copies, waits for them, and re-layouts: 85.7 us -> 26.9 us
  other arithmetic: 27.3 us -> 4.79 us
  Pallas kernels: 0 us -> 14.8 us
    reduce_scatter x3 -> x0, waiting for transfers between devices: 378 us -> none  [body(): lax.psum_scatter(gradient.reshape(count, -1), 'dp', scatter_dimension=1,...]
    unnamed x14 -> x3, waiting for transfers between devices: 414 us -> 146 us
    all_gather x3 -> x1, waiting for transfers between devices: 164 us -> 66.7 us  [exchange(): gathered = lax.all_gather(w_next, 'dp', axis=0, tiled=True)]
    all_gather x2 -> x0, blocking collectives: 76.6 us -> none  [body(): lax.all_gather(w_part - moment_next, 'dp', axis=1, tiled=True)]
    unnamed x1 -> x0, blocking collectives: 43 us -> none
    reshape x13 -> x5, local copies, waits for them, and re-layouts: 36.1 us -> 2.58 us  [the longest x1 0.76 us: body(): v_fc.reshape(8, CLASSES)]
    unnamed x69 -> x36, local copies, waits for them, and re-layouts: 44.5 us -> 20.4 us
    pallas_call x0 -> x2, Pallas kernels: none -> 14.8 us  [the longest x1 8.61 us: pack_grads(): pl.pallas_call(pack_kernel, out_shape=(jax.ShapeDtypeStruct((N_DEV * ROWS...]
  transfers between devices with their start and end apart: 10 -> 2, of which waited for: 10 -> 2; matrix products, arithmetic and copies ran while one was open for 7% -> 0% of each run, Pallas kernels for 0% -> 0%
where the time goes in v1:
time: 312 us; the launch traced here: 311 us
  waiting for transfers between devices  213 us (68%)
  blocking collectives  36.8 us (12%)
  local copies, waits for them, and re-layouts  26.9 us (9%)
  Pallas kernels  14.8 us (5%)
  between operations  14.8 us (5%)
  other arithmetic  4.79 us (2%)
    unnamed x3, waiting for transfers between devices  146 us
    all_gather x1, waiting for transfers between devices, exchange(): gathered = lax.all_gather(w_next, 'dp', axis=0, tiled=True)  66.7 us
    psum x1, blocking collectives, exchange(): total = lax.psum(partial, 'dp')  36.8 us
    unnamed x36, local copies, waits for them, and re-layouts  20.4 us
    pallas_call x1, Pallas kernels, pack_grads(): pl.pallas_call(pack_kernel, out_shape=(jax.ShapeDtypeStruct((N_DEV * ROWS...  8.61 us
  transfers between devices with their start and end apart: 2, of which 2 were waited for; matrix products, arithmetic and copies ran while one was open for 0% of the time, Pallas kernels for 0%

profile of v1, /device:TPU:0, one launch (start us, length us, event | category | flops | bytes accessed | tf_op | source)
XLA Modules:
  0.0 310.9 jit_solution(14387701645974107659)
XLA Ops:
  7.2 0.0 reduce-scatter.5.cloned.1.call-start
  7.2 0.7 pad_bitcast_fusion.w_bias
  7.9 0.8 reshape.225
  8.7 0.7 pad.21
  9.4 0.8 select_bitcast_fusion
  10.2 0.8 dynamic_update_slice.3
  10.9 0.7 concatenate.3.v_small
  11.7 0.0 copy-start.1
  11.7 2.5 copy-done.1
  14.2 0.0 copy-start.2
  14.2 1.3 copy-done.2
  15.4 0.0 copy-start.3
  15.4 1.3 copy-done.3
  16.7 0.0 copy-start.4
  16.7 1.2 copy-done.4
  18.0 0.0 copy-start.5
  18.0 1.2 copy-done.5
  19.2 0.0 copy-start.6
  19.2 1.0 copy-done.6
  20.2 0.0 copy-start.7
  20.2 0.9 copy-done.7
  21.2 0.0 copy-start.8
  21.2 0.9 copy-done.8
  22.1 0.0 copy-start.9
  22.1 0.9 copy-done.9
  23.0 0.0 copy-start.10
  23.0 0.9 copy-done.10
  23.9 0.0 copy-start.11
  23.9 0.9 copy-done.11
  24.8 0.0 copy-start.12
  24.8 0.8 copy-done.12
  25.6 0.0 copy-start.13
  25.6 0.8 copy-done.13
  26.4 0.0 copy-start.14
  26.4 0.8 copy-done.14
  27.2 0.0 copy-start.15
  27.2 0.8 copy-done.15
  28.0 0.0 copy-start.16
  28.0 0.8 copy-done.16
  28.8 0.0 copy-start.17
  28.8 0.8 copy-done.17
  29.5 8.6 %shard_map.408 = (f32[10496,128]{1,0:T(8,128)}, f32[328,128]{1,0:T(8,128)S(1)}, f32[328,128]{1,0:T(8,128)S(1)}) custom-call(f32[18,576,64]{2,1,0:T(8,128)S(1)} %bitcast.55, f32[17,64,256]{2,1,0:T(8,128)S(1)} %bitcast.57, f32[64,128]{1,0:T(8,128)S(1)} %bitcast.64, f32[18,64,256]{2,1,0:T(8,128)S(1)} %bitcast.56, f32[128,256]{1,0:T(8,128)S(1)} %bitcast.60, ...), custom_call_target="tpu_custom_call" | custom-call | tf_op jit(solution)/shard_map/pallas_call | solution.py:210
  38.2 0.0 reduce-scatter.5.cloned.1.call-update
  38.2 0.0 all-gather.2.cloned.1.call-start
  38.9 0.1 multiply_reduce_fusion
  39.1 145.9 %reduce-scatter.5.cloned.1.call-done = f32[1,328,128]{2,1,0:T(8,128)} async-done(((f32[32,328,128]{2,1,0:T(8,128)}), f32[1,328,128]{2,1,0:T(8,128)}) %reduce-scatter.5.cloned.1.call-update) | async-done | bytes 167952
  185.0 1.1 fusion
  186.1 0.1 select_reduce_fusion
  186.2 36.8 %psum.7 = f32[2,64]{1,0:T(2,128)S(1)} all-reduce(f32[2,64]{1,0:T(2,128)S(1)} %select_reduce_fusion), channel_id=1, replica_groups=mesh['dp'=32] {'dp'}, use_global_device_ids=true, to_apply=%region_4.5 | all-reduce | flops 128 | bytes 1024 | tf_op jit(solution)/shard_map/psum | solution.py:382
  223.1 0.1 select_reduce_fusion.1
  223.2 1.8 subtract_select_fusion
  225.0 0.0 all-gather.2.cloned.1.call-update
  225.0 66.7 %all-gather.2.cloned.1.call-done.packed = f32[10496,128]{1,0:T(8,128)} async-done(((f32[328,128]{1,0:T(8,128)}), f32[10496,128]{1,0:T(8,128)}) %all-gather.2.cloned.1.call-update) | async-done | bytes 5373968 | tf_op jit(solution)/shard_map/all_gather | solution.py:394
  291.8 0.0 copy-start
  291.8 2.5 copy-done
  294.3 6.1 %shard_map.409 = (f32[18,576,64]{2,1,0:T(8,128)}, f32[17,64,256]{2,1,0:T(8,128)}, f32[64,128]{1,0:T(8,128)}, f32[18,64,256]{2,1,0:T(8,128)}, f32[128,256]{1,0:T(...) custom-call(f32[10496,128]{1,0:T(8,128)S(1)} %copy-done, ...), custom_call_target="tpu_custom_call" | custom-call | tf_op jit(solution)/shard_map/pallas_call | solution.py:364
  300.5 0.6 dynamic-slice_bitcast_fusion
  301.0 0.6 slice_bitcast_fusion.2
  301.6 0.6 slice_bitcast_fusion
  302.2 0.5 slice_bitcast_fusion.3
  302.7 0.6 slice_select_fusion
  303.4 0.7 reshape.233
  (15 shorter events, 0.1 us)
Async XLA Ops:
  7.2 177.9 %reduce-scatter.5.cloned.1.call-start = ((), (), s32[]{:S(2)}) async-start(), calls=%async_computation.2 | async-start | bytes 5541888
  11.7 2.5 copy-start.1
  14.2 1.3 copy-start.2
  15.4 1.3 copy-start.3
  16.7 1.2 copy-start.4
  18.0 1.2 copy-start.5
  19.2 1.0 copy-start.6
  20.2 0.9 copy-start.7
  21.2 0.9 copy-start.8
  22.1 0.9 copy-start.9
  23.0 0.9 copy-start.10
  23.9 0.9 copy-start.11
  24.8 0.8 copy-start.12
  25.6 0.8 copy-start.13
  26.4 0.8 copy-start.14
  27.2 0.8 copy-start.15
  28.0 0.8 copy-start.16
  28.8 0.8 copy-start.17
  38.2 253.6 %all-gather.2.cloned.1.call-start = ((), (), s32[]{:S(2)}) async-start(), calls=%async_computation.1 | async-start | bytes 5541888 | tf_op jit(solution)/shard_map/all_gather | solution.py:394
  291.8 2.5 copy-start
Sparse Core Ops, SparseCore 0:
  38.3 146.7 reduce-scatter.4
  225.2 66.5 all-gather.1

commit v2 on v1

--- a/solution.py
+++ b/solution.py
@@ -17,14 +17,6 @@
 ID_IN0, ID_IN, ID_OUT, ID_SHORT, ID_FC, ID_PLAIN = 18, 19, 36, 54, 55, 56
 F32 = jnp.float32
 VMEM = pltpu.VMEM
-
-
-def tensor_of_row(row):
-    out = jnp.where(row < IN0, row // 9, ID_IN0)
-    out = jnp.where(row >= IN, ID_IN + (row - IN) // 4, out)
-    out = jnp.where(row >= OUT, ID_OUT + (row - OUT) // 4, out)
-    out = jnp.where(row >= SHORT, ID_SHORT + (row - SHORT) // 8, out)
-    return jnp.where(row >= BN, ID_PLAIN, out)
 
 
 def left(a, b):
@@ -223,7 +215,7 @@
             VMEM((112, 128), F32), VMEM((128, 128), F32),
             pltpu.SemaphoreType.DMA((24,)),
         ],
-        compiler_params=pltpu.CompilerParams(vmem_limit_bytes=40 * 2**20),
+        compiler_params=pltpu.CompilerParams(vmem_limit_bytes=60 * 2**20),
     )(*ops)
 
 
@@ -368,31 +360,200 @@
         out_specs=[any_] * 6 + [vm] * 2 + [any_] * 6 + [vm] * 4,
         scratch_shapes=[VMEM(s, F32) for s in scratch] + [VMEM(s, bf) for s in scratch]
         + [VMEM((256, 128), F32), pltpu.SemaphoreType.DMA((12,))],
-        compiler_params=pltpu.CompilerParams(vmem_limit_bytes=40 * 2**20),
+        compiler_params=pltpu.CompilerParams(vmem_limit_bytes=60 * 2**20),
     )(packed, v_own)
 
+CHUNKS = ((0, 72, 'x'), (72, 72, 'y'), (144, 48, 'x'), (192, 48, 'y'), (240, 48, 'x'), (288, 40, 'y'))
+STEPS = (
+    (0, 0), (1, 0), (0, 1), (4, 0), (2, 0), (3, 0), (4, 1), (1, 1), (0, 2), (3, 1), (1, 2), (0, 3), (2, 1), (4, 2),
+    (5, 0), (1, 3), (5, 1), (3, 2), (4, 3), (2, 2), (3, 3), (1, 4), (5, 2), (2, 3), (0, 4), (4, 4), (5, 3), (1, 5),
+    (3, 4), (0, 5), (2, 4), (5, 4), (3, 5), (1, 6), (5, 5), (0, 6), (2, 5), (1, 7), (3, 6), (0, 7), (4, 5), (2, 6),
+    (4, 6), (1, 8), (5, 6), (3, 7), (2, 7), (4, 7), (5, 7), (2, 8), (1, 9), (0, 8), (2, 9), (3, 8), (5, 8), (0, 9),
+    (3, 9), (4, 8), (5, 9), (4, 9),
+)
+STAGES = 10
+S_CORE, S_ONE, S_TWO, S_Z, A_Z, A_TWO, A_ONE, A_CORE, N_SEMS = 0, 1, 2, 2, 5, 9, 10, 11, 12
+MESH = pl.DeviceIdType.MESH
+
+
+def first_row(t):
+    out = jnp.where(t < N_MID, 9 * t, IN0)
+    out = jnp.where(t >= ID_IN, IN + 4 * (t - ID_IN), out)
+    out = jnp.where(t >= ID_OUT, OUT + 4 * (t - ID_OUT), out)
+    return jnp.where(t >= ID_SHORT, SHORT + 8 * (t - ID_SHORT), out)
+
+
+def exchange_kernel(lr, packed, w_own, v_own, full, v_new,
+                    got_core, acc, got_one, got_two, got_z, grad, norms, send, recv, n_send, n_recv):
+    rank = lax.axis_index('dp')
+    core = lax.rem(rank, 2)
+    x = lax.rem(rank // 2, 2)
+    y = lax.rem(rank // 4, 2)
+    z = rank // 8
+
+    def device(zz, yy, xx, cc):
+        return (((zz * 2 + yy) * 2 + xx) * 2 + cc,)
+
+    core_peer = device(z, y, x, 1 - core)
+    x_peer = device(z, y, 1 - x, core)
+    y_peer = device(z, 1 - y, x, core)
+
+    barrier = pltpu.get_barrier_semaphore()
+
+    def greet(d, carry):
+        pl.semaphore_signal(barrier, inc=1, device_id=(lax.rem(rank + d, N_DEV),), device_id_type=MESH)
+        return carry
+
+    lax.fori_loop(1, N_DEV, greet, 0)
+    pl.semaphore_wait(barrier, N_DEV - 1)
+
+    copies = {}
+
+    def start(c, k, src, dst, peer):
+        copy = pltpu.make_async_remote_copy(src_ref=src, dst_ref=dst, send_sem=send.at[c * N_SEMS + k],
+                                            recv_sem=recv.at[c * N_SEMS + k], device_id=peer, device_id_type=MESH)
+        copy.start()
+        copies[c, k] = copy
+
+    def arrived(c, k):
+        copies[c, k].wait_recv()
+
+    def step(c, stage):
+        at, size, first = CHUNKS[c]
+        rows = pl.ds(at, size)
+        x_first = first == 'x'
+        one_peer, two_peer = (x_peer, y_peer) if x_first else (y_peer, x_peer)
+
+        def half(zz, yx, mine):
+            return (zz, yx, x if mine else 1 - x) if x_first else (zz, y if mine else 1 - y, yx)
+
+        if stage == 0:
+            start(c, S_CORE, packed.at[:, :, :, 1 - core, rows, :], got_core.at[:, :, :, rows, :], core_peer)
+        elif stage == 1:
+            arrived(c, S_CORE)
+
+            def add(mine):
+                def body(m, carry):
+                    zz, yx = m // 2, lax.rem(m, 2)
+                    a, b, d = half(zz, yx, mine)
+                    acc[a, b, d, rows, :] = packed[a, b, d, core, rows, :] + got_core[a, b, d, rows, :]
+                    return carry
+
+                lax.fori_loop(0, 8, body, 0)
+
+            add(False)
+            src = acc.at[:, :, 1 - x, rows, :] if x_first else acc.at[:, 1 - y, :, rows, :]
+            start(c, S_ONE, src, got_one.at[:, :, rows, :], one_peer)
+            add(True)
+        elif stage == 2:
+            arrived(c, S_ONE)
+
+            def add(other):
+                def body(zz, carry):
+                    a, b, d = half(zz, other, True)
+                    acc[a, b, d, rows, :] = acc[a, b, d, rows, :] + got_one[zz, other, rows, :]
+                    return carry
+
+                lax.fori_loop(0, 4, body, 0)
+
+            here = y if x_first else x
+            add(1 - here)
+            src = acc.at[:, 1 - y, x, rows, :] if x_first else acc.at[:, y, 1 - x, rows, :]
+            start(c, S_TWO, src, got_two.at[:, rows, :], two_peer)
+            add(here)
+        elif stage == 3:
+            arrived(c, S_TWO)
+            for d in (1, 2, 3, 0):
+                zz = lax.rem(z + d, 4)
+                acc[zz, y, x, rows, :] = acc[zz, y, x, rows, :] + got_two[zz, rows, :]
+                if d:
+                    start(c, S_Z + d, acc.at[zz, y, x, rows, :], got_z.at[d - 1, rows, :], device(zz, y, x, core))
+        elif stage == 4:
+            for d in (1, 2, 3):
+                arrived(c, S_Z + d)
+            mean = (acc[z, y, x, rows, :] + got_z[0, rows, :] + got_z[1, rows, :] + got_z[2, rows, :]) * (1.0 / N_DEV)
+            grad[rows, :] = mean
+            own = w_own[rows, :]
+            g_sum = jnp.sum(mean * mean, axis=1, keepdims=True)
+            w_sum = jnp.sum(own * own, axis=1, keepdims=True)
+            row = lax.broadcasted_iota(jnp.int32, (size, LANES), 0) + at
+            lane = lax.broadcasted_iota(jnp.int32, (size, LANES), 1)
+            tensor = jnp.where(lane < 64, lane, lane - 64)
+            member = (row >= first_row(tensor)) & (row < first_row(tensor + 1))
+            part = jnp.where(member, jnp.where(lane < 64, g_sum, w_sum), 0.0)
+            norms[c, rank] = jnp.sum(part, axis=0, keepdims=True)
+
+            def tell(d, carry):
+                pltpu.make_async_remote_copy(
+                    src_ref=norms.at[c, rank], dst_ref=norms.at[c, rank], send_sem=n_send.at[c],
+                    recv_sem=n_recv.at[c], device_id=(lax.rem(rank + d, N_DEV),), device_id_type=MESH).start()
+                return carry
+
+            lax.fori_loop(1, N_DEV, tell, 0)
+        elif stage == 5:
+            others = norms.at[c, pl.ds(0, N_DEV - 1)]
+            pltpu.make_async_copy(others, others, n_recv.at[c]).wait()
+            total = jnp.sum(norms[c], axis=0)
+            g_norm = jnp.sqrt(total)
+            w_norm = pltpu.roll(g_norm, 64, 1)
+            trust = jnp.where((w_norm > 0) & (g_norm > 0), TRUST_COEF * w_norm / (g_norm + DECAY * w_norm), 1.0)
+            row = lax.broadcasted_iota(jnp.int32, (size, LANES), 0) + at
+            lane = lax.broadcasted_iota(jnp.int32, (size, LANES), 1)
+            trust = jnp.where(lane == ID_PLAIN, 1.0, trust)
+            member = (row >= first_row(lane)) & (row < first_row(lane + 1)) & (lane <= ID_PLAIN)
+            rate = lr[0] * jnp.sum(jnp.where(member, trust, 0.0), axis=1, keepdims=True)
+            decay = jnp.where(row < BN, DECAY, 0.0)
+            own = w_own[rows, :]
+            moment = MOMENTUM * v_own[rows, :] + rate * (grad[rows, :] + decay * own)
+            v_new[rows, :] = moment
+            mine = (row != BIAS) | ((lane >= 4 * rank) & (lane < 4 * rank + 4))
+            full[z, y, x, core, rows, :] = jnp.where(mine, own - moment, 0.0)
+            for d in (1, 2, 3):
+                piece = full.at[z, y, x, core, rows, :]
+                start(c, A_Z + d, piece, piece, device(lax.rem(z + d, 4), y, x, core))
+        elif stage == 6:
+            for d in (1, 2, 3):
+                arrived(c, A_Z + d)
+            pieces = full.at[:, y, x, core, rows, :]
+            start(c, A_TWO, pieces, pieces, two_peer)
+        elif stage == 7:
+            arrived(c, A_TWO)
+            pieces = full.at[:, :, x, core, rows, :] if x_first else full.at[:, y, :, core, rows, :]
+            start(c, A_ONE, pieces, pieces, one_peer)
+        elif stage == 8:
+            arrived(c, A_ONE)
+            pieces = full.at[:, :, :, core, rows, :]
+            start(c, A_CORE, pieces, pieces, core_peer)
+        else:
+            arrived(c, A_CORE)
+
+    for c, stage in STEPS:
+        step(c, stage)
+    for copy in copies.values():
+        copy.wait_send()
+    for c in range(len(CHUNKS)):
+        others = norms.at[c, pl.ds(0, N_DEV - 1)]
+        pltpu.make_async_copy(others, others, n_send.at[c]).wait()
+
 
 def exchange(packed, w_own, v_own, learn_rate):
-    rank = lax.axis_index('dp')
-    grad = lax.psum_scatter(packed.reshape(N_DEV, ROWS, LANES), 'dp', scatter_dimension=0, tiled=True)[0] / N_DEV
-    ids = tensor_of_row(jnp.arange(ROWS))
-    member = ids[:, None] == jnp.arange(64)[None, :]
-    sums = jnp.stack([jnp.sum(grad * grad, axis=1), jnp.sum(w_own * w_own, axis=1)])
-    partial = jnp.sum(jnp.where(member[None], sums[:, :, None], 0.0), axis=1)
-    total = lax.psum(partial, 'dp')
-    g_norm = jnp.sqrt(total[0])
-    w_norm = jnp.sqrt(total[1])
-    trust = jnp.where((w_norm > 0) & (g_norm > 0), TRUST_COEF * w_norm / (g_norm + DECAY * w_norm), 1.0)
-    trust = jnp.sum(jnp.where(member, trust[None], 0.0), axis=1)
-    plain = ids == ID_PLAIN
-    trust = jnp.where(plain, 1.0, trust)[:, None]
-    decay = jnp.where(plain, 0.0, DECAY)[:, None]
-    v_next = MOMENTUM * v_own + learn_rate * trust * (grad + decay * w_own)
-    lane = jnp.arange(LANES)
-    mine = (jnp.arange(ROWS)[:, None] != BIAS) | ((lane >= 4 * rank) & (lane < 4 * rank + 4))[None]
-    w_next = jnp.where(mine, w_own - v_next, 0.0)
-    gathered = lax.all_gather(w_next, 'dp', axis=0, tiled=True)
-    return gathered, v_next
+    vm = pl.BlockSpec(memory_space=VMEM)
+    count = len(CHUNKS)
+    full, v_new = pl.pallas_call(
+        exchange_kernel,
+        out_shape=(jax.ShapeDtypeStruct((4, 2, 2, 2, ROWS, LANES), F32), jax.ShapeDtypeStruct((ROWS, LANES), F32)),
+        in_specs=[pl.BlockSpec(memory_space=pltpu.SMEM)] + [vm] * 3,
+        out_specs=(vm, vm),
+        scratch_shapes=[
+            VMEM((4, 2, 2, ROWS, LANES), F32), VMEM((4, 2, 2, ROWS, LANES), F32), VMEM((4, 2, ROWS, LANES), F32),
+            VMEM((4, ROWS, LANES), F32), VMEM((3, ROWS, LANES), F32), VMEM((ROWS, LANES), F32),
+            VMEM((count, N_DEV, 1, LANES), F32),
+            pltpu.SemaphoreType.DMA((count * N_SEMS,)), pltpu.SemaphoreType.DMA((count * N_SEMS,)),
+            pltpu.SemaphoreType.DMA((count,)), pltpu.SemaphoreType.DMA((count,)),
+        ],
+        compiler_params=pltpu.CompilerParams(vmem_limit_bytes=60 * 2**20, collective_id=0, has_side_effects=True),
+    )(learn_rate.reshape(1), packed.reshape(4, 2, 2, 2, ROWS, LANES), w_own, v_own)
+    return full.reshape(N_DEV * ROWS, LANES), v_new
 
 
 def solution(mesh):

time: 312 us -> 119 us (0.38)
  waiting for transfers between devices: 213 us -> 0 us
  Pallas kernels: 14.8 us -> 102 us
  blocking collectives: 36.8 us -> 0 us
  local copies, waits for them, and re-layouts: 26.9 us -> 13.4 us
  between operations: 14.8 us -> 1.36 us
  other arithmetic: 4.79 us -> 1.48 us
    unnamed x3 -> x0, waiting for transfers between devices: 146 us -> none
    pallas_call x0 -> x1, Pallas kernels: none -> 82.7 us  [exchange(): pl.pallas_call(exchange_kernel, out_shape=(jax.ShapeDtypeStruct((4, 2, 2,...]
    all_gather x1 -> x0, waiting for transfers between devices: 66.7 us -> none  [exchange(): gathered = lax.all_gather(w_next, 'dp', axis=0, tiled=True)]
    psum x1 -> x0, blocking collectives: 36.8 us -> none  [exchange(): total = lax.psum(partial, 'dp')]
    unnamed x36 -> x0, local copies, waits for them, and re-layouts: 20.4 us -> none
  transfers between devices with their start and end apart: 2 -> 0, of which waited for: 2 -> 0; matrix products, arithmetic and copies ran while one was open for 0% -> 0% of each run, Pallas kernels for 0% -> 0%
where the time goes in v2:
time: 119 us; the launch traced here: 118 us
  Pallas kernels  102 us (86%)
  local copies, waits for them, and re-layouts  13.4 us (11%)
  other arithmetic  1.48 us (1%)
  between operations  1.36 us (1%)
    pallas_call x1, Pallas kernels, exchange(): pl.pallas_call(exchange_kernel, out_shape=(jax.ShapeDtypeStruct((4, 2, 2,...  82.7 us
    pallas_call x1, Pallas kernels, pack_grads(): pl.pallas_call(pack_kernel, out_shape=(jax.ShapeDtypeStruct((N_DEV * ROWS...  10.5 us
    pallas_call x1, Pallas kernels, unpack_weights(): pl.pallas_call(unpack_kernel, out_shape=[jax.ShapeDtypeStruct(s, d) for s...  8.69 us
    concatenate x1, local copies, waits for them, and re-layouts, body(): jnp.concatenate([jnp.pad(v_in0.reshape(2, LANES), ((0, 6), (0, 0))), v_sh...  3.07 us

profile of v2, /device:TPU:0, one launch (start us, length us, event | category | flops | bytes accessed | tf_op | source)
XLA Modules:
  0.0 118.1 jit_solution(9670098093053321611)
XLA Ops:
  1.3 1.2 pad_bitcast_fusion.w_bias
  2.5 0.8 dynamic_update_slice.3
  3.2 0.8 select_bitcast_fusion
  4.1 0.7 pad.21
  4.8 0.8 reshape.105
  5.5 3.1 %concatenate.3.v_small = f32[32,128]{1,0:T(8,128)} concatenate(f32[8,128]{1,0:T(8,128)S(1)} %pad.21, f32[8,128]{1,0:T(8,128)} %bitcast.60, f32[8,128]{1,0:T(8,128)S(1)} %pad.22, f32[4,128]{1,0:T(4,128)S(1)} %select_bitcast_fusion, f32[1,128]{1,0:T(1,128)S(1)} %dynamic_update_slice.3, f32[3,128]{1,0:T(4,128)S(1)} %broadcast_in_dim.15), dimensions={0} | concatenate | bytes 32768 | tf_op jit(solution)/shard_map/concatenate | solution.py:575
  8.6 10.5 %shard_map.408 = (f32[10496,128]{1,0:T(8,128)}, f32[328,128]{1,0:T(8,128)}, f32[328,128]{1,0:T(8,128)}) custom-call(f32[18,576,64]{2,1,0:T(8,128)} %bitcast.48, f32[17,64,256]{2,1,0:T(8,128)} %bitcast.51, f32[64,128]{1,0:T(8,128)} %bitcast.58, f32[18,64,256]{2,1,0:T(8,128)} %bitcast.50, f32[128,256]{1,0:T(8,128)} %bitcast.54, f32[112,128]{1,0:T(8,128)} %bitcast.56, ...), custom_call_target="tpu_custom_call" | custom-call | tf_op jit(solution)/shard_map/pallas_call | solution.py:202
  19.1 82.7 %shard_map.409 = (f32[4,2,2,2,328,128]{5,4,3,2,1,0:T(8,128)}, f32[328,128]{1,0:T(8,128)}) custom-call(f32[1]{0:T(128)} %bitcast.45.lr, f32[4,2,2,2,328,128]{5,4,3,2,1,0:T(8,128)} %bitcast.47, f32[328,128]{1,0:T(8,128)} %get-tuple-element.46.w_own, f32[328,128]{1,0:T(8,128)} %get-tuple-element.47.v_own), custom_call_target="tpu_custom_call" | custom-call | tf_op jit(solution)/shard_map/pallas_call | solution.py:542
  101.8 8.7 %shard_map.410 = (f32[18,576,64]{2,1,0:T(8,128)}, f32[17,64,256]{2,1,0:T(8,128)}, f32[64,128]{1,0:T(8,128)}, f32[18,64,256]{2,1,0:T(8,128)}, f32[128,256]{1,0:T(...) custom-call(f32[10496,128]{1,0:T(8,128)} %bitcast.46, ...), custom_call_target="tpu_custom_call" | custom-call | tf_op jit(solution)/shard_map/pallas_call | solution.py:356
  110.5 1.3 %dynamic-slice_bitcast_fusion = f32[4]{0:T(128)} fusion(f32[32,128]{1,0:T(8,128)} %get-tuple-element.64, s32[]{:T(128)S(6)} %select_n.30), kind=kLoop, calls=%fused_computation.5 | loop fusion | bytes 36 | tf_op jit(solution)/shard_map/squeeze | solution.py:589
  111.8 1.2 slice_bitcast_fusion.3
  113.0 1.2 %slice_bitcast_fusion.2 = f32[256]{0:T(256)} fusion(f32[32,128]{1,0:T(8,128)} %get-tuple-element.64), kind=kLoop, calls=%fused_computation.4 | loop fusion | bytes 2048 | tf_op jit(solution)/shard_map/reshape | solution.py:593
  114.2 0.7 slice_bitcast_fusion.1
  114.9 0.7 slice_select_fusion
  115.5 0.7 slice.24
  116.2 1.3 %slice_bitcast_fusion = f32[1024]{0:T(1024)} fusion(f32[32,128]{1,0:T(8,128)} %get-tuple-element.64), kind=kLoop, calls=%fused_computation | loop fusion | bytes 8192 | tf_op jit(solution)/shard_map/reshape | solution.py:593
  117.5 0.7 reshape.114
  (3 shorter events, 0.0 us)

commit v3 on v0

v3 whole, which is shorter than its diff:
```python
import jax
import jax.numpy as jnp
from jax import lax
from jax.experimental import pallas as pl
from jax.experimental.pallas import tpu as pltpu
from jax.sharding import PartitionSpec as P

MOMENTUM = 0.9
TRUST_COEF = 0.001
DECAY = 0.0001
N_DEV = 32
LANES = 128
MID, IN0, IN, OUT, SHORT, FC, BN, BIAS, ROWS = 0, 162, 164, 232, 304, 312, 320, 324, 328
N_MID, N_IN, N_OUT = 18, 17, 18
CLASSES = 100
ID_IN0, ID_IN, ID_OUT, ID_SHORT, ID_FC, ID_PLAIN = 18, 19, 36, 54, 55, 56
F32 = jnp.float32
VMEM = pltpu.VMEM
MESH = pl.DeviceIdType.MESH
CHUNKS = ((0, 72, 'x'), (72, 72, 'y'), (144, 48, 'x'), (192, 48, 'y'), (240, 48, 'x'), (288, 40, 'y'))
STEPS = (
    (0, 0), (1, 0), (0, 1), (4, 0), (2, 0), (3, 0), (4, 1), (1, 1), (0, 2), (3, 1), (1, 2), (0, 3), (2, 1), (4, 2),
    (5, 0), (1, 3), (5, 1), (3, 2), (4, 3), (2, 2), (3, 3), (1, 4), (5, 2), (2, 3), (0, 4), (4, 4), (5, 3), (1, 5),
    (3, 4), (0, 5), (2, 4), (5, 4), (3, 5), (1, 6), (5, 5), (0, 6), (2, 5), (1, 7), (3, 6), (0, 7), (4, 5), (2, 6),
    (4, 6), (1, 8), (5, 6), (3, 7), (2, 7), (4, 7), (5, 7), (2, 8), (1, 9), (0, 8), (2, 9), (3, 8), (5, 8), (0, 9),
    (3, 9), (4, 8), (5, 9), (4, 9),
)
S_CORE, S_ONE, S_TWO, S_Z, A_Z, A_TWO, A_ONE, A_CORE, N_SEMS = 0, 1, 2, 2, 5, 9, 10, 11, 12
VMEM_LIMIT = 60 * 2**20


def first_row(t):
    out = jnp.where(t < N_MID, 9 * t, IN0)
    out = jnp.where(t >= ID_IN, IN + 4 * (t - ID_IN), out)
    out = jnp.where(t >= ID_OUT, OUT + 4 * (t - ID_OUT), out)
    return jnp.where(t >= ID_SHORT, SHORT + 8 * (t - ID_SHORT), out)


def left(a, b):
    return jnp.concatenate([a[:, :64], b[:, :64]], axis=1)


def right(a, b):
    return jnp.concatenate([a[:, 64:], b[:, 64:]], axis=1)


def across(piece8, row):
    return pl.ds(piece8 * 8 * ROWS + row, 8, stride=ROWS)


def exchange_kernel(lr, g_mid, g_in, g_in0, g_out, g_short, g_bn, pooled, dlog_t,
                    w_mid, w_in, w_in0, w_out, w_short, w_fc, w_bn, w_bias,
                    v_mid, v_in, v_in0, v_out, v_short, v_fc, v_bn, v_bias,
                    full_out, v_out_rows,
                    s_mid, s_in, s_in0, s_out, s_short, s_bn, s_x, s_d, xt, fct,
                    o_mid, o_in, o_in0, o_out, o_short, o_fc, o_bn, o_bias, ot,
                    p_mid, p_in, p_in0, p_out, p_short, p_fc, p_bn, p_bias,
                    packed, w_own, v_own, v_new, full,
                    got_core, acc, got_one, got_two, got_z, grad, norms,
                    sems, out_sems, send, recv, n_send, n_recv):
    rank = lax.axis_index('dp')
    core = lax.rem(rank, 2)
    x = lax.rem(rank // 2, 2)
    y = lax.rem(rank // 4, 2)
    z = rank // 8

    def device(zz, yy, xx, cc):
        return (((zz * 2 + yy) * 2 + xx) * 2 + cc,)

    core_peer = device(z, y, x, 1 - core)
    x_peer = device(z, y, 1 - x, core)
    y_peer = device(z, 1 - y, x, core)

    barrier = pltpu.get_barrier_semaphore()

    def greet(d, carry):
        pl.semaphore_signal(barrier, inc=1, device_id=(lax.rem(rank + d, N_DEV),), device_id_type=MESH)
        return carry

    lax.fori_loop(1, N_DEV, greet, 0)

    waiting = {}
    count = [0]

    def fetch(name, src, dst):
        copy = pltpu.make_async_copy(src, dst, sems.at[count[0]])
        count[0] += 1
        copy.start()
        waiting.setdefault(name, []).append(copy)

    def need(*names):
        for name in names:
            for copy in waiting.pop(name, []):
                copy.wait()

    def halves(name, src, dst):
        for h in range(2):
            fetch(name, src(pl.ds(128 * h, 128)), dst.at[h])

    fetchers = {
        'mid0': lambda: fetch('mid0', g_mid.at[pl.ds(0, 8)], s_mid.at[pl.ds(0, 8)]),
        'mid1': lambda: fetch('mid1', g_mid.at[pl.ds(8, 8)], s_mid.at[pl.ds(8, 8)]),
        'mid2': lambda: fetch('mid2', g_mid.at[pl.ds(16, 2)], s_mid.at[pl.ds(16, 2)]),
        'in': lambda: fetch('in', g_in, s_in),
        'in0': lambda: fetch('in0', g_in0, s_in0),
        'out': lambda: halves('out', lambda c: g_out.at[:, :, c], s_out),
        'short': lambda: halves('short', lambda c: g_short.at[:, c], s_short),
        'fc': lambda: (fetch('fc', pooled, s_x), fetch('fc', dlog_t, s_d)),
        'bn': lambda: fetch('bn', g_bn, s_bn),
    }
    units = [(0, 72, ('mid0',)), (72, 144, ('mid1',)), (144, 168, ('mid2', 'in0', 'in'))]
    units += [(168 + 8 * j, 176 + 8 * j, ('in',)) for j in range(8)]
    units += [(232 + 8 * j, 240 + 8 * j, ('out',)) for j in range(9)]
    units += [(304, 312, ('short',)), (312, 320, ('fc',)), (320, 328, ('bn', 'fc'))]
    for at, size, _ in CHUNKS:
        for lo, hi, names in units:
            if at <= lo < at + size:
                for name in names:
                    if name in fetchers:
                        fetchers.pop(name)()

    mid_at = pl.multiple_of((18 * rank) // 8 * 8, 8)
    mid_off = lax.rem(18 * rank, 8)
    out_at = pl.multiple_of((2 * rank) // 8 * 8, 8)
    out_off = 2 * lax.rem(rank, 4)
    short_at = pl.multiple_of((4 * rank) // 8 * 8, 8)
    short_off = 4 * lax.rem(rank, 2)
    col_at = pl.multiple_of((rank // 16) * 128, 128)
    col_off = pl.multiple_of(lax.rem(rank, 16) * 8, 8)
    fetch('own', w_mid.at[:, pl.ds(mid_at, 24), :], o_mid)
    fetch('own', w_in.at[:, :, pl.ds(col_at, 128)], o_in)
    fetch('own', w_in0, o_in0)
    halves('own', lambda c: w_out.at[:, pl.ds(out_at, 8), c], o_out)
    halves('own', lambda c: w_short.at[pl.ds(short_at, 8), c], o_short)
    fetch('own', w_fc.at[:, pl.ds(col_at, 128)], o_fc)
    fetch('own', w_bn, o_bn)
    fetch('own', w_bias, o_bias)
    for src, dst in ((v_mid, p_mid), (v_in, p_in), (v_in0, p_in0), (v_out, p_out), (v_short, p_short), (v_fc, p_fc),
                     (v_bn, p_bn), (v_bias, p_bias)):
        fetch('own', src, dst)

    pieces = packed.reshape(N_DEV * ROWS, LANES)

    def pack_mid(first, last):
        def body(t, carry):
            for a in range(4):
                for k in range(9):
                    even = s_mid[t, pl.ds(144 * a + 2 * k, 8, stride=18), :]
                    odd = s_mid[t, pl.ds(144 * a + 2 * k + 1, 8, stride=18), :]
                    pieces[across(a, MID + 9 * t + k), :] = jnp.concatenate([even, odd], axis=1)
            return carry

        lax.fori_loop(first, last, body, 0)

    def pack_in_rows(t, pair):
        for a in range(4):
            for k in range(4):
                even = xt[pl.ds(64 * a + 2 * k, 8, stride=8), :]
                odd = xt[pl.ds(64 * a + 2 * k + 1, 8, stride=8), :]
                pieces[across(a, IN + 4 * t + k), :] = left(even, odd)
                if pair:
                    pieces[across(a, IN + 4 * t + 4 + k), :] = right(even, odd)

    def pack_in(first, last):
        def body(j, carry):
            t = 2 * j + 1
            both = jnp.concatenate([s_in[t], s_in[t + 1]], axis=0)
            for h in range(2):
                xt[128 * h:128 * h + 128, :] = both[:, 128 * h:128 * h + 128].T
            pack_in_rows(t, True)
            return carry

        lax.fori_loop(first, last, body, 0)

    def pack_in_first():
        both = jnp.concatenate([s_in[0], jnp.concatenate([s_in0[...], s_in0[...]], axis=1)], axis=0)
        for h in range(2):
            xt[128 * h:128 * h + 128, :] = both[:, 128 * h:128 * h + 128].T
        pack_in_rows(0, False)
        for a in range(4):
            for k in range(2):
                even = xt[pl.ds(32 * a + 2 * k, 8, stride=4), :]
                odd = xt[pl.ds(32 * a + 2 * k + 1, 8, stride=4), :]
                pieces[across(a, IN0 + k), :] = right(even, odd)

    def pack_out(first, last):
        def body(t, carry):
            for a in range(4):
                for p in range(2):
                    for h in range(2):
                        pieces[across(a, OUT + 4 * t + 2 * p + h), :] = s_out[h, t, pl.ds(16 * a + p, 8, stride=2), :]
            return carry

        lax.fori_loop(first, last, body, 0)

    def pack_short():
        for a in range(4):
            for p in range(4):
                for h in range(2):
                    pieces[across(a, SHORT + 2 * p + h), :] = s_short[h, pl.ds(32 * a + p, 8, stride=4), :]

    scale = 1.0 / pooled.shape[0]

    def pack_fc():
        fct[CLASSES:LANES, :] = jnp.zeros((LANES - CLASSES, 256), F32)
        fct[0:CLASSES, :] = jnp.dot(s_d[...], s_x[...], preferred_element_type=F32) * scale
        for h in range(2):
            cols = fct[:, 128 * h:128 * h + 128].T
            for j in range(16):
                at = (16 * h + j) * ROWS + FC
                pieces[at:at + 8, :] = cols[8 * j:8 * j + 8, :]

    def pack_bn():
        for i in range(N_DEV):
            pieces[i * ROWS + BN:i * ROWS + ROWS, :] = jnp.zeros((8, LANES), F32)
        for b in range(2):
            for k in range(4):
                for half in range(2):
                    pieces[pl.ds((16 * b + half) * ROWS + BN + k, 8, stride=2 * ROWS), :] = (
                        s_bn[pl.ds(56 * b + 3 * half + k, 8, stride=7), :])
        bias = lax.dot_general(jnp.ones((8, s_d.shape[1]), jnp.bfloat16), s_d[...], (((1,), (1,)), ((), ())),
                               preferred_element_type=F32) * scale
        bias = jnp.concatenate([bias, jnp.zeros((8, LANES - CLASSES), F32)], axis=1)
        for a in range(4):
            pieces[across(a, BIAS), :] = bias

    def pack(at, size):
        end = at + size
        for lo, hi, names in units:
            if at <= lo < end:
                need(*names)
        for lo, first, last in ((0, 0, 8), (72, 8, 16), (144, 16, 18)):
            if at <= lo < end:
                pack_mid(first, last)
        if at <= 144 < end:
            pack_in_first()
        lo, hi = max(at, 168), min(end, 232)
        if lo < hi:
            pack_in((lo - 168) // 8, (hi - 168) // 8)
        lo, hi = max(at, OUT), min(end, SHORT)
        if lo < hi:
            pack_out((lo - OUT) // 4, (hi - OUT) // 4)
        if at <= SHORT < end:
            pack_short()
        if at <= FC < end:
            pack_fc()
        if at <= BN < end:
            pack_bn()

    lane_row = lax.broadcasted_iota(jnp.int32, (1, LANES), 1)

    def own_pieces():
        need('own')
        for ref, base, tiles, tensors in ((p_mid, MID, 9, N_MID), (p_in, IN, 4, N_IN), (p_out, OUT, 4, N_OUT)):
            for m in range(tiles):
                for t in range(0, tensors, 8):
                    size = min(8, tensors - t)
                    v_own[pl.ds(base + tiles * t + m, size, stride=tiles), :] = (
                        ref[t:t + size, 128 * m:128 * m + 128])
        v_own[IN0:IN0 + 2, :] = p_in0[...]
        v_own[SHORT:SHORT + 8, :] = p_short[...]
        flat = [p_fc[pl.ds(128 * q, 128)].reshape(1, LANES) for q in range(6)]
        flat.append(jnp.concatenate([p_fc[pl.ds(768, 32)].reshape(1, 32), jnp.zeros((1, 96), F32)], axis=1))
        for r in range(8):
            q, s = divmod(CLASSES * r, LANES)
            row = pltpu.roll(flat[q], (LANES - s) % LANES, 1)
            if s + CLASSES > LANES:
                row = jnp.where(lane_row < LANES - s, row, pltpu.roll(flat[q + 1], LANES - s, 1))
            v_own[FC + r:FC + r + 1, :] = jnp.where(lane_row < CLASSES, row, 0.0)
        v_own[BN:ROWS, :] = jnp.zeros((8, LANES), F32)
        odd = lax.rem(rank, 2) == 1
        rows = [p_bn[pl.ds(128 * k, 128)].reshape(1, LANES) for k in range(3)]
        rows.append(jnp.concatenate([p_bn[pl.ds(384, 64)].reshape(1, 64), jnp.zeros((1, 64), F32)], axis=1))
        for k in range(4):
            before = pltpu.roll(rows[k - 1], 64, 1) if k else jnp.zeros((1, LANES), F32)
            moved = jnp.where(lane_row < 64, before, pltpu.roll(rows[k], 64, 1))
            v_own[BN + k:BN + k + 1, :] = jnp.where(odd, moved, rows[k])
        four = jnp.concatenate([p_bias[...].reshape(1, 4), jnp.zeros((1, LANES - 4), F32)], axis=1)
        v_own[BIAS:BIAS + 1, :] = pltpu.roll(four, 4 * rank, 1)

        for t in range(N_MID):
            even = o_mid[t, pl.ds(mid_off, 9, stride=2), :]
            odds = o_mid[t, pl.ds(mid_off + 1, 9, stride=2), :]
            w_own[MID + 9 * t:MID + 9 * t + 9, :] = jnp.concatenate([even, odds], axis=1)
        for j in range(9):
            other = o_in[2 * j - 1] if j else o_in0[...]
            ot[...] = jnp.concatenate([other, o_in[2 * j]], axis=0).T
            if j == 0:
                w_own[IN0:IN0 + 2, :] = left(ot[pl.ds(4 * rank, 2, stride=2), :], ot[pl.ds(4 * rank + 1, 2, stride=2), :])
            even = ot[pl.ds(col_off, 4, stride=2), :]
            odds = ot[pl.ds(col_off + 1, 4, stride=2), :]
            if j:
                w_own[IN + 8 * j - 4:IN + 8 * j, :] = left(even, odds)
            w_own[IN + 8 * j:IN + 8 * j + 4, :] = right(even, odds)
        for p in range(2):
            for h in range(2):
                for t in range(N_OUT):
                    at = OUT + 4 * t + 2 * p + h
                    w_own[at:at + 1, :] = o_out[h, t, pl.ds(out_off + p, 1), :]
        for p in range(4):
            for h in range(2):
                w_own[SHORT + 2 * p + h:SHORT + 2 * p + h + 1, :] = o_short[h, pl.ds(short_off + p, 1), :]
        ot[0:CLASSES, :] = o_fc[...]
        ot[CLASSES:LANES, :] = jnp.zeros((LANES - CLASSES, LANES), F32)
        ot[...] = ot[...].T
        w_own[FC:FC + 8, :] = ot[pl.ds(col_off, 8), :]
        w_own[BN:ROWS, :] = jnp.zeros((8, LANES), F32)
        bn_at = 7 * (rank // 2) + 3 * lax.rem(rank, 2)
        for k in range(4):
            w_own[BN + k:BN + k + 1, :] = o_bn[pl.ds(bn_at + k, 1), :]
        bias = jnp.concatenate([o_bias[...].reshape(1, CLASSES), jnp.zeros((1, LANES - CLASSES), F32)], axis=1)
        w_own[BIAS:BIAS + 1, :] = jnp.where((lane_row >= 4 * rank) & (lane_row < 4 * rank + 4), bias, 0.0)

    copies = {}
    outs = []

    def start(c, k, src, dst, peer):
        copy = pltpu.make_async_remote_copy(src_ref=src, dst_ref=dst, send_sem=send.at[c * N_SEMS + k],
                                            recv_sem=recv.at[c * N_SEMS + k], device_id=peer, device_id_type=MESH)
        copy.start()
        copies[c, k] = copy

    def arrived(c, k):
        copies[c, k].wait_recv()

    def keep(src, dst):
        copy = pltpu.make_async_copy(src, dst, out_sems.at[len(outs)])
        copy.start()
        outs.append(copy)

    def step(c, stage):
        at, size, first = CHUNKS[c]
        rows = pl.ds(at, size)
        x_first = first == 'x'
        one_peer, two_peer = (x_peer, y_peer) if x_first else (y_peer, x_peer)

        def half(zz, yx, mine):
            return (zz, yx, x if mine else 1 - x) if x_first else (zz, y if mine else 1 - y, yx)

        if stage == 0:
            pack(at, size)
            if not copies:
                pl.semaphore_wait(barrier, N_DEV - 1)
            start(c, S_CORE, packed.at[:, :, :, 1 - core, rows, :], got_core.at[:, :, :, rows, :], core_peer)
        elif stage == 1:
            arrived(c, S_CORE)

            def add(mine):
                def body(m, carry):
                    zz, yx = m // 2, lax.rem(m, 2)
                    a, b, d = half(zz, yx, mine)
                    acc[a, b, d, rows, :] = packed[a, b, d, core, rows, :] + got_core[a, b, d, rows, :]
                    return carry

                lax.fori_loop(0, 8, body, 0)

            add(False)
            src = acc.at[:, :, 1 - x, rows, :] if x_first else acc.at[:, 1 - y, :, rows, :]
            start(c, S_ONE, src, got_one.at[:, :, rows, :], one_peer)
            add(True)
        elif stage == 2:
            arrived(c, S_ONE)

            def add(other):
                def body(zz, carry):
                    a, b, d = half(zz, other, True)
                    acc[a, b, d, rows, :] = acc[a, b, d, rows, :] + got_one[zz, other, rows, :]
                    return carry

                lax.fori_loop(0, 4, body, 0)

            here = y if x_first else x
            add(1 - here)
            src = acc.at[:, 1 - y, x, rows, :] if x_first else acc.at[:, y, 1 - x, rows, :]
            start(c, S_TWO, src, got_two.at[:, rows, :], two_peer)
            add(here)
        elif stage == 3:
            arrived(c, S_TWO)
            for d in (1, 2, 3, 0):
                zz = lax.rem(z + d, 4)
                acc[zz, y, x, rows, :] = acc[zz, y, x, rows, :] + got_two[zz, rows, :]
                if d:
                    start(c, S_Z + d, acc.at[zz, y, x, rows, :], got_z.at[d - 1, rows, :], device(zz, y, x, core))
        elif stage == 4:
            for d in (1, 2, 3):
                arrived(c, S_Z + d)
            mean = (acc[z, y, x, rows, :] + got_z[0, rows, :] + got_z[1, rows, :] + got_z[2, rows, :]) * (1.0 / N_DEV)
            grad[rows, :] = mean
            own = w_own[rows, :]
            g_sum = jnp.sum(mean * mean, axis=1, keepdims=True)
            w_sum = jnp.sum(own * own, axis=1, keepdims=True)
            row = lax.broadcasted_iota(jnp.int32, (size, LANES), 0) + at
            lane = lax.broadcasted_iota(jnp.int32, (size, LANES), 1)
            tensor = jnp.where(lane < 64, lane, lane - 64)
            member = (row >= first_row(tensor)) & (row < first_row(tensor + 1))
            part = jnp.where(member, jnp.where(lane < 64, g_sum, w_sum), 0.0)
            norms[c, rank] = jnp.sum(part, axis=0, keepdims=True)

            def tell(d, carry):
                pltpu.make_async_remote_copy(
                    src_ref=norms.at[c, rank], dst_ref=norms.at[c, rank], send_sem=n_send.at[c],
                    recv_sem=n_recv.at[c], device_id=(lax.rem(rank + d, N_DEV),), device_id_type=MESH).start()
                return carry

            lax.fori_loop(1, N_DEV, tell, 0)
        elif stage == 5:
            others = norms.at[c, pl.ds(0, N_DEV - 1)]
            pltpu.make_async_copy(others, others, n_recv.at[c]).wait()
            total = jnp.sum(norms[c], axis=0)
            g_norm = jnp.sqrt(total)
            w_norm = pltpu.roll(g_norm, 64, 1)
            trust = jnp.where((w_norm > 0) & (g_norm > 0), TRUST_COEF * w_norm / (g_norm + DECAY * w_norm), 1.0)
            row = lax.broadcasted_iota(jnp.int32, (size, LANES), 0) + at
            lane = lax.broadcasted_iota(jnp.int32, (size, LANES), 1)
            trust = jnp.where(lane == ID_PLAIN, 1.0, trust)
            member = (row >= first_row(lane)) & (row < first_row(lane + 1)) & (lane <= ID_PLAIN)
            rate = lr[0] * jnp.sum(jnp.where(member, trust, 0.0), axis=1, keepdims=True)
            decay = jnp.where(row < BN, DECAY, 0.0)
            own = w_own[rows, :]
            moment = MOMENTUM * v_own[rows, :] + rate * (grad[rows, :] + decay * own)
            v_new[rows, :] = moment
            keep(v_new.at[rows, :], v_out_rows.at[rows, :])
            mine = (row != BIAS) | ((lane >= 4 * rank) & (lane < 4 * rank + 4))
            full[z, y, x, core, rows, :] = jnp.where(mine, own - moment, 0.0)
            for d in (1, 2, 3):
                piece = full.at[z, y, x, core, rows, :]
                start(c, A_Z + d, piece, piece, device(lax.rem(z + d, 4), y, x, core))
        elif stage == 6:
            for d in (1, 2, 3):
                arrived(c, A_Z + d)
            pieces = full.at[:, y, x, core, rows, :]
            start(c, A_TWO, pieces, pieces, two_peer)
        elif stage == 7:
            arrived(c, A_TWO)
            pieces = full.at[:, :, x, core, rows, :] if x_first else full.at[:, y, :, core, rows, :]
            start(c, A_ONE, pieces, pieces, one_peer)
        elif stage == 8:
            arrived(c, A_ONE)
            pieces = full.at[:, :, :, core, rows, :]
            start(c, A_CORE, pieces, pieces, core_peer)
        else:
            arrived(c, A_CORE)
            keep(full.at[:, :, :, :, rows, :], full_out.at[:, :, :, :, rows, :])

    for c, stage in STEPS:
        if stage == 3 and not any(k[1] == S_Z + 1 for k in copies):
            own_pieces()
        step(c, stage)
    for copy in copies.values():
        copy.wait_send()
    for c in range(len(CHUNKS)):
        others = norms.at[c, pl.ds(0, N_DEV - 1)]
        pltpu.make_async_copy(others, others, n_send.at[c]).wait()
    for copy in outs:
        copy.wait()


def exchange(operands):
    any_ = pl.BlockSpec(memory_space=pl.ANY)
    count = len(CHUNKS)
    bf = jnp.bfloat16
    shapes = [(N_MID, 576, 64), (N_IN, 64, 256), (64, 128), (2, N_OUT, 64, 128), (2, 128, 128), (112, 128)]
    own = [(N_MID, 24, 64), (N_IN, 64, 128), (64, 128), (2, N_OUT, 8, 128), (2, 8, 128), (CLASSES, 128), (112, 128),
           (CLASSES,), (128, 128), (N_MID, 1152), (N_IN, 512), (2, LANES), (N_OUT, 512), (8, LANES), (800,), (448,), (4,)]
    rows = (ROWS, LANES)
    exchanged = [(4, 2, 2) + rows, (4, 2, 2) + rows, (4, 2) + rows, (4,) + rows, (3,) + rows, rows,
                 (count, N_DEV, 1, LANES)]
    dma = pltpu.SemaphoreType.DMA
    full, v_new = pl.pallas_call(
        exchange_kernel,
        out_shape=(jax.ShapeDtypeStruct((4, 2, 2, 2) + rows, F32), jax.ShapeDtypeStruct(rows, F32)),
        in_specs=[pl.BlockSpec(memory_space=pltpu.SMEM)] + [any_] * 24,
        out_specs=(any_, any_),
        scratch_shapes=[VMEM(s, F32) for s in shapes]
        + [VMEM((1024, 256), bf), VMEM((CLASSES, 1024), bf), VMEM((256, 128), F32), VMEM((128, 256), F32)]
        + [VMEM(s, F32) for s in own]
        + [VMEM((4, 2, 2, 2) + rows, F32), VMEM(rows, F32), VMEM(rows, F32), VMEM(rows, F32),
           VMEM((4, 2, 2, 2) + rows, F32)]
        + [VMEM(s, F32) for s in exchanged]
        + [dma((32,)), dma((2 * count,)), dma((count * N_SEMS,)), dma((count * N_SEMS,)), dma((count,)), dma((count,))],
        compiler_params=pltpu.CompilerParams(vmem_limit_bytes=VMEM_LIMIT, collective_id=0, has_side_effects=True),
    )(*operands)
    return full.reshape(N_DEV, ROWS, LANES), v_new


def unpack_kernel(packed_rows, v_rows, n_mid, n_in, n_in0, n_out, n_short, n_fc, n_bn, n_bias,
                  b_mid, b_in, b_in0, b_out, b_short, b_fc, v_mid, v_in, v_in0, v_out, v_short, v_fc, v_bn, v_bias,
                  packed, v_own, s_mid, s_in, s_out, s_short, s_in0, s_fc, t_mid, t_in, t_out, t_short, t_in0, t_fc, xt, sems):
    bf = jnp.bfloat16
    lane_row = lax.broadcasted_iota(jnp.int32, (1, LANES), 1)
    pieces = packed.reshape(N_DEV, ROWS, LANES)
    fetches = []
    for k, (at, size) in enumerate(((0, 40), (40, 104), (144, 24), (168, 64), (232, 72), (304, 24))):
        fetches.append(pltpu.make_async_copy(packed_rows.at[:, pl.ds(at, size), :], pieces.at[:, pl.ds(at, size), :],
                                             sems.at[12 + k]))
    fetches.append(pltpu.make_async_copy(v_rows, v_own, sems.at[18]))
    for copy in fetches:
        copy.start()

    def put(src, dst, k):
        pltpu.make_async_copy(src, dst, sems.at[k]).start()

    def mid_body(t, carry):
        for a in range(4):
            for k in range(9):
                x = packed[across(a, MID + 9 * t + k), :]
                s_mid[t, pl.ds(144 * a + 2 * k, 8, stride=18), :] = x[:, :64]
                s_mid[t, pl.ds(144 * a + 2 * k + 1, 8, stride=18), :] = x[:, 64:]
        put(s_mid.at[t], n_mid.at[t], 0)
        t_mid[t] = s_mid[t].astype(bf)
        put(t_mid.at[t], b_mid.at[t], 1)
        return carry

    fetches[0].wait()
    lax.fori_loop(0, 4, mid_body, 0)
    fetches[1].wait()
    lax.fori_loop(4, 15, mid_body, 0)
    fetches[2].wait()
    lax.fori_loop(15, N_MID, mid_body, 0)
    fetches[3].wait()

    def in_rows(t, other):
        for a in range(4):
            for k in range(4):
                x = packed[across(a, IN + 4 * t + k), :]
                y = packed[across(a, IN + 4 * other + k), :]
                xt[pl.ds(64 * a + 2 * k, 8, stride=8), :] = left(x, y)
                xt[pl.ds(64 * a + 2 * k + 1, 8, stride=8), :] = right(x, y)

    def in_body(j, carry):
        t = 2 * j + 1
        in_rows(t, t + 1)
        for h in range(2):
            cols = xt[128 * h:128 * h + 128, :].T
            for u in range(2):
                s_in[t + u, :, 128 * h:128 * h + 128] = cols[64 * u:64 * u + 64]
                t_in[t + u, :, 128 * h:128 * h + 128] = cols[64 * u:64 * u + 64].astype(bf)
        for u in range(2):
            put(s_in.at[t + u], n_in.at[t + u], 2)
            put(t_in.at[t + u], b_in.at[t + u], 3)
        return carry

    lax.fori_loop(0, 8, in_body, 0)
    in_rows(0, 0)
    for h in range(2):
        cols = xt[128 * h:128 * h + 128, :].T
        s_in[0, :, 128 * h:128 * h + 128] = cols[:64]
        t_in[0, :, 128 * h:128 * h + 128] = cols[:64].astype(bf)
    put(s_in.at[0], n_in.at[0], 2)
    put(t_in.at[0], b_in.at[0], 3)
    for a in range(4):
        for k in range(2):
            x = packed[across(a, IN0 + k), :]
            xt[pl.ds(32 * a + 2 * k, 8, stride=4), :] = x
            xt[pl.ds(32 * a + 2 * k + 1, 8, stride=4), :] = right(x, x)
    cols = xt[0:128, :].T
    s_in0[...] = cols[:64]
    t_in0[...] = cols[:64].astype(bf)
    put(s_in0, n_in0, 4)
    put(t_in0, b_in0, 5)

    def out_body(t, carry):
        for a in range(4):
            for p in range(2):
                for h in range(2):
                    s_out[h, t, pl.ds(16 * a + p, 8, stride=2), :] = packed[across(a, OUT + 4 * t + 2 * p + h), :]
        for h in range(2):
            t_out[h, t] = s_out[h, t].astype(bf)
            put(s_out.at[h, t], n_out.at[t, :, pl.ds(128 * h, 128)], 6)
            put(t_out.at[h, t], b_out.at[t, :, pl.ds(128 * h, 128)], 7)
        return carry

    fetches[4].wait()
    lax.fori_loop(0, N_OUT, out_body, 0)
    fetches[5].wait()
    for h in range(2):
        for a in range(4):
            for p in range(4):
                s_short[h, pl.ds(32 * a + p, 8, stride=4), :] = packed[across(a, SHORT + 2 * p + h), :]
        t_short[h] = s_short[h].astype(bf)
        put(s_short.at[h], n_short.at[:, pl.ds(128 * h, 128)], 8)
        put(t_short.at[h], b_short.at[:, pl.ds(128 * h, 128)], 9)
    for i in range(N_DEV):
        xt[8 * i:8 * i + 8, :] = packed[i * ROWS + FC:i * ROWS + FC + 8, :]
    for h in range(2):
        cols = xt[128 * h:128 * h + 128, :].T
        s_fc[:, 128 * h:128 * h + 128] = cols[:CLASSES]
        t_fc[:, 128 * h:128 * h + 128] = cols[:CLASSES].astype(bf)
    put(s_fc, n_fc, 10)
    put(t_fc, b_fc, 11)

    lane = lax.broadcasted_iota(jnp.int32, (8, LANES), 1)
    for b in range(2):
        def even(k):
            return packed[pl.ds(16 * b * ROWS + BN + k, 8, stride=2 * ROWS), :]

        def odd(k):
            return packed[pl.ds((16 * b + 1) * ROWS + BN + k, 8, stride=2 * ROWS), :]

        for k in range(3):
            n_bn[pl.ds(56 * b + k, 8, stride=7), :] = even(k)
            n_bn[pl.ds(56 * b + 4 + k, 8, stride=7), :] = odd(1 + k)
        n_bn[pl.ds(56 * b + 3, 8, stride=7), :] = jnp.where(lane < 64, even(3), odd(0))
    total = packed[across(0, BIAS), :]
    for a in range(1, 4):
        total = total + packed[across(a, BIAS), :]
    n_bias[...] = jnp.sum(total, axis=0, keepdims=True)[0, :CLASSES]
    fetches[6].wait()

    for ref, base, tiles, count in ((v_mid, MID, 9, N_MID), (v_in, IN, 4, N_IN), (v_out, OUT, 4, N_OUT)):
        for m in range(tiles):
            for t in range(0, count, 8):
                size = min(8, count - t)
                ref[t:t + size, 128 * m:128 * m + 128] = v_own[pl.ds(base + tiles * t + m, size, stride=tiles), :]
    rank = lax.axis_index('dp')
    v_in0[...] = v_own[IN0:IN0 + 2, :]
    v_short[...] = v_own[SHORT:SHORT + 8, :]
    for q in range(7):
        flat = jnp.zeros((1, LANES), F32)
        for r in range(8):
            d = CLASSES * r - LANES * q
            if -CLASSES < d < LANES:
                row = pltpu.roll(v_own[FC + r:FC + r + 1, :], d % LANES, 1)
                flat = jnp.where((lane_row >= d) & (lane_row < d + CLASSES), row, flat)
        size = min(LANES, 800 - LANES * q)
        v_fc[pl.ds(LANES * q, size)] = flat[0, :size]
    odd = lax.rem(rank, 2) == 1
    for k in range(4):
        here = v_own[BN + k:BN + k + 1, :]
        after = v_own[BN + k + 1:BN + k + 2, :]
        moved = jnp.where(lane_row < 64, pltpu.roll(here, 64, 1), pltpu.roll(after, 64, 1))
        size = min(LANES, 448 - LANES * k)
        v_bn[pl.ds(LANES * k, size)] = jnp.where(odd, moved, here)[0, :size]
    v_bias[...] = pltpu.roll(v_own[BIAS:BIAS + 1, :], lax.rem(N_DEV - rank, N_DEV) * 4, 1)[0, :4]

    for k, (src, dst) in enumerate(((s_mid, n_mid), (t_mid, b_mid), (s_in, n_in), (t_in, b_in), (s_in0, n_in0),
                                    (t_in0, b_in0))):
        pltpu.make_async_copy(src, dst, sems.at[k]).wait()
    for h in range(2):
        half = pl.ds(128 * h, 128)
        for k, (src, dst) in enumerate(((s_out, n_out.at[:, :, half]), (t_out, b_out.at[:, :, half]),
                                        (s_short, n_short.at[:, half]), (t_short, b_short.at[:, half]))):
            pltpu.make_async_copy(src.at[h], dst, sems.at[6 + k]).wait()
    pltpu.make_async_copy(s_fc, n_fc, sems.at[10]).wait()
    pltpu.make_async_copy(t_fc, b_fc, sems.at[11]).wait()


def unpack_weights(packed, v_own):
    any_ = pl.BlockSpec(memory_space=pl.ANY)
    vm = pl.BlockSpec(memory_space=VMEM)
    bf = jnp.bfloat16
    kernels = ((N_MID, 576, 64), (N_IN, 64, 256), (64, 128), (N_OUT, 64, 256), (128, 256), (CLASSES, 256))
    shapes = [(s, F32) for s in kernels] + [((112, 128), F32), ((CLASSES,), F32)] + [(s, bf) for s in kernels]
    shapes += [(s, F32) for s in ((N_MID, 1152), (N_IN, 512), (2, LANES), (N_OUT, 512), (8, LANES), (800,), (448,), (4,))]
    scratch = ((N_MID, 576, 64), (N_IN, 64, 256), (2, N_OUT, 64, 128), (2, 128, 128), (64, 128), (CLASSES, 256))
    return pl.pallas_call(
        unpack_kernel,
        out_shape=[jax.ShapeDtypeStruct(s, d) for s, d in shapes],
        in_specs=[any_, any_],
        out_specs=[any_] * 6 + [vm] * 2 + [any_] * 6 + [vm] * 8,
        scratch_shapes=[VMEM((N_DEV * ROWS, LANES), F32), VMEM((ROWS, LANES), F32)] + [VMEM(s, F32) for s in scratch] + [VMEM(s, bf) for s in scratch]
        + [VMEM((256, 128), F32), pltpu.SemaphoreType.DMA((19,))],
        compiler_params=pltpu.CompilerParams(vmem_limit_bytes=VMEM_LIMIT),
    )(packed, v_own)


def solution(mesh):
    spec_full = P()
    spec_lead = P('dp')
    spec_cols = P(None, 'dp')
    moment_specs = (spec_lead, spec_lead, spec_cols, spec_cols, spec_cols, spec_lead, spec_lead, spec_lead)
    in_specs = (spec_full,) * 8 + (spec_lead,) * 8 + moment_specs + (spec_full,)
    out_specs = (spec_full,) * 14 + moment_specs

    def body(w_in0, w_short, w_in, w_mid, w_out, w_fc, w_bn, w_bias,
             g_in0, g_short, g_in, g_mid, g_out, g_bn, pooled, dlogits,
             v_in0, v_short, v_in, v_mid, v_out, v_fc, v_bn, v_bias, learn_rate):
        gathered, v_next = exchange((
            learn_rate.reshape(1), g_mid.reshape(N_MID, 576, 64), jnp.swapaxes(g_in[0], 1, 2), g_in0[0].T, g_out[0],
            g_short[0], g_bn.reshape(112, LANES), pooled, dlogits.T,
            w_mid.reshape(N_MID, 576, 64), jnp.swapaxes(w_in, 1, 2), w_in0.T, w_out, w_short, w_fc.T,
            w_bn.reshape(112, LANES), w_bias, v_mid, v_in, v_in0.reshape(2, LANES), v_out, v_short.reshape(8, LANES),
            v_fc, v_bn, v_bias))
        (n_mid, n_in, n_in0, n_out, n_short, n_fc, n_bn, n_bias, b_mid, b_in, b_in0, b_out, b_short, b_fc,
         m_mid, m_in, m_in0, m_out, m_short, m_fc, m_bn, m_bias) = unpack_weights(gathered, v_next)
        return (n_in0.T, n_short, jnp.swapaxes(n_in, 1, 2), n_mid.reshape(w_mid.shape), n_out, n_fc.T,
                n_bn.reshape(-1), n_bias,
                b_in0.T, b_short, jnp.swapaxes(b_in, 1, 2), b_mid.reshape(w_mid.shape), b_out, b_fc.T,
                m_in0.reshape(-1), m_short.reshape(-1), m_in, m_mid, m_out, m_fc, m_bn, m_bias)

    return jax.shard_map(body, mesh=mesh, in_specs=in_specs, out_specs=out_specs, check_vma=False)
```

time: 1250 us -> 89.3 us (0.07)
  waiting for transfers between devices: 956 us -> 0 us
  blocking collectives: 161 us -> 0 us
  Pallas kernels: 0 us -> 87.8 us
  local copies, waits for them, and re-layouts: 85.7 us -> 0 us
  other arithmetic: 27.3 us -> 0 us
  between operations: 19.6 us -> 1.32 us
    unnamed x14 -> x0, waiting for transfers between devices: 414 us -> none
    reduce_scatter x3 -> x0, waiting for transfers between devices: 378 us -> none  [body(): lax.psum_scatter(gradient.reshape(count, -1), 'dp', scatter_dimension=1,...]
    all_gather x3 -> x0, waiting for transfers between devices: 164 us -> none  [body(): lax.all_gather(w_part - moment_next, 'dp', axis=1, tiled=True)]
    pallas_call x0 -> x2, Pallas kernels: none -> 87.8 us  [the longest x1 80.5 us: exchange(): pl.pallas_call(exchange_kernel, out_shape=(jax.ShapeDtypeStruct((4, 2, 2,...]
    all_gather x2 -> x0, blocking collectives: 76.6 us -> none  [body(): lax.all_gather(w_part - moment_next, 'dp', axis=1, tiled=True)]
    unnamed x69 -> x0, local copies, waits for them, and re-layouts: 44.5 us -> none
    unnamed x1 -> x0, blocking collectives: 43 us -> none
    psum x1 -> x0, blocking collectives: 41 us -> none  [body(): sq_total = lax.psum(jnp.concatenate(squares), 'dp')]
  transfers between devices with their start and end apart: 10 -> 0, of which waited for: 10 -> 0; matrix products, arithmetic and copies ran while one was open for 7% -> 0% of each run, Pallas kernels for 0% -> 0%
where the time goes in v3:
time: 89.3 us; the launch traced here: 89.1 us
  Pallas kernels  87.8 us (98%)
  between operations  1.32 us (1%)
    pallas_call x1, Pallas kernels, exchange(): pl.pallas_call(exchange_kernel, out_shape=(jax.ShapeDtypeStruct((4, 2, 2,...  80.5 us
    pallas_call x1, Pallas kernels, unpack_weights(): pl.pallas_call(unpack_kernel, out_shape=[jax.ShapeDtypeStruct(s, d) for s...  7.36 us

profile of v3, /device:TPU:0, one launch (start us, length us, event | category | flops | bytes accessed | tf_op | source)
XLA Modules:
  0.0 89.1 jit_solution(7048919616158924931)
XLA Ops:
  1.3 80.5 %shard_map.408 = (f32[4,2,2,2,328,128]{5,4,3,2,1,0:T(8,128)}, f32[328,128]{1,0:T(8,128)}) custom-call(f32[1]{0:T(128)} %bitcast.31.lr, f32[18,576,64]{2,1,0:T(8,128)} %bitcast.33, f32[17,64,256]{2,1,0:T(8,128)} %bitcast.36, f32[64,128]{1,0:T(8,128)} %bitcast.43, f32[18,64,256]{2,1,0:T(8,128)} %bitcast.35, f32[128,256]{1,0:T(8,128)} %bitcast.39, ...), custom_call_target="tpu_custom_call" | custom-call | tf_op jit(solution)/shard_map/pallas_call | solution.py:469
  81.8 7.4 %shard_map.409 = (f32[18,576,64]{2,1,0:T(8,128)}, f32[17,64,256]{2,1,0:T(8,128)}, f32[64,128]{1,0:T(8,128)}, f32[18,64,256]{2,1,0:T(8,128)}, f32[128,256]{1,0:T(...) custom-call(f32[32,328,128]{2,1,0:T(8,128)} %bitcast.32, ...), custom_call_target="tpu_custom_call" | custom-call | tf_op jit(solution)/shard_map/pallas_call | solution.py:656

commit v4 on v3

--- a/solution.py
+++ b/solution.py
@@ -10,30 +10,60 @@
 DECAY = 0.0001
 N_DEV = 32
 LANES = 128
-MID, IN0, IN, OUT, SHORT, FC, BN, BIAS, ROWS = 0, 162, 164, 232, 304, 312, 320, 324, 328
+IN0, OUT, SHORT, FC, BN, BIAS, ROWS = 178, 232, 304, 312, 320, 324, 328
 N_MID, N_IN, N_OUT = 18, 17, 18
 CLASSES = 100
 ID_IN0, ID_IN, ID_OUT, ID_SHORT, ID_FC, ID_PLAIN = 18, 19, 36, 54, 55, 56
 F32 = jnp.float32
 VMEM = pltpu.VMEM
 MESH = pl.DeviceIdType.MESH
-CHUNKS = ((0, 72, 'x'), (72, 72, 'y'), (144, 48, 'x'), (192, 48, 'y'), (240, 48, 'x'), (288, 40, 'y'))
+CHUNKS = (
+    (0, 40, 'x'), (40, 40, 'y'), (80, 40, 'y'), (120, 40, 'x'), (160, 24, 'x'),
+    (184, 24, 'y'), (208, 24, 'x'), (232, 24, 'y'), (256, 24, 'y'), (280, 24, 'x'),
+    (304, 24, 'y'),
+)
 STEPS = (
-    (0, 0), (1, 0), (0, 1), (4, 0), (2, 0), (3, 0), (4, 1), (1, 1), (0, 2), (3, 1), (1, 2), (0, 3), (2, 1), (4, 2),
-    (5, 0), (1, 3), (5, 1), (3, 2), (4, 3), (2, 2), (3, 3), (1, 4), (5, 2), (2, 3), (0, 4), (4, 4), (5, 3), (1, 5),
-    (3, 4), (0, 5), (2, 4), (5, 4), (3, 5), (1, 6), (5, 5), (0, 6), (2, 5), (1, 7), (3, 6), (0, 7), (4, 5), (2, 6),
-    (4, 6), (1, 8), (5, 6), (3, 7), (2, 7), (4, 7), (5, 7), (2, 8), (1, 9), (0, 8), (2, 9), (3, 8), (5, 8), (0, 9),
-    (3, 9), (4, 8), (5, 9), (4, 9),
+    (10, 0), (9, 0), (8, 0), (10, 1), (9, 1), (4, 0), (6, 0), (8, 1), (4, 1), (7, 0), (2, 0), (10, 2), (9, 2), (7, 1),
+    (6, 1), (5, 0), (8, 2), (3, 0), (4, 2), (2, 1), (9, 3), (7, 2), (3, 1), (10, 3), (0, 0), (8, 3), (6, 2), (1, 0),
+    (4, 3), (2, 2), (5, 1), (7, 3), (9, 4), (10, 4), (3, 2), (6, 3), (8, 4), (5, 2), (1, 1), (2, 3), (4, 4), (0, 1),
+    (7, 4), (3, 3), (5, 3), (6, 4), (9, 5), (1, 2), (0, 2), (10, 5), (2, 4), (8, 5), (3, 4), (1, 3), (5, 4), (9, 6),
+    (0, 3), (10, 6), (7, 5), (4, 5), (8, 6), (6, 5), (10, 7), (1, 4), (3, 5), (8, 7), (9, 7), (0, 4), (7, 6), (10, 8),
+    (5, 5), (2, 5), (4, 6), (6, 6), (7, 7), (3, 6), (1, 5), (5, 6), (0, 5), (4, 7), (8, 8), (2, 6), (10, 9), (6, 7),
+    (5, 7), (1, 6), (3, 7), (0, 6), (7, 8), (2, 7), (4, 8), (9, 8), (7, 9), (1, 7), (5, 8), (8, 9), (0, 7), (6, 8),
+    (6, 9), (2, 8), (3, 8), (1, 8), (0, 8), (3, 9), (2, 9), (1, 9), (5, 9), (9, 9), (4, 9), (0, 9),
 )
-S_CORE, S_ONE, S_TWO, S_Z, A_Z, A_TWO, A_ONE, A_CORE, N_SEMS = 0, 1, 2, 2, 5, 9, 10, 11, 12
+S_CORE, S_ONE, S_TWO, S_Z, A_Z, A_TWO, A_ONE, A_CORE, N_SEMS = 0, 2, 4, 6, 7, 8, 10, 12, 14
 VMEM_LIMIT = 60 * 2**20
 
 
-def first_row(t):
-    out = jnp.where(t < N_MID, 9 * t, IN0)
-    out = jnp.where(t >= ID_IN, IN + 4 * (t - ID_IN), out)
-    out = jnp.where(t >= ID_OUT, OUT + 4 * (t - ID_OUT), out)
-    return jnp.where(t >= ID_SHORT, SHORT + 8 * (t - ID_SHORT), out)
+def mid_row(t):
+    return 40 * (t // 4) + 9 * (t % 4)
+
+
+def in_row(t):
+    return 36 + 40 * t if t < 4 else 164 + 4 * t
+
+
+def member_rows(row, t):
+    first = 9 * t
+    for group in (4, 8, 12, 16):
+        first = jnp.where(t >= group, first + 4, first)
+    size = jnp.where(t < N_MID, 9, jnp.where(t == ID_IN0, 2, jnp.where(t < ID_SHORT, 4, 8)))
+    first = jnp.where(t >= ID_IN0, IN0, first)
+    first = jnp.where(t >= ID_IN, 36 + 40 * (t - ID_IN), first)
+    first = jnp.where(t >= ID_IN + 4, 164 + 4 * (t - ID_IN), first)
+    first = jnp.where(t >= ID_OUT, OUT + 4 * (t - ID_OUT), first)
+    first = jnp.where(t >= ID_SHORT, SHORT + 8 * (t - ID_SHORT), first)
+    return (row >= first) & (row < first + size)
+
+
+def momentum_rows(mid, inn, out):
+    runs = [(mid, mid_row(t), 9, t, min(4, N_MID - t)) for t in range(0, N_MID, 4)]
+    runs += [(inn, 36, 40, 0, 4)] + [(inn, 164 + 4 * t, 4, t, min(8, N_IN - t)) for t in (4, 12)]
+    runs += [(out, OUT + 4 * t, 4, t, min(8, N_OUT - t)) for t in (0, 8, 16)]
+    for ref, base, stride, t, count in runs:
+        for m in range(9 if ref is mid else 4):
+            yield pl.ds(base + m, count, stride=stride), pl.ds(128 * m, 128), ref, pl.ds(t, count)
 
 
 def left(a, b):
@@ -98,18 +128,19 @@
             fetch(name, src(pl.ds(128 * h, 128)), dst.at[h])
 
     fetchers = {
-        'mid0': lambda: fetch('mid0', g_mid.at[pl.ds(0, 8)], s_mid.at[pl.ds(0, 8)]),
-        'mid1': lambda: fetch('mid1', g_mid.at[pl.ds(8, 8)], s_mid.at[pl.ds(8, 8)]),
-        'mid2': lambda: fetch('mid2', g_mid.at[pl.ds(16, 2)], s_mid.at[pl.ds(16, 2)]),
-        'in': lambda: fetch('in', g_in, s_in),
+        'in': lambda: fetch('in', g_in.at[pl.ds(5, 12)], s_in.at[pl.ds(5, 12)]),
+        'in1': lambda: fetch('in1', g_in.at[pl.ds(0, 5)], s_in.at[pl.ds(0, 5)]),
         'in0': lambda: fetch('in0', g_in0, s_in0),
         'out': lambda: halves('out', lambda c: g_out.at[:, :, c], s_out),
         'short': lambda: halves('short', lambda c: g_short.at[:, c], s_short),
         'fc': lambda: (fetch('fc', pooled, s_x), fetch('fc', dlog_t, s_d)),
         'bn': lambda: fetch('bn', g_bn, s_bn),
     }
-    units = [(0, 72, ('mid0',)), (72, 144, ('mid1',)), (144, 168, ('mid2', 'in0', 'in'))]
-    units += [(168 + 8 * j, 176 + 8 * j, ('in',)) for j in range(8)]
+    for i in range(5):
+        part = pl.ds(4 * i, min(4, N_MID - 4 * i))
+        fetchers['mid%d' % i] = lambda i=i, part=part: fetch('mid%d' % i, g_mid.at[part], s_mid.at[part])
+    units = [(40 * i, 40 * i + 40, ('mid%d' % i, 'in1')) for i in range(4)] + [(160, 184, ('mid4', 'in0', 'in1'))]
+    units += [(184 + 8 * j, 192 + 8 * j, ('in',)) for j in range(6)]
     units += [(232 + 8 * j, 240 + 8 * j, ('out',)) for j in range(9)]
     units += [(304, 312, ('short',)), (312, 320, ('fc',)), (320, 328, ('bn', 'fc'))]
     for at, size, _ in CHUNKS:
@@ -141,47 +172,50 @@
 
     pieces = packed.reshape(N_DEV * ROWS, LANES)
 
-    def pack_mid(first, last):
-        def body(t, carry):
+    def pack_mid(base, first, count):
+        def body(u, carry):
+            t = first + u
             for a in range(4):
                 for k in range(9):
                     even = s_mid[t, pl.ds(144 * a + 2 * k, 8, stride=18), :]
                     odd = s_mid[t, pl.ds(144 * a + 2 * k + 1, 8, stride=18), :]
-                    pieces[across(a, MID + 9 * t + k), :] = jnp.concatenate([even, odd], axis=1)
+                    pieces[across(a, base + 9 * u + k), :] = jnp.concatenate([even, odd], axis=1)
             return carry
 
-        lax.fori_loop(first, last, body, 0)
-
-    def pack_in_rows(t, pair):
+        lax.fori_loop(0, count, body, 0)
+
+    def pack_in_rows(base, pair):
         for a in range(4):
             for k in range(4):
                 even = xt[pl.ds(64 * a + 2 * k, 8, stride=8), :]
                 odd = xt[pl.ds(64 * a + 2 * k + 1, 8, stride=8), :]
-                pieces[across(a, IN + 4 * t + k), :] = left(even, odd)
+                pieces[across(a, base + k), :] = left(even, odd)
                 if pair:
-                    pieces[across(a, IN + 4 * t + 4 + k), :] = right(even, odd)
+                    pieces[across(a, base + 4 + k), :] = right(even, odd)
+
+    def transpose(a, b):
+        both = jnp.concatenate([a, b], axis=0)
+        for h in range(2):
+            xt[128 * h:128 * h + 128, :] = both[:, 128 * h:128 * h + 128].T
 
     def pack_in(first, last):
         def body(j, carry):
-            t = 2 * j + 1
-            both = jnp.concatenate([s_in[t], s_in[t + 1]], axis=0)
-            for h in range(2):
-                xt[128 * h:128 * h + 128, :] = both[:, 128 * h:128 * h + 128].T
-            pack_in_rows(t, True)
+            transpose(s_in[2 * j + 5], s_in[2 * j + 6])
+            pack_in_rows(184 + 8 * j, True)
             return carry
 
         lax.fori_loop(first, last, body, 0)
 
-    def pack_in_first():
-        both = jnp.concatenate([s_in[0], jnp.concatenate([s_in0[...], s_in0[...]], axis=1)], axis=0)
-        for h in range(2):
-            xt[128 * h:128 * h + 128, :] = both[:, 128 * h:128 * h + 128].T
-        pack_in_rows(0, False)
-        for a in range(4):
-            for k in range(2):
-                even = xt[pl.ds(32 * a + 2 * k, 8, stride=4), :]
-                odd = xt[pl.ds(32 * a + 2 * k + 1, 8, stride=4), :]
-                pieces[across(a, IN0 + k), :] = right(even, odd)
+    def pack_in_one(t):
+        wide = jnp.concatenate([s_in0[...], s_in0[...]], axis=1) if t == 4 else s_in[t]
+        transpose(s_in[t], wide)
+        pack_in_rows(in_row(t), False)
+        if t == 4:
+            for a in range(4):
+                for k in range(2):
+                    even = xt[pl.ds(32 * a + 2 * k, 8, stride=4), :]
+                    odd = xt[pl.ds(32 * a + 2 * k + 1, 8, stride=4), :]
+                    pieces[across(a, IN0 + k), :] = right(even, odd)
 
     def pack_out(first, last):
         def body(t, carry):
@@ -211,8 +245,11 @@
                 pieces[at:at + 8, :] = cols[8 * j:8 * j + 8, :]
 
     def pack_bn():
-        for i in range(N_DEV):
-            pieces[i * ROWS + BN:i * ROWS + ROWS, :] = jnp.zeros((8, LANES), F32)
+        def clear(i, carry):
+            pieces[pl.ds(pl.multiple_of(i * ROWS + BN, 8), 8), :] = jnp.zeros((8, LANES), F32)
+            return carry
+
+        lax.fori_loop(0, N_DEV, clear, 0)
         for b in range(2):
             for k in range(4):
                 for half in range(2):
@@ -229,14 +266,13 @@
         for lo, hi, names in units:
             if at <= lo < end:
                 need(*names)
-        for lo, first, last in ((0, 0, 8), (72, 8, 16), (144, 16, 18)):
-            if at <= lo < end:
-                pack_mid(first, last)
-        if at <= 144 < end:
-            pack_in_first()
-        lo, hi = max(at, 168), min(end, 232)
+        for i in range(5):
+            if at <= 40 * i < end:
+                pack_mid(40 * i, 4 * i, min(4, N_MID - 4 * i))
+                pack_in_one(i)
+        lo, hi = max(at, 184), min(end, 232)
         if lo < hi:
-            pack_in((lo - 168) // 8, (hi - 168) // 8)
+            pack_in((lo - 184) // 8, (hi - 184) // 8)
         lo, hi = max(at, OUT), min(end, SHORT)
         if lo < hi:
             pack_out((lo - OUT) // 4, (hi - OUT) // 4)
@@ -251,12 +287,8 @@
 
     def own_pieces():
         need('own')
-        for ref, base, tiles, tensors in ((p_mid, MID, 9, N_MID), (p_in, IN, 4, N_IN), (p_out, OUT, 4, N_OUT)):
-            for m in range(tiles):
-                for t in range(0, tensors, 8):
-                    size = min(8, tensors - t)
-                    v_own[pl.ds(base + tiles * t + m, size, stride=tiles), :] = (
-                        ref[t:t + size, 128 * m:128 * m + 128])
+        for rows, tile, ref, tensors in momentum_rows(p_mid, p_in, p_out):
+            v_own[rows, :] = ref[tensors, tile]
         v_own[IN0:IN0 + 2, :] = p_in0[...]
         v_own[SHORT:SHORT + 8, :] = p_short[...]
         flat = [p_fc[pl.ds(128 * q, 128)].reshape(1, LANES) for q in range(6)]
@@ -281,7 +313,7 @@
         for t in range(N_MID):
             even = o_mid[t, pl.ds(mid_off, 9, stride=2), :]
             odds = o_mid[t, pl.ds(mid_off + 1, 9, stride=2), :]
-            w_own[MID + 9 * t:MID + 9 * t + 9, :] = jnp.concatenate([even, odds], axis=1)
+            w_own[mid_row(t):mid_row(t) + 9, :] = jnp.concatenate([even, odds], axis=1)
         for j in range(9):
             other = o_in[2 * j - 1] if j else o_in0[...]
             ot[...] = jnp.concatenate([other, o_in[2 * j]], axis=0).T
@@ -290,13 +322,15 @@
             even = ot[pl.ds(col_off, 4, stride=2), :]
             odds = ot[pl.ds(col_off + 1, 4, stride=2), :]
             if j:
-                w_own[IN + 8 * j - 4:IN + 8 * j, :] = left(even, odds)
-            w_own[IN + 8 * j:IN + 8 * j + 4, :] = right(even, odds)
-        for p in range(2):
-            for h in range(2):
-                for t in range(N_OUT):
-                    at = OUT + 4 * t + 2 * p + h
-                    w_own[at:at + 1, :] = o_out[h, t, pl.ds(out_off + p, 1), :]
+                w_own[in_row(2 * j - 1):in_row(2 * j - 1) + 4, :] = left(even, odds)
+            w_own[in_row(2 * j):in_row(2 * j) + 4, :] = right(even, odds)
+        def own_out(t, carry):
+            for p in range(2):
+                for h in range(2):
+                    w_own[pl.ds(OUT + 4 * t + 2 * p + h, 1), :] = o_out[h, t, pl.ds(out_off + p, 1), :]
+            return carry
+
+        lax.fori_loop(0, N_OUT, own_out, 0)
         for p in range(4):
             for h in range(2):
                 w_own[SHORT + 2 * p + h:SHORT + 2 * p + h + 1, :] = o_short[h, pl.ds(short_off + p, 1), :]
@@ -311,17 +345,29 @@
         bias = jnp.concatenate([o_bias[...].reshape(1, CLASSES), jnp.zeros((1, LANES - CLASSES), F32)], axis=1)
         w_own[BIAS:BIAS + 1, :] = jnp.where((lane_row >= 4 * rank) & (lane_row < 4 * rank + 4), bias, 0.0)
 
-    copies = {}
     outs = []
+    sent = {}
 
     def start(c, k, src, dst, peer):
-        copy = pltpu.make_async_remote_copy(src_ref=src, dst_ref=dst, send_sem=send.at[c * N_SEMS + k],
-                                            recv_sem=recv.at[c * N_SEMS + k], device_id=peer, device_id_type=MESH)
-        copy.start()
-        copies[c, k] = copy
-
-    def arrived(c, k):
-        copies[c, k].wait_recv()
+        pltpu.make_async_remote_copy(src_ref=src, dst_ref=dst, send_sem=send.at[c * N_SEMS + k],
+                                     recv_sem=recv.at[c * N_SEMS + k], device_id=peer, device_id_type=MESH).start()
+        sent[c, k] = sent.get((c, k), 0) + (1 if len(src.shape) == 2 else src.size // (src.shape[-1] * src.shape[-2]))
+
+    def wait(c, k, semaphores):
+        at, size, _ = CHUNKS[c]
+        rows = pl.ds(at, size)
+        count = sent[c, k]
+        if count == 8:
+            block = got_core.at[:, :, 0, rows, :]
+        elif count == 1:
+            block = got_core.at[0, 0, 0, rows, :]
+        else:
+            block = got_core.at[pl.ds(0, count), 0, 0, rows, :]
+        pltpu.make_async_copy(block, block, semaphores.at[c * N_SEMS + k]).wait()
+
+    def arrived(c, *numbers):
+        for k in numbers:
+            wait(c, k, recv)
 
     def keep(src, dst):
         copy = pltpu.make_async_copy(src, dst, out_sems.at[len(outs)])
@@ -334,57 +380,65 @@
         x_first = first == 'x'
         one_peer, two_peer = (x_peer, y_peer) if x_first else (y_peer, x_peer)
 
-        def half(zz, yx, mine):
-            return (zz, yx, x if mine else 1 - x) if x_first else (zz, y if mine else 1 - y, yx)
+        here = y if x_first else x
+
+        def block(ref, near, *rest):
+            first_at = (x if near else 1 - x) if x_first else (y if near else 1 - y)
+            return ref.at[(slice(None), slice(None), first_at) + rest] if x_first else (
+                ref.at[(slice(None), first_at, slice(None)) + rest])
+
+        def spot(second, near):
+            return (second, x if near else 1 - x) if x_first else (y if near else 1 - y, second)
+
+        def both_cores(zz, second, near):
+            a, b = spot(second, near)
+            return packed[zz, a, b, core, rows, :] + got_core[zz, a, b, rows, :]
+
+        def over_z(body):
+            def run(zz, carry):
+                body(zz)
+                return carry
+
+            lax.fori_loop(0, 4, run, 0)
 
         if stage == 0:
             pack(at, size)
-            if not copies:
+            if not sent:
                 pl.semaphore_wait(barrier, N_DEV - 1)
-            start(c, S_CORE, packed.at[:, :, :, 1 - core, rows, :], got_core.at[:, :, :, rows, :], core_peer)
+            for k, near in enumerate((False, True)):
+                start(c, S_CORE + k, block(packed, near, 1 - core, rows), block(got_core, near, rows), core_peer)
         elif stage == 1:
             arrived(c, S_CORE)
-
-            def add(mine):
-                def body(m, carry):
-                    zz, yx = m // 2, lax.rem(m, 2)
-                    a, b, d = half(zz, yx, mine)
-                    acc[a, b, d, rows, :] = packed[a, b, d, core, rows, :] + got_core[a, b, d, rows, :]
-                    return carry
-
-                lax.fori_loop(0, 8, body, 0)
-
-            add(False)
-            src = acc.at[:, :, 1 - x, rows, :] if x_first else acc.at[:, 1 - y, :, rows, :]
-            start(c, S_ONE, src, got_one.at[:, :, rows, :], one_peer)
-            add(True)
+            for k, second in enumerate((1 - here, here)):
+                a, b = spot(second, False)
+
+                def body(zz, a=a, b=b, second=second):
+                    acc[zz, a, b, rows, :] = both_cores(zz, second, False)
+
+                over_z(body)
+                start(c, S_ONE + k, acc.at[:, a, b, rows, :], got_one.at[:, second, rows, :], one_peer)
         elif stage == 2:
-            arrived(c, S_ONE)
-
-            def add(other):
-                def body(zz, carry):
-                    a, b, d = half(zz, other, True)
-                    acc[a, b, d, rows, :] = acc[a, b, d, rows, :] + got_one[zz, other, rows, :]
-                    return carry
-
-                lax.fori_loop(0, 4, body, 0)
-
-            here = y if x_first else x
-            add(1 - here)
-            src = acc.at[:, 1 - y, x, rows, :] if x_first else acc.at[:, y, 1 - x, rows, :]
-            start(c, S_TWO, src, got_two.at[:, rows, :], two_peer)
-            add(here)
-        elif stage == 3:
-            arrived(c, S_TWO)
+            arrived(c, S_CORE + 1, S_ONE)
+            a, b = spot(1 - here, True)
+
+            def body(zz):
+                acc[zz, a, b, rows, :] = both_cores(zz, 1 - here, True) + got_one[zz, 1 - here, rows, :]
+
+            over_z(body)
             for d in (1, 2, 3, 0):
                 zz = lax.rem(z + d, 4)
-                acc[zz, y, x, rows, :] = acc[zz, y, x, rows, :] + got_two[zz, rows, :]
-                if d:
-                    start(c, S_Z + d, acc.at[zz, y, x, rows, :], got_z.at[d - 1, rows, :], device(zz, y, x, core))
+                start(c, S_TWO + (d == 0), acc.at[zz, a, b, rows, :], got_two.at[zz, rows, :], two_peer)
+        elif stage == 3:
+            arrived(c, S_ONE + 1, S_TWO)
+            for d in (2, 3, 1):
+                zz = lax.rem(z + d, 4)
+                acc[zz, y, x, rows, :] = (
+                    both_cores(zz, here, True) + got_one[zz, here, rows, :] + got_two[zz, rows, :])
+                start(c, S_Z, acc.at[zz, y, x, rows, :], got_z.at[d - 1, rows, :], device(zz, y, x, core))
         elif stage == 4:
-            for d in (1, 2, 3):
-                arrived(c, S_Z + d)
-            mean = (acc[z, y, x, rows, :] + got_z[0, rows, :] + got_z[1, rows, :] + got_z[2, rows, :]) * (1.0 / N_DEV)
+            arrived(c, S_TWO + 1, S_Z)
+            mean = both_cores(z, here, True) + got_one[z, here, rows, :] + got_two[z, rows, :]
+            mean = (mean + got_z[0, rows, :] + got_z[1, rows, :] + got_z[2, rows, :]) * (1.0 / N_DEV)
             grad[rows, :] = mean
             own = w_own[rows, :]
             g_sum = jnp.sum(mean * mean, axis=1, keepdims=True)
@@ -392,7 +446,7 @@
             row = lax.broadcasted_iota(jnp.int32, (size, LANES), 0) + at
             lane = lax.broadcasted_iota(jnp.int32, (size, LANES), 1)
             tensor = jnp.where(lane < 64, lane, lane - 64)
-            member = (row >= first_row(tensor)) & (row < first_row(tensor + 1))
+            member = member_rows(row, tensor)
             part = jnp.where(member, jnp.where(lane < 64, g_sum, w_sum), 0.0)
             norms[c, rank] = jnp.sum(part, axis=0, keepdims=True)
 
@@ -413,7 +467,7 @@
             row = lax.broadcasted_iota(jnp.int32, (size, LANES), 0) + at
             lane = lax.broadcasted_iota(jnp.int32, (size, LANES), 1)
             trust = jnp.where(lane == ID_PLAIN, 1.0, trust)
-            member = (row >= first_row(lane)) & (row < first_row(lane + 1)) & (lane <= ID_PLAIN)
+            member = member_rows(row, lane) & (lane <= ID_PLAIN)
             rate = lr[0] * jnp.sum(jnp.where(member, trust, 0.0), axis=1, keepdims=True)
             decay = jnp.where(row < BN, DECAY, 0.0)
             own = w_own[rows, :]
@@ -422,32 +476,38 @@
             keep(v_new.at[rows, :], v_out_rows.at[rows, :])
             mine = (row != BIAS) | ((lane >= 4 * rank) & (lane < 4 * rank + 4))
             full[z, y, x, core, rows, :] = jnp.where(mine, own - moment, 0.0)
+            piece = full.at[z, y, x, core, rows, :]
+            for d in (2, 3, 1):
+                start(c, A_Z, piece, piece, device(lax.rem(z + d, 4), y, x, core))
+            start(c, A_TWO, piece, piece, two_peer)
+        elif stage == 6:
+            arrived(c, A_Z)
             for d in (1, 2, 3):
-                piece = full.at[z, y, x, core, rows, :]
-                start(c, A_Z + d, piece, piece, device(lax.rem(z + d, 4), y, x, core))
-        elif stage == 6:
-            for d in (1, 2, 3):
-                arrived(c, A_Z + d)
-            pieces = full.at[:, y, x, core, rows, :]
-            start(c, A_TWO, pieces, pieces, two_peer)
+                piece = full.at[lax.rem(z + d, 4), y, x, core, rows, :]
+                start(c, A_TWO + 1, piece, piece, two_peer)
+            line = full.at[:, y, x, core, rows, :]
+            start(c, A_ONE, line, line, one_peer)
         elif stage == 7:
-            arrived(c, A_TWO)
-            pieces = full.at[:, :, x, core, rows, :] if x_first else full.at[:, y, :, core, rows, :]
-            start(c, A_ONE, pieces, pieces, one_peer)
+            arrived(c, A_TWO, A_TWO + 1)
+            a, b = spot(1 - here, True)
+            line = full.at[:, a, b, core, rows, :]
+            start(c, A_ONE + 1, line, line, one_peer)
+            plane = block(full, True, core, rows)
+            start(c, A_CORE, plane, plane, core_peer)
         elif stage == 8:
-            arrived(c, A_ONE)
-            pieces = full.at[:, :, :, core, rows, :]
-            start(c, A_CORE, pieces, pieces, core_peer)
+            arrived(c, A_ONE, A_ONE + 1)
+            plane = block(full, False, core, rows)
+            start(c, A_CORE + 1, plane, plane, core_peer)
         else:
-            arrived(c, A_CORE)
+            arrived(c, A_CORE, A_CORE + 1)
             keep(full.at[:, :, :, :, rows, :], full_out.at[:, :, :, :, rows, :])
 
     for c, stage in STEPS:
-        if stage == 3 and not any(k[1] == S_Z + 1 for k in copies):
+        if stage == 3 and not any(k == S_Z for _, k in sent):
             own_pieces()
         step(c, stage)
-    for copy in copies.values():
-        copy.wait_send()
+    for c, k in sent:
+        wait(c, k, send)
     for c in range(len(CHUNKS)):
         others = norms.at[c, pl.ds(0, N_DEV - 1)]
         pltpu.make_async_copy(others, others, n_send.at[c]).wait()
@@ -477,7 +537,7 @@
         + [VMEM((4, 2, 2, 2) + rows, F32), VMEM(rows, F32), VMEM(rows, F32), VMEM(rows, F32),
            VMEM((4, 2, 2, 2) + rows, F32)]
         + [VMEM(s, F32) for s in exchanged]
-        + [dma((32,)), dma((2 * count,)), dma((count * N_SEMS,)), dma((count * N_SEMS,)), dma((count,)), dma((count,))],
+        + [dma((40,)), dma((2 * count,)), dma((count * N_SEMS,)), dma((count * N_SEMS,)), dma((count,)), dma((count,))],
         compiler_params=pltpu.CompilerParams(vmem_limit_bytes=VMEM_LIMIT, collective_id=0, has_side_effects=True),
     )(*operands)
     return full.reshape(N_DEV, ROWS, LANES), v_new
@@ -490,7 +550,7 @@
     lane_row = lax.broadcasted_iota(jnp.int32, (1, LANES), 1)
     pieces = packed.reshape(N_DEV, ROWS, LANES)
     fetches = []
-    for k, (at, size) in enumerate(((0, 40), (40, 104), (144, 24), (168, 64), (232, 72), (304, 24))):
+    for k, (at, size) in enumerate(((0, 40), (40, 120), (160, 24), (184, 48), (232, 72), (304, 24))):
         fetches.append(pltpu.make_async_copy(packed_rows.at[:, pl.ds(at, size), :], pieces.at[:, pl.ds(at, size), :],
                                              sems.at[12 + k]))
     fetches.append(pltpu.make_async_copy(v_rows, v_own, sems.at[18]))
@@ -503,7 +563,7 @@
     def mid_body(t, carry):
         for a in range(4):
             for k in range(9):
-                x = packed[across(a, MID + 9 * t + k), :]
+                x = packed[across(a, mid_row(t) + k), :]
                 s_mid[t, pl.ds(144 * a + 2 * k, 8, stride=18), :] = x[:, :64]
                 s_mid[t, pl.ds(144 * a + 2 * k + 1, 8, stride=18), :] = x[:, 64:]
         put(s_mid.at[t], n_mid.at[t], 0)
@@ -514,40 +574,45 @@
     fetches[0].wait()
     lax.fori_loop(0, 4, mid_body, 0)
     fetches[1].wait()
-    lax.fori_loop(4, 15, mid_body, 0)
+    lax.fori_loop(4, 16, mid_body, 0)
     fetches[2].wait()
-    lax.fori_loop(15, N_MID, mid_body, 0)
+    lax.fori_loop(16, N_MID, mid_body, 0)
     fetches[3].wait()
 
-    def in_rows(t, other):
+    def in_pair(first, second, row, other):
         for a in range(4):
             for k in range(4):
-                x = packed[across(a, IN + 4 * t + k), :]
-                y = packed[across(a, IN + 4 * other + k), :]
+                x = packed[across(a, row + k), :]
+                y = packed[across(a, other + k), :]
                 xt[pl.ds(64 * a + 2 * k, 8, stride=8), :] = left(x, y)
                 xt[pl.ds(64 * a + 2 * k + 1, 8, stride=8), :] = right(x, y)
-
-    def in_body(j, carry):
-        t = 2 * j + 1
-        in_rows(t, t + 1)
         for h in range(2):
             cols = xt[128 * h:128 * h + 128, :].T
-            for u in range(2):
-                s_in[t + u, :, 128 * h:128 * h + 128] = cols[64 * u:64 * u + 64]
-                t_in[t + u, :, 128 * h:128 * h + 128] = cols[64 * u:64 * u + 64].astype(bf)
-        for u in range(2):
-            put(s_in.at[t + u], n_in.at[t + u], 2)
-            put(t_in.at[t + u], b_in.at[t + u], 3)
+            for u, t in enumerate((first, second)):
+                s_in[t, :, 128 * h:128 * h + 128] = cols[64 * u:64 * u + 64]
+                t_in[t, :, 128 * h:128 * h + 128] = cols[64 * u:64 * u + 64].astype(bf)
+        for t in (first, second):
+            put(s_in.at[t], n_in.at[t], 2)
+            put(t_in.at[t], b_in.at[t], 3)
+
+    def in_body(j, carry):
+        in_pair(2 * j + 5, 2 * j + 6, 184 + 8 * j, 188 + 8 * j)
         return carry
 
-    lax.fori_loop(0, 8, in_body, 0)
-    in_rows(0, 0)
+    lax.fori_loop(0, 6, in_body, 0)
+    in_pair(0, 1, in_row(0), in_row(1))
+    in_pair(2, 3, in_row(2), in_row(3))
+    for a in range(4):
+        for k in range(4):
+            x = packed[across(a, in_row(4) + k), :]
+            xt[pl.ds(64 * a + 2 * k, 8, stride=8), :] = x
+            xt[pl.ds(64 * a + 2 * k + 1, 8, stride=8), :] = right(x, x)
     for h in range(2):
         cols = xt[128 * h:128 * h + 128, :].T
-        s_in[0, :, 128 * h:128 * h + 128] = cols[:64]
-        t_in[0, :, 128 * h:128 * h + 128] = cols[:64].astype(bf)
-    put(s_in.at[0], n_in.at[0], 2)
-    put(t_in.at[0], b_in.at[0], 3)
+        s_in[4, :, 128 * h:128 * h + 128] = cols[:64]
+        t_in[4, :, 128 * h:128 * h + 128] = cols[:64].astype(bf)
+    put(s_in.at[4], n_in.at[4], 2)
+    put(t_in.at[4], b_in.at[4], 3)
     for a in range(4):
         for k in range(2):
             x = packed[across(a, IN0 + k), :]
@@ -607,11 +672,8 @@
     n_bias[...] = jnp.sum(total, axis=0, keepdims=True)[0, :CLASSES]
     fetches[6].wait()
 
-    for ref, base, tiles, count in ((v_mid, MID, 9, N_MID), (v_in, IN, 4, N_IN), (v_out, OUT, 4, N_OUT)):
-        for m in range(tiles):
-            for t in range(0, count, 8):
-                size = min(8, count - t)
-                ref[t:t + size, 128 * m:128 * m + 128] = v_own[pl.ds(base + tiles * t + m, size, stride=tiles), :]
+    for rows, tile, ref, tensors in momentum_rows(v_mid, v_in, v_out):
+        ref[tensors, tile] = v_own[rows, :]
     rank = lax.axis_index('dp')
     v_in0[...] = v_own[IN0:IN0 + 2, :]
     v_short[...] = v_own[SHORT:SHORT + 8, :]

time: 89.3 us -> 83.5 us (0.935)
  Pallas kernels: 87.8 us -> 82 us
    pallas_call x1, Pallas kernels: 80.5 us -> 74.7 us  [exchange(): pl.pallas_call(exchange_kernel, out_shape=(jax.ShapeDtypeStruct((4, 2, 2,...]
where the time goes in v4:
time: 83.5 us; the launch traced here: 83.3 us
  Pallas kernels  82 us (98%)
  between operations  1.32 us (2%)
    pallas_call x1, Pallas kernels, exchange(): pl.pallas_call(exchange_kernel, out_shape=(jax.ShapeDtypeStruct((4, 2, 2,...  74.7 us
    pallas_call x1, Pallas kernels, unpack_weights(): pl.pallas_call(unpack_kernel, out_shape=[jax.ShapeDtypeStruct(s, d) for s...  7.3 us

profile of v4, /device:TPU:0, one launch (start us, length us, event | category | flops | bytes accessed | tf_op | source)
XLA Modules:
  0.0 83.3 jit_solution(1453859779624454105)
XLA Ops:
  1.3 74.7 %shard_map.408 = (f32[4,2,2,2,328,128]{5,4,3,2,1,0:T(8,128)}, f32[328,128]{1,0:T(8,128)}) custom-call(f32[1]{0:T(128)} %bitcast.31.lr, f32[18,576,64]{2,1,0:T(8,128)} %bitcast.33, f32[17,64,256]{2,1,0:T(8,128)} %bitcast.36, f32[64,128]{1,0:T(8,128)} %bitcast.43, f32[18,64,256]{2,1,0:T(8,128)} %bitcast.35, f32[128,256]{1,0:T(8,128)} %bitcast.39, ...), custom_call_target="tpu_custom_call" | custom-call | tf_op jit(solution)/shard_map/pallas_call | solution.py:529
  76.0 7.3 %shard_map.409 = (f32[18,576,64]{2,1,0:T(8,128)}, f32[17,64,256]{2,1,0:T(8,128)}, f32[64,128]{1,0:T(8,128)}, f32[18,64,256]{2,1,0:T(8,128)}, f32[128,256]{1,0:T(...) custom-call(f32[32,328,128]{2,1,0:T(8,128)} %bitcast.32, ...), custom_call_target="tpu_custom_call" | custom-call | tf_op jit(solution)/shard_map/pallas_call | solution.py:718

commit v5 on v4

--- a/solution.py
+++ b/solution.py
@@ -18,19 +18,18 @@
 VMEM = pltpu.VMEM
 MESH = pl.DeviceIdType.MESH
 CHUNKS = (
-    (0, 40, 'x'), (40, 40, 'y'), (80, 40, 'y'), (120, 40, 'x'), (160, 24, 'x'),
-    (184, 24, 'y'), (208, 24, 'x'), (232, 24, 'y'), (256, 24, 'y'), (280, 24, 'x'),
-    (304, 24, 'y'),
+    (0, 40, 'x'), (40, 40, 'y'), (80, 40, 'x'), (120, 40, 'y'), (160, 24, 'y'),
+    (184, 24, 'y'), (208, 24, 'y'), (232, 32, 'y'), (264, 40, 'x'), (304, 24, 'x'),
 )
 STEPS = (
-    (10, 0), (9, 0), (8, 0), (10, 1), (9, 1), (4, 0), (6, 0), (8, 1), (4, 1), (7, 0), (2, 0), (10, 2), (9, 2), (7, 1),
-    (6, 1), (5, 0), (8, 2), (3, 0), (4, 2), (2, 1), (9, 3), (7, 2), (3, 1), (10, 3), (0, 0), (8, 3), (6, 2), (1, 0),
-    (4, 3), (2, 2), (5, 1), (7, 3), (9, 4), (10, 4), (3, 2), (6, 3), (8, 4), (5, 2), (1, 1), (2, 3), (4, 4), (0, 1),
-    (7, 4), (3, 3), (5, 3), (6, 4), (9, 5), (1, 2), (0, 2), (10, 5), (2, 4), (8, 5), (3, 4), (1, 3), (5, 4), (9, 6),
-    (0, 3), (10, 6), (7, 5), (4, 5), (8, 6), (6, 5), (10, 7), (1, 4), (3, 5), (8, 7), (9, 7), (0, 4), (7, 6), (10, 8),
-    (5, 5), (2, 5), (4, 6), (6, 6), (7, 7), (3, 6), (1, 5), (5, 6), (0, 5), (4, 7), (8, 8), (2, 6), (10, 9), (6, 7),
-    (5, 7), (1, 6), (3, 7), (0, 6), (7, 8), (2, 7), (4, 8), (9, 8), (7, 9), (1, 7), (5, 8), (8, 9), (0, 7), (6, 8),
-    (6, 9), (2, 8), (3, 8), (1, 8), (0, 8), (3, 9), (2, 9), (1, 9), (5, 9), (9, 9), (4, 9), (0, 9),
+    (3, 0), (8, 0), (6, 0), (3, 1), (8, 1), (0, 0), (6, 1), (5, 0), (4, 0), (3, 2), (7, 0), (4, 1), (2, 0), (8, 2),
+    (0, 1), (1, 0), (6, 2), (3, 3), (4, 2), (0, 2), (1, 1), (8, 3), (2, 1), (9, 0), (6, 3), (4, 3), (3, 4), (0, 3),
+    (1, 2), (2, 2), (8, 4), (7, 1), (9, 1), (3, 5), (1, 3), (6, 4), (2, 3), (4, 4), (5, 1), (7, 2), (8, 5), (9, 2),
+    (3, 6), (4, 5), (7, 3), (0, 4), (6, 5), (1, 4), (5, 2), (9, 3), (2, 4), (8, 6), (3, 7), (0, 5), (5, 3), (4, 6),
+    (1, 5), (7, 4), (6, 6), (9, 4), (3, 8), (2, 5), (8, 7), (0, 6), (5, 4), (7, 5), (4, 7), (1, 6), (6, 7), (9, 5),
+    (2, 6), (8, 8), (4, 8), (5, 5), (0, 7), (6, 8), (7, 6), (1, 7), (9, 6), (0, 8), (2, 7), (5, 6), (1, 8), (7, 7),
+    (9, 7), (5, 7), (2, 8), (4, 9), (6, 9), (7, 8), (4, 10), (9, 8), (8, 9), (0, 9), (5, 8), (2, 9), (3, 9), (1, 9),
+    (7, 9), (8, 10), (9, 9), (5, 9), (1, 10), (7, 10), (0, 10), (6, 10), (9, 10), (3, 10), (2, 10), (5, 10),
 )
 S_CORE, S_ONE, S_TWO, S_Z, A_Z, A_TWO, A_ONE, A_CORE, N_SEMS = 0, 2, 4, 6, 7, 8, 10, 12, 14
 VMEM_LIMIT = 60 * 2**20
@@ -86,7 +85,7 @@
                     o_mid, o_in, o_in0, o_out, o_short, o_fc, o_bn, o_bias, ot,
                     p_mid, p_in, p_in0, p_out, p_short, p_fc, p_bn, p_bias,
                     packed, w_own, v_own, v_new, full,
-                    got_core, acc, got_one, got_two, got_z, grad, norms,
+                    got_core, acc, got_one, got_two, got_z, grad, layer_norms, norms,
                     sems, out_sems, send, recv, n_send, n_recv):
     rank = lax.axis_index('dp')
     core = lax.rem(rank, 2)
@@ -103,11 +102,16 @@
 
     barrier = pltpu.get_barrier_semaphore()
 
-    def greet(d, carry):
-        pl.semaphore_signal(barrier, inc=1, device_id=(lax.rem(rank + d, N_DEV),), device_id_type=MESH)
-        return carry
-
-    lax.fori_loop(1, N_DEV, greet, 0)
+    def layer(d):
+        return (z * 8 + lax.rem(rank + d, 8),)
+
+    def line(d):
+        return (lax.rem(rank + 8 * d, N_DEV),)
+
+    for d in range(1, 8):
+        pl.semaphore_signal(barrier, inc=1, device_id=layer(d), device_id_type=MESH)
+    for d in range(1, 4):
+        pl.semaphore_signal(barrier, inc=1, device_id=line(d), device_id_type=MESH)
 
     waiting = {}
     count = [0]
@@ -374,6 +378,14 @@
         copy.start()
         outs.append(copy)
 
+    def tell(k, row, peer):
+        pltpu.make_async_remote_copy(src_ref=row, dst_ref=row, send_sem=n_send.at[k], recv_sem=n_recv.at[k],
+                                     device_id=peer, device_id_type=MESH).start()
+
+    def told(k, semaphores):
+        rows = layer_norms.at[k // 2, pl.ds(0, 3 if k % 2 else 7)]
+        pltpu.make_async_copy(rows, rows, semaphores.at[k]).wait()
+
     def step(c, stage):
         at, size, first = CHUNKS[c]
         rows = pl.ds(at, size)
@@ -404,7 +416,7 @@
         if stage == 0:
             pack(at, size)
             if not sent:
-                pl.semaphore_wait(barrier, N_DEV - 1)
+                pl.semaphore_wait(barrier, 10)
             for k, near in enumerate((False, True)):
                 start(c, S_CORE + k, block(packed, near, 1 - core, rows), block(got_core, near, rows), core_peer)
         elif stage == 1:
@@ -434,7 +446,7 @@
                 zz = lax.rem(z + d, 4)
                 acc[zz, y, x, rows, :] = (
                     both_cores(zz, here, True) + got_one[zz, here, rows, :] + got_two[zz, rows, :])
-                start(c, S_Z, acc.at[zz, y, x, rows, :], got_z.at[d - 1, rows, :], device(zz, y, x, core))
+                start(c, S_Z, acc.at[zz, y, x, rows, :], got_z.at[d - 1, rows, :], line(d))
         elif stage == 4:
             arrived(c, S_TWO + 1, S_Z)
             mean = both_cores(z, here, True) + got_one[z, here, rows, :] + got_two[z, rows, :]
@@ -448,18 +460,18 @@
             tensor = jnp.where(lane < 64, lane, lane - 64)
             member = member_rows(row, tensor)
             part = jnp.where(member, jnp.where(lane < 64, g_sum, w_sum), 0.0)
-            norms[c, rank] = jnp.sum(part, axis=0, keepdims=True)
-
-            def tell(d, carry):
-                pltpu.make_async_remote_copy(
-                    src_ref=norms.at[c, rank], dst_ref=norms.at[c, rank], send_sem=n_send.at[c],
-                    recv_sem=n_recv.at[c], device_id=(lax.rem(rank + d, N_DEV),), device_id_type=MESH).start()
-                return carry
-
-            lax.fori_loop(1, N_DEV, tell, 0)
+            here8 = lax.rem(rank, 8)
+            layer_norms[c, here8] = jnp.sum(part, axis=0, keepdims=True)
+            row8 = layer_norms.at[c, here8]
+            for d in range(1, 8):
+                tell(2 * c, row8, layer(d))
         elif stage == 5:
-            others = norms.at[c, pl.ds(0, N_DEV - 1)]
-            pltpu.make_async_copy(others, others, n_recv.at[c]).wait()
+            told(2 * c, n_recv)
+            norms[c, z] = jnp.sum(layer_norms[c], axis=0)
+            for d in range(1, 4):
+                tell(2 * c + 1, norms.at[c, z], line(d))
+        elif stage == 6:
+            told(2 * c + 1, n_recv)
             total = jnp.sum(norms[c], axis=0)
             g_norm = jnp.sqrt(total)
             w_norm = pltpu.roll(g_norm, 64, 1)
@@ -478,23 +490,23 @@
             full[z, y, x, core, rows, :] = jnp.where(mine, own - moment, 0.0)
             piece = full.at[z, y, x, core, rows, :]
             for d in (2, 3, 1):
-                start(c, A_Z, piece, piece, device(lax.rem(z + d, 4), y, x, core))
+                start(c, A_Z, piece, piece, line(d))
             start(c, A_TWO, piece, piece, two_peer)
-        elif stage == 6:
+        elif stage == 7:
             arrived(c, A_Z)
             for d in (1, 2, 3):
                 piece = full.at[lax.rem(z + d, 4), y, x, core, rows, :]
                 start(c, A_TWO + 1, piece, piece, two_peer)
-            line = full.at[:, y, x, core, rows, :]
-            start(c, A_ONE, line, line, one_peer)
-        elif stage == 7:
+            column = full.at[:, y, x, core, rows, :]
+            start(c, A_ONE, column, column, one_peer)
+        elif stage == 8:
             arrived(c, A_TWO, A_TWO + 1)
             a, b = spot(1 - here, True)
-            line = full.at[:, a, b, core, rows, :]
-            start(c, A_ONE + 1, line, line, one_peer)
+            column = full.at[:, a, b, core, rows, :]
+            start(c, A_ONE + 1, column, column, one_peer)
             plane = block(full, True, core, rows)
             start(c, A_CORE, plane, plane, core_peer)
-        elif stage == 8:
+        elif stage == 9:
             arrived(c, A_ONE, A_ONE + 1)
             plane = block(full, False, core, rows)
             start(c, A_CORE + 1, plane, plane, core_peer)
@@ -508,9 +520,8 @@
         step(c, stage)
     for c, k in sent:
         wait(c, k, send)
-    for c in range(len(CHUNKS)):
-        others = norms.at[c, pl.ds(0, N_DEV - 1)]
-        pltpu.make_async_copy(others, others, n_send.at[c]).wait()
+    for k in range(2 * len(CHUNKS)):
+        told(k, n_send)
     for copy in outs:
         copy.wait()
 
@@ -524,7 +535,7 @@
            (CLASSES,), (128, 128), (N_MID, 1152), (N_IN, 512), (2, LANES), (N_OUT, 512), (8, LANES), (800,), (448,), (4,)]
     rows = (ROWS, LANES)
     exchanged = [(4, 2, 2) + rows, (4, 2, 2) + rows, (4, 2) + rows, (4,) + rows, (3,) + rows, rows,
-                 (count, N_DEV, 1, LANES)]
+                 (count, 8, 1, LANES), (count, 4, 1, LANES)]
     dma = pltpu.SemaphoreType.DMA
     full, v_new = pl.pallas_call(
         exchange_kernel,
@@ -537,7 +548,7 @@
         + [VMEM((4, 2, 2, 2) + rows, F32), VMEM(rows, F32), VMEM(rows, F32), VMEM(rows, F32),
            VMEM((4, 2, 2, 2) + rows, F32)]
         + [VMEM(s, F32) for s in exchanged]
-        + [dma((40,)), dma((2 * count,)), dma((count * N_SEMS,)), dma((count * N_SEMS,)), dma((count,)), dma((count,))],
+        + [dma((40,)), dma((2 * count,)), dma((count * N_SEMS,)), dma((count * N_SEMS,)), dma((2 * count,)), dma((2 * count,))],
         compiler_params=pltpu.CompilerParams(vmem_limit_bytes=VMEM_LIMIT, collective_id=0, has_side_effects=True),
     )(*operands)
     return full.reshape(N_DEV, ROWS, LANES), v_new

time: 83.5 us -> 75.6 us (0.905)
  Pallas kernels: 82 us -> 74 us
    pallas_call x1, Pallas kernels: 74.7 us -> 66.7 us  [exchange(): pl.pallas_call(exchange_kernel, out_shape=(jax.ShapeDtypeStruct((4, 2, 2,...]
where the time goes in v5:
time: 75.6 us; the launch traced here: 75.3 us
  Pallas kernels  74 us (98%)
  between operations  1.32 us (2%)
    pallas_call x1, Pallas kernels, exchange(): pl.pallas_call(exchange_kernel, out_shape=(jax.ShapeDtypeStruct((4, 2, 2,...  66.7 us
    pallas_call x1, Pallas kernels, unpack_weights(): pl.pallas_call(unpack_kernel, out_shape=[jax.ShapeDtypeStruct(s, d) for s...  7.3 us

profile of v5, /device:TPU:0, one launch (start us, length us, event | category | flops | bytes accessed | tf_op | source)
XLA Modules:
  0.0 75.3 jit_solution(14145115729423796487)
XLA Ops:
  1.3 66.7 %shard_map.408 = (f32[4,2,2,2,328,128]{5,4,3,2,1,0:T(8,128)}, f32[328,128]{1,0:T(8,128)}) custom-call(f32[1]{0:T(128)} %bitcast.31.lr, f32[18,576,64]{2,1,0:T(8,128)} %bitcast.33, f32[17,64,256]{2,1,0:T(8,128)} %bitcast.36, f32[64,128]{1,0:T(8,128)} %bitcast.43, f32[18,64,256]{2,1,0:T(8,128)} %bitcast.35, f32[128,256]{1,0:T(8,128)} %bitcast.39, ...), custom_call_target="tpu_custom_call" | custom-call | tf_op jit(solution)/shard_map/pallas_call | solution.py:540
  68.0 7.3 %shard_map.409 = (f32[18,576,64]{2,1,0:T(8,128)}, f32[17,64,256]{2,1,0:T(8,128)}, f32[64,128]{1,0:T(8,128)}, f32[18,64,256]{2,1,0:T(8,128)}, f32[128,256]{1,0:T(...) custom-call(f32[32,328,128]{2,1,0:T(8,128)} %bitcast.32, ...), custom_call_target="tpu_custom_call" | custom-call | tf_op jit(solution)/shard_map/pallas_call | solution.py:729

commit v6 on v5

--- a/solution.py
+++ b/solution.py
@@ -19,18 +19,21 @@
 MESH = pl.DeviceIdType.MESH
 CHUNKS = (
     (0, 40, 'x'), (40, 40, 'y'), (80, 40, 'x'), (120, 40, 'y'), (160, 24, 'y'),
-    (184, 24, 'y'), (208, 24, 'y'), (232, 32, 'y'), (264, 40, 'x'), (304, 24, 'x'),
+    (184, 24, 'x'), (208, 24, 'zx'), (232, 24, 'y'), (256, 24, 'x'), (280, 24, 'zx'),
+    (304, 24, 'y'),
 )
 STEPS = (
-    (3, 0), (8, 0), (6, 0), (3, 1), (8, 1), (0, 0), (6, 1), (5, 0), (4, 0), (3, 2), (7, 0), (4, 1), (2, 0), (8, 2),
-    (0, 1), (1, 0), (6, 2), (3, 3), (4, 2), (0, 2), (1, 1), (8, 3), (2, 1), (9, 0), (6, 3), (4, 3), (3, 4), (0, 3),
-    (1, 2), (2, 2), (8, 4), (7, 1), (9, 1), (3, 5), (1, 3), (6, 4), (2, 3), (4, 4), (5, 1), (7, 2), (8, 5), (9, 2),
-    (3, 6), (4, 5), (7, 3), (0, 4), (6, 5), (1, 4), (5, 2), (9, 3), (2, 4), (8, 6), (3, 7), (0, 5), (5, 3), (4, 6),
-    (1, 5), (7, 4), (6, 6), (9, 4), (3, 8), (2, 5), (8, 7), (0, 6), (5, 4), (7, 5), (4, 7), (1, 6), (6, 7), (9, 5),
-    (2, 6), (8, 8), (4, 8), (5, 5), (0, 7), (6, 8), (7, 6), (1, 7), (9, 6), (0, 8), (2, 7), (5, 6), (1, 8), (7, 7),
-    (9, 7), (5, 7), (2, 8), (4, 9), (6, 9), (7, 8), (4, 10), (9, 8), (8, 9), (0, 9), (5, 8), (2, 9), (3, 9), (1, 9),
-    (7, 9), (8, 10), (9, 9), (5, 9), (1, 10), (7, 10), (0, 10), (6, 10), (9, 10), (3, 10), (2, 10), (5, 10),
+    (1, 0), (8, 0), (9, 0), (7, 0), (1, 1), (8, 1), (2, 0), (9, 1), (6, 0), (2, 1), (4, 0), (8, 2), (1, 2), (6, 1),
+    (7, 1), (3, 0), (0, 0), (2, 2), (0, 1), (3, 1), (8, 3), (7, 2), (1, 3), (10, 0), (2, 3), (0, 2), (9, 2), (5, 0),
+    (3, 2), (4, 1), (7, 3), (8, 4), (10, 1), (5, 1), (0, 3), (1, 4), (9, 3), (3, 3), (4, 2), (2, 4), (5, 2), (6, 2),
+    (7, 4), (8, 5), (10, 2), (4, 3), (9, 4), (6, 3), (1, 5), (5, 3), (0, 4), (2, 5), (10, 3), (3, 4), (8, 6), (7, 5),
+    (6, 4), (9, 5), (1, 6), (4, 4), (0, 5), (5, 4), (3, 5), (2, 6), (10, 4), (7, 6), (9, 6), (6, 5), (8, 7), (5, 5),
+    (4, 5), (1, 7), (0, 6), (9, 7), (10, 5), (3, 6), (2, 7), (7, 7), (4, 6), (6, 6), (1, 8), (8, 8), (5, 6), (2, 8),
+    (10, 6), (9, 8), (7, 8), (6, 7), (3, 7), (0, 7), (4, 7), (2, 9), (10, 7), (6, 8), (5, 7), (3, 8), (0, 8), (8, 9),
+    (4, 8), (7, 9), (9, 9), (2, 10), (5, 8), (1, 9), (10, 8), (1, 10), (3, 9), (0, 9), (3, 10), (4, 9), (9, 10),
+    (5, 9), (6, 9), (7, 10), (8, 10), (10, 9), (5, 10), (6, 10), (0, 10), (4, 10), (10, 10),
 )
+FIRST_NORMS = [step for step in STEPS if step[1] == 4][0]
 S_CORE, S_ONE, S_TWO, S_Z, A_Z, A_TWO, A_ONE, A_CORE, N_SEMS = 0, 2, 4, 6, 7, 8, 10, 12, 14
 VMEM_LIMIT = 60 * 2**20
 
@@ -85,7 +88,7 @@
                     o_mid, o_in, o_in0, o_out, o_short, o_fc, o_bn, o_bias, ot,
                     p_mid, p_in, p_in0, p_out, p_short, p_fc, p_bn, p_bias,
                     packed, w_own, v_own, v_new, full,
-                    got_core, acc, got_one, got_two, got_z, grad, layer_norms, norms,
+                    got_core, acc, got_one, got_two, got_z, got_line, grad, layer_norms, norms,
                     sems, out_sems, send, recv, n_send, n_recv):
     rank = lax.axis_index('dp')
     core = lax.rem(rank, 2)
@@ -361,12 +364,8 @@
         at, size, _ = CHUNKS[c]
         rows = pl.ds(at, size)
         count = sent[c, k]
-        if count == 8:
-            block = got_core.at[:, :, 0, rows, :]
-        elif count == 1:
-            block = got_core.at[0, 0, 0, rows, :]
-        else:
-            block = got_core.at[pl.ds(0, count), 0, 0, rows, :]
+        lead = {1: (0, 0, 0), 2: (0, 0), 3: (pl.ds(0, 3), 0, 0), 4: (0,), 8: (pl.ds(0, 2),), 12: (pl.ds(0, 3),), 16: ()}[count]
+        block = got_core.at[lead + (slice(None),) * (3 - len(lead)) + (rows,)]
         pltpu.make_async_copy(block, block, semaphores.at[c * N_SEMS + k]).wait()
 
     def arrived(c, *numbers):
@@ -389,7 +388,7 @@
     def step(c, stage):
         at, size, first = CHUNKS[c]
         rows = pl.ds(at, size)
-        x_first = first == 'x'
+        x_first, z_first = first[-1] == 'x', first[0] == 'z'
         one_peer, two_peer = (x_peer, y_peer) if x_first else (y_peer, x_peer)
 
         here = y if x_first else x
@@ -419,6 +418,13 @@
                 pl.semaphore_wait(barrier, 10)
             for k, near in enumerate((False, True)):
                 start(c, S_CORE + k, block(packed, near, 1 - core, rows), block(got_core, near, rows), core_peer)
+        elif stage == 1 and z_first:
+            arrived(c, S_CORE, S_CORE + 1)
+            for d in (2, 3, 1, 0):
+                zz = lax.rem(z + d, 4)
+                acc[zz, :, :, rows, :] = packed[zz, :, :, core, rows, :] + got_core[zz, :, :, rows, :]
+                if d:
+                    start(c, S_Z, acc.at[zz, :, :, rows, :], got_line.at[d - 1, :, :, rows, :], line(d))
         elif stage == 1:
             arrived(c, S_CORE)
             for k, second in enumerate((1 - here, here)):
@@ -429,6 +435,16 @@
 
                 over_z(body)
                 start(c, S_ONE + k, acc.at[:, a, b, rows, :], got_one.at[:, second, rows, :], one_peer)
+        elif stage == 2 and z_first:
+            arrived(c, S_Z)
+            for near in (False, True):
+                for second in range(2):
+                    a, b = spot(second, near)
+                    total = acc[z, a, b, rows, :] + got_line[0, a, b, rows, :]
+                    acc[z, a, b, rows, :] = total + got_line[1, a, b, rows, :] + got_line[2, a, b, rows, :]
+                if not near:
+                    far = acc.at[z, :, 1 - x, rows, :] if x_first else acc.at[z, 1 - y, :, rows, :]
+                    start(c, S_ONE, far, got_one.at[0, :, rows, :], one_peer)
         elif stage == 2:
             arrived(c, S_CORE + 1, S_ONE)
             a, b = spot(1 - here, True)
@@ -440,6 +456,11 @@
             for d in (1, 2, 3, 0):
                 zz = lax.rem(z + d, 4)
                 start(c, S_TWO + (d == 0), acc.at[zz, a, b, rows, :], got_two.at[zz, rows, :], two_peer)
+        elif stage == 3 and z_first:
+            arrived(c, S_ONE)
+            a, b = spot(1 - here, True)
+            acc[z, a, b, rows, :] = acc[z, a, b, rows, :] + got_one[0, 1 - here, rows, :]
+            start(c, S_TWO, acc.at[z, a, b, rows, :], got_two.at[0, rows, :], two_peer)
         elif stage == 3:
             arrived(c, S_ONE + 1, S_TWO)
             for d in (2, 3, 1):
@@ -448,9 +469,14 @@
                     both_cores(zz, here, True) + got_one[zz, here, rows, :] + got_two[zz, rows, :])
                 start(c, S_Z, acc.at[zz, y, x, rows, :], got_z.at[d - 1, rows, :], line(d))
         elif stage == 4:
-            arrived(c, S_TWO + 1, S_Z)
-            mean = both_cores(z, here, True) + got_one[z, here, rows, :] + got_two[z, rows, :]
-            mean = (mean + got_z[0, rows, :] + got_z[1, rows, :] + got_z[2, rows, :]) * (1.0 / N_DEV)
+            if z_first:
+                arrived(c, S_TWO)
+                mean = acc[z, y, x, rows, :] + got_one[0, here, rows, :] + got_two[0, rows, :]
+            else:
+                arrived(c, S_TWO + 1, S_Z)
+                mean = both_cores(z, here, True) + got_one[z, here, rows, :] + got_two[z, rows, :]
+                mean = mean + got_z[0, rows, :] + got_z[1, rows, :] + got_z[2, rows, :]
+            mean = mean * (1.0 / N_DEV)
             grad[rows, :] = mean
             own = w_own[rows, :]
             g_sum = jnp.sum(mean * mean, axis=1, keepdims=True)
@@ -489,9 +515,26 @@
             mine = (row != BIAS) | ((lane >= 4 * rank) & (lane < 4 * rank + 4))
             full[z, y, x, core, rows, :] = jnp.where(mine, own - moment, 0.0)
             piece = full.at[z, y, x, core, rows, :]
+            if not z_first:
+                for d in (2, 3, 1):
+                    start(c, A_Z, piece, piece, line(d))
+            start(c, A_TWO, piece, piece, two_peer)
+        elif stage == 7 and z_first:
+            arrived(c, A_TWO)
+            pair = full.at[z, :, x, core, rows, :] if x_first else full.at[z, y, :, core, rows, :]
+            start(c, A_ONE, pair, pair, one_peer)
+        elif stage == 8 and z_first:
+            arrived(c, A_ONE)
+            plane = full.at[z, :, :, core, rows, :]
             for d in (2, 3, 1):
-                start(c, A_Z, piece, piece, line(d))
-            start(c, A_TWO, piece, piece, two_peer)
+                start(c, A_Z, plane, plane, line(d))
+        elif stage == 9 and z_first:
+            arrived(c, A_Z)
+            everything = full.at[:, :, :, core, rows, :]
+            start(c, A_CORE, everything, everything, core_peer)
+        elif stage == 10 and z_first:
+            arrived(c, A_CORE)
+            keep(full.at[:, :, :, :, rows, :], full_out.at[:, :, :, :, rows, :])
         elif stage == 7:
             arrived(c, A_Z)
             for d in (1, 2, 3):
@@ -515,7 +558,7 @@
             keep(full.at[:, :, :, :, rows, :], full_out.at[:, :, :, :, rows, :])
 
     for c, stage in STEPS:
-        if stage == 3 and not any(k == S_Z for _, k in sent):
+        if stage == 4 and (c, stage) == FIRST_NORMS:
             own_pieces()
         step(c, stage)
     for c, k in sent:
@@ -534,7 +577,7 @@
     own = [(N_MID, 24, 64), (N_IN, 64, 128), (64, 128), (2, N_OUT, 8, 128), (2, 8, 128), (CLASSES, 128), (112, 128),
            (CLASSES,), (128, 128), (N_MID, 1152), (N_IN, 512), (2, LANES), (N_OUT, 512), (8, LANES), (800,), (448,), (4,)]
     rows = (ROWS, LANES)
-    exchanged = [(4, 2, 2) + rows, (4, 2, 2) + rows, (4, 2) + rows, (4,) + rows, (3,) + rows, rows,
+    exchanged = [(4, 2, 2) + rows, (4, 2, 2) + rows, (4, 2) + rows, (4,) + rows, (3,) + rows, (3, 2, 2) + rows, rows,
                  (count, 8, 1, LANES), (count, 4, 1, LANES)]
     dma = pltpu.SemaphoreType.DMA
     full, v_new = pl.pallas_call(
@@ -554,9 +597,12 @@
     return full.reshape(N_DEV, ROWS, LANES), v_new
 
 
-def unpack_kernel(packed_rows, v_rows, n_mid, n_in, n_in0, n_out, n_short, n_fc, n_bn, n_bias,
-                  b_mid, b_in, b_in0, b_out, b_short, b_fc, v_mid, v_in, v_in0, v_out, v_short, v_fc, v_bn, v_bias,
-                  packed, v_own, s_mid, s_in, s_out, s_short, s_in0, s_fc, t_mid, t_in, t_out, t_short, t_in0, t_fc, xt, sems):
+def unpack_kernel(packed_rows, v_rows, n_mid, n_in, n_in0, n_out, n_short, n_fc, bn_out, bias_out,
+                  b_mid, b_in, b_in0, b_out, b_short, b_fc, *rest):
+    v_outs, rest = rest[:8], rest[8:]
+    n_bn, n_bias = rest[:2]
+    (v_mid, v_in, v_in0, v_out, v_short, v_fc, v_bn, v_bias), rest = rest[2:10], rest[10:]
+    (packed, v_own, s_mid, s_in, s_out, s_short, s_in0, s_fc, t_mid, t_in, t_out, t_short, t_in0, t_fc, xt, sems) = rest
     bf = jnp.bfloat16
     lane_row = lax.broadcasted_iota(jnp.int32, (1, LANES), 1)
     pieces = packed.reshape(N_DEV, ROWS, LANES)
@@ -584,6 +630,33 @@
 
     fetches[0].wait()
     lax.fori_loop(0, 4, mid_body, 0)
+    fetches[6].wait()
+    for rows, tile, ref, tensors in momentum_rows(v_mid, v_in, v_out):
+        ref[tensors, tile] = v_own[rows, :]
+    rank = lax.axis_index('dp')
+    v_in0[...] = v_own[IN0:IN0 + 2, :]
+    v_short[...] = v_own[SHORT:SHORT + 8, :]
+    for q in range(7):
+        flat = jnp.zeros((1, LANES), F32)
+        for r in range(8):
+            d = CLASSES * r - LANES * q
+            if -CLASSES < d < LANES:
+                row = pltpu.roll(v_own[FC + r:FC + r + 1, :], d % LANES, 1)
+                flat = jnp.where((lane_row >= d) & (lane_row < d + CLASSES), row, flat)
+        size = min(LANES, 800 - LANES * q)
+        v_fc[pl.ds(LANES * q, size)] = flat[0, :size]
+    odd = lax.rem(rank, 2) == 1
+    for k in range(4):
+        here = v_own[BN + k:BN + k + 1, :]
+        after = v_own[BN + k + 1:BN + k + 2, :]
+        turned = jnp.where(lane_row < 64, pltpu.roll(here, 64, 1), pltpu.roll(after, 64, 1))
+        size = min(LANES, 448 - LANES * k)
+        v_bn[pl.ds(LANES * k, size)] = jnp.where(odd, turned, here)[0, :size]
+    v_bias[...] = pltpu.roll(v_own[BIAS:BIAS + 1, :], lax.rem(N_DEV - rank, N_DEV) * 4, 1)[0, :4]
+    momenta = (v_mid, v_in, v_in0, v_out, v_short, v_fc, v_bn, v_bias)
+    moved = [pltpu.make_async_copy(src, dst, sems.at[19 + k]) for k, (src, dst) in enumerate(zip(momenta, v_outs))]
+    for copy in moved:
+        copy.start()
     fetches[1].wait()
     lax.fori_loop(4, 16, mid_body, 0)
     fetches[2].wait()
@@ -681,31 +754,11 @@
     for a in range(1, 4):
         total = total + packed[across(a, BIAS), :]
     n_bias[...] = jnp.sum(total, axis=0, keepdims=True)[0, :CLASSES]
-    fetches[6].wait()
-
-    for rows, tile, ref, tensors in momentum_rows(v_mid, v_in, v_out):
-        ref[tensors, tile] = v_own[rows, :]
-    rank = lax.axis_index('dp')
-    v_in0[...] = v_own[IN0:IN0 + 2, :]
-    v_short[...] = v_own[SHORT:SHORT + 8, :]
-    for q in range(7):
-        flat = jnp.zeros((1, LANES), F32)
-        for r in range(8):
-            d = CLASSES * r - LANES * q
-            if -CLASSES < d < LANES:
-                row = pltpu.roll(v_own[FC + r:FC + r + 1, :], d % LANES, 1)
-                flat = jnp.where((lane_row >= d) & (lane_row < d + CLASSES), row, flat)
-        size = min(LANES, 800 - LANES * q)
-        v_fc[pl.ds(LANES * q, size)] = flat[0, :size]
-    odd = lax.rem(rank, 2) == 1
-    for k in range(4):
-        here = v_own[BN + k:BN + k + 1, :]
-        after = v_own[BN + k + 1:BN + k + 2, :]
-        moved = jnp.where(lane_row < 64, pltpu.roll(here, 64, 1), pltpu.roll(after, 64, 1))
-        size = min(LANES, 448 - LANES * k)
-        v_bn[pl.ds(LANES * k, size)] = jnp.where(odd, moved, here)[0, :size]
-    v_bias[...] = pltpu.roll(v_own[BIAS:BIAS + 1, :], lax.rem(N_DEV - rank, N_DEV) * 4, 1)[0, :4]
-
+
+    last = []
+    for k, (src, dst) in enumerate(((n_bn, bn_out), (n_bias, bias_out))):
+        last.append(pltpu.make_async_copy(src, dst, sems.at[27 + k]))
+        last[-1].start()
     for k, (src, dst) in enumerate(((s_mid, n_mid), (t_mid, b_mid), (s_in, n_in), (t_in, b_in), (s_in0, n_in0),
                                     (t_in0, b_in0))):
         pltpu.make_async_copy(src, dst, sems.at[k]).wait()
@@ -716,11 +769,12 @@
             pltpu.make_async_copy(src.at[h], dst, sems.at[6 + k]).wait()
     pltpu.make_async_copy(s_fc, n_fc, sems.at[10]).wait()
     pltpu.make_async_copy(t_fc, b_fc, sems.at[11]).wait()
+    for copy in moved + last:
+        copy.wait()
 
 
 def unpack_weights(packed, v_own):
     any_ = pl.BlockSpec(memory_space=pl.ANY)
-    vm = pl.BlockSpec(memory_space=VMEM)
     bf = jnp.bfloat16
     kernels = ((N_MID, 576, 64), (N_IN, 64, 256), (64, 128), (N_OUT, 64, 256), (128, 256), (CLASSES, 256))
     shapes = [(s, F32) for s in kernels] + [((112, 128), F32), ((CLASSES,), F32)] + [(s, bf) for s in kernels]
@@ -730,9 +784,9 @@
         unpack_kernel,
         out_shape=[jax.ShapeDtypeStruct(s, d) for s, d in shapes],
         in_specs=[any_, any_],
-        out_specs=[any_] * 6 + [vm] * 2 + [any_] * 6 + [vm] * 8,
-        scratch_shapes=[VMEM((N_DEV * ROWS, LANES), F32), VMEM((ROWS, LANES), F32)] + [VMEM(s, F32) for s in scratch] + [VMEM(s, bf) for s in scratch]
-        + [VMEM((256, 128), F32), pltpu.SemaphoreType.DMA((19,))],
+        out_specs=[any_] * 22,
+        scratch_shapes=[VMEM(s, d) for s, d in shapes[6:8] + shapes[14:]] + [VMEM((N_DEV * ROWS, LANES), F32), VMEM((ROWS, LANES), F32)] + [VMEM(s, F32) for s in scratch] + [VMEM(s, bf) for s in scratch]
+        + [VMEM((256, 128), F32), pltpu.SemaphoreType.DMA((29,))],
         compiler_params=pltpu.CompilerParams(vmem_limit_bytes=VMEM_LIMIT),
     )(packed, v_own)
 

time: 75.6 us -> 74.2 us (0.981)
  Pallas kernels: 74 us -> 72.1 us
    pallas_call x1, Pallas kernels: 66.7 us -> 63.9 us  [exchange(): pl.pallas_call(exchange_kernel, out_shape=(jax.ShapeDtypeStruct((4, 2, 2,...]
    pallas_call x1, Pallas kernels: 7.3 us -> 8.18 us  [unpack_weights(): pl.pallas_call(unpack_kernel, out_shape=[jax.ShapeDtypeStruct(s, d) for s...]
where the time goes in v6:
time: 74.2 us; the launch traced here: 73.4 us
  Pallas kernels  72.1 us (97%)
  between operations  1.32 us (2%)
    pallas_call x1, Pallas kernels, exchange(): pl.pallas_call(exchange_kernel, out_shape=(jax.ShapeDtypeStruct((4, 2, 2,...  63.9 us
    pallas_call x1, Pallas kernels, unpack_weights(): pl.pallas_call(unpack_kernel, out_shape=[jax.ShapeDtypeStruct(s, d) for s...  8.18 us

profile of v6, /device:TPU:0, one launch (start us, length us, event | category | flops | bytes accessed | tf_op | source)
XLA Modules:
  0.0 73.4 jit_solution(9177161602763374924)
XLA Ops:
  1.3 63.9 %shard_map.408 = (f32[4,2,2,2,328,128]{5,4,3,2,1,0:T(8,128)}, f32[328,128]{1,0:T(8,128)}) custom-call(f32[1]{0:T(128)} %bitcast.31.lr, f32[18,576,64]{2,1,0:T(8,128)} %bitcast.33, f32[17,64,256]{2,1,0:T(8,128)} %bitcast.36, f32[64,128]{1,0:T(8,128)} %bitcast.43, f32[18,64,256]{2,1,0:T(8,128)} %bitcast.35, f32[128,256]{1,0:T(8,128)} %bitcast.39, ...), custom_call_target="tpu_custom_call" | custom-call | tf_op jit(solution)/shard_map/pallas_call | solution.py:583
  65.2 8.2 %shard_map.409 = (f32[18,576,64]{2,1,0:T(8,128)}, f32[17,64,256]{2,1,0:T(8,128)}, f32[64,128]{1,0:T(8,128)}, f32[18,64,256]{2,1,0:T(8,128)}, f32[128,256]{1,0:T(...) custom-call(f32[32,328,128]{2,1,0:T(8,128)} %bitcast.32, ...), custom_call_target="tpu_custom_call" | custom-call | tf_op jit(solution)/shard_map/pallas_call | solution.py:783

commit v7 on v6

--- a/solution.py
+++ b/solution.py
@@ -35,7 +35,7 @@
 )
 FIRST_NORMS = [step for step in STEPS if step[1] == 4][0]
 S_CORE, S_ONE, S_TWO, S_Z, A_Z, A_TWO, A_ONE, A_CORE, N_SEMS = 0, 2, 4, 6, 7, 8, 10, 12, 14
-VMEM_LIMIT = 60 * 2**20
+EXCHANGE_VMEM, UNPACK_VMEM = 30 * 2**20, 20 * 2**20
 
 
 def mid_row(t):
@@ -83,13 +83,13 @@
 def exchange_kernel(lr, g_mid, g_in, g_in0, g_out, g_short, g_bn, pooled, dlog_t,
                     w_mid, w_in, w_in0, w_out, w_short, w_fc, w_bn, w_bias,
                     v_mid, v_in, v_in0, v_out, v_short, v_fc, v_bn, v_bias,
-                    full_out, v_out_rows,
+                    full, v_new,
                     s_mid, s_in, s_in0, s_out, s_short, s_bn, s_x, s_d, xt, fct,
                     o_mid, o_in, o_in0, o_out, o_short, o_fc, o_bn, o_bias, ot,
                     p_mid, p_in, p_in0, p_out, p_short, p_fc, p_bn, p_bias,
-                    packed, w_own, v_own, v_new, full,
+                    packed, w_own, v_own,
                     got_core, acc, got_one, got_two, got_z, got_line, grad, layer_norms, norms,
-                    sems, out_sems, send, recv, n_send, n_recv):
+                    sems, send, recv, n_send, n_recv):
     rank = lax.axis_index('dp')
     core = lax.rem(rank, 2)
     x = lax.rem(rank // 2, 2)
@@ -352,7 +352,6 @@
         bias = jnp.concatenate([o_bias[...].reshape(1, CLASSES), jnp.zeros((1, LANES - CLASSES), F32)], axis=1)
         w_own[BIAS:BIAS + 1, :] = jnp.where((lane_row >= 4 * rank) & (lane_row < 4 * rank + 4), bias, 0.0)
 
-    outs = []
     sent = {}
 
     def start(c, k, src, dst, peer):
@@ -371,11 +370,6 @@
     def arrived(c, *numbers):
         for k in numbers:
             wait(c, k, recv)
-
-    def keep(src, dst):
-        copy = pltpu.make_async_copy(src, dst, out_sems.at[len(outs)])
-        copy.start()
-        outs.append(copy)
 
     def tell(k, row, peer):
         pltpu.make_async_remote_copy(src_ref=row, dst_ref=row, send_sem=n_send.at[k], recv_sem=n_recv.at[k],
@@ -511,7 +505,6 @@
             own = w_own[rows, :]
             moment = MOMENTUM * v_own[rows, :] + rate * (grad[rows, :] + decay * own)
             v_new[rows, :] = moment
-            keep(v_new.at[rows, :], v_out_rows.at[rows, :])
             mine = (row != BIAS) | ((lane >= 4 * rank) & (lane < 4 * rank + 4))
             full[z, y, x, core, rows, :] = jnp.where(mine, own - moment, 0.0)
             piece = full.at[z, y, x, core, rows, :]
@@ -534,7 +527,6 @@
             start(c, A_CORE, everything, everything, core_peer)
         elif stage == 10 and z_first:
             arrived(c, A_CORE)
-            keep(full.at[:, :, :, :, rows, :], full_out.at[:, :, :, :, rows, :])
         elif stage == 7:
             arrived(c, A_Z)
             for d in (1, 2, 3):
@@ -555,7 +547,6 @@
             start(c, A_CORE + 1, plane, plane, core_peer)
         else:
             arrived(c, A_CORE, A_CORE + 1)
-            keep(full.at[:, :, :, :, rows, :], full_out.at[:, :, :, :, rows, :])
 
     for c, stage in STEPS:
         if stage == 4 and (c, stage) == FIRST_NORMS:
@@ -565,12 +556,11 @@
         wait(c, k, send)
     for k in range(2 * len(CHUNKS)):
         told(k, n_send)
-    for copy in outs:
-        copy.wait()
 
 
 def exchange(operands):
-    any_ = pl.BlockSpec(memory_space=pl.ANY)
+    hbm = pl.BlockSpec(memory_space=pltpu.HBM)
+    vm = pl.BlockSpec(memory_space=VMEM)
     count = len(CHUNKS)
     bf = jnp.bfloat16
     shapes = [(N_MID, 576, 64), (N_IN, 64, 256), (64, 128), (2, N_OUT, 64, 128), (2, 128, 128), (112, 128)]
@@ -580,39 +570,31 @@
     exchanged = [(4, 2, 2) + rows, (4, 2, 2) + rows, (4, 2) + rows, (4,) + rows, (3,) + rows, (3, 2, 2) + rows, rows,
                  (count, 8, 1, LANES), (count, 4, 1, LANES)]
     dma = pltpu.SemaphoreType.DMA
+    placed = [pltpu.with_memory_space_constraint(operand, pltpu.HBM) for operand in operands[1:]]
     full, v_new = pl.pallas_call(
         exchange_kernel,
         out_shape=(jax.ShapeDtypeStruct((4, 2, 2, 2) + rows, F32), jax.ShapeDtypeStruct(rows, F32)),
-        in_specs=[pl.BlockSpec(memory_space=pltpu.SMEM)] + [any_] * 24,
-        out_specs=(any_, any_),
+        in_specs=[pl.BlockSpec(memory_space=pltpu.SMEM)] + [hbm] * 24,
+        out_specs=(vm, vm),
         scratch_shapes=[VMEM(s, F32) for s in shapes]
         + [VMEM((1024, 256), bf), VMEM((CLASSES, 1024), bf), VMEM((256, 128), F32), VMEM((128, 256), F32)]
         + [VMEM(s, F32) for s in own]
-        + [VMEM((4, 2, 2, 2) + rows, F32), VMEM(rows, F32), VMEM(rows, F32), VMEM(rows, F32),
-           VMEM((4, 2, 2, 2) + rows, F32)]
+        + [VMEM((4, 2, 2, 2) + rows, F32), VMEM(rows, F32), VMEM(rows, F32)]
         + [VMEM(s, F32) for s in exchanged]
-        + [dma((40,)), dma((2 * count,)), dma((count * N_SEMS,)), dma((count * N_SEMS,)), dma((2 * count,)), dma((2 * count,))],
-        compiler_params=pltpu.CompilerParams(vmem_limit_bytes=VMEM_LIMIT, collective_id=0, has_side_effects=True),
-    )(*operands)
-    return full.reshape(N_DEV, ROWS, LANES), v_new
-
-
-def unpack_kernel(packed_rows, v_rows, n_mid, n_in, n_in0, n_out, n_short, n_fc, bn_out, bias_out,
+        + [dma((40,)), dma((count * N_SEMS,)), dma((count * N_SEMS,)), dma((2 * count,)), dma((2 * count,))],
+        compiler_params=pltpu.CompilerParams(vmem_limit_bytes=EXCHANGE_VMEM, collective_id=0, has_side_effects=True),
+    )(operands[0], *placed)
+    return full.reshape(N_DEV * ROWS, LANES), v_new
+
+
+def unpack_kernel(packed, v_own, n_mid, n_in, n_in0, n_out, n_short, n_fc, bn_out, bias_out,
                   b_mid, b_in, b_in0, b_out, b_short, b_fc, *rest):
     v_outs, rest = rest[:8], rest[8:]
     n_bn, n_bias = rest[:2]
     (v_mid, v_in, v_in0, v_out, v_short, v_fc, v_bn, v_bias), rest = rest[2:10], rest[10:]
-    (packed, v_own, s_mid, s_in, s_out, s_short, s_in0, s_fc, t_mid, t_in, t_out, t_short, t_in0, t_fc, xt, sems) = rest
+    (s_mid, s_in, s_out, s_short, s_in0, s_fc, t_mid, t_in, t_out, t_short, t_in0, t_fc, xt, sems) = rest
     bf = jnp.bfloat16
     lane_row = lax.broadcasted_iota(jnp.int32, (1, LANES), 1)
-    pieces = packed.reshape(N_DEV, ROWS, LANES)
-    fetches = []
-    for k, (at, size) in enumerate(((0, 40), (40, 120), (160, 24), (184, 48), (232, 72), (304, 24))):
-        fetches.append(pltpu.make_async_copy(packed_rows.at[:, pl.ds(at, size), :], pieces.at[:, pl.ds(at, size), :],
-                                             sems.at[12 + k]))
-    fetches.append(pltpu.make_async_copy(v_rows, v_own, sems.at[18]))
-    for copy in fetches:
-        copy.start()
 
     def put(src, dst, k):
         pltpu.make_async_copy(src, dst, sems.at[k]).start()
@@ -628,9 +610,98 @@
         put(t_mid.at[t], b_mid.at[t], 1)
         return carry
 
-    fetches[0].wait()
-    lax.fori_loop(0, 4, mid_body, 0)
-    fetches[6].wait()
+    lax.fori_loop(0, N_MID, mid_body, 0)
+
+    def in_pair(first, second, row, other):
+        for a in range(4):
+            for k in range(4):
+                x = packed[across(a, row + k), :]
+                y = packed[across(a, other + k), :]
+                xt[pl.ds(64 * a + 2 * k, 8, stride=8), :] = left(x, y)
+                xt[pl.ds(64 * a + 2 * k + 1, 8, stride=8), :] = right(x, y)
+        for h in range(2):
+            cols = xt[128 * h:128 * h + 128, :].T
+            for u, t in enumerate((first, second)):
+                s_in[t, :, 128 * h:128 * h + 128] = cols[64 * u:64 * u + 64]
+                t_in[t, :, 128 * h:128 * h + 128] = cols[64 * u:64 * u + 64].astype(bf)
+        for t in (first, second):
+            put(s_in.at[t], n_in.at[t], 2)
+            put(t_in.at[t], b_in.at[t], 3)
+
+    def in_body(j, carry):
+        in_pair(2 * j + 5, 2 * j + 6, 184 + 8 * j, 188 + 8 * j)
+        return carry
+
+    lax.fori_loop(0, 6, in_body, 0)
+    in_pair(0, 1, in_row(0), in_row(1))
+    in_pair(2, 3, in_row(2), in_row(3))
+    for a in range(4):
+        for k in range(4):
+            x = packed[across(a, in_row(4) + k), :]
+            xt[pl.ds(64 * a + 2 * k, 8, stride=8), :] = x
+            xt[pl.ds(64 * a + 2 * k + 1, 8, stride=8), :] = right(x, x)
+    for h in range(2):
+        cols = xt[128 * h:128 * h + 128, :].T
+        s_in[4, :, 128 * h:128 * h + 128] = cols[:64]
+        t_in[4, :, 128 * h:128 * h + 128] = cols[:64].astype(bf)
+    put(s_in.at[4], n_in.at[4], 2)
+    put(t_in.at[4], b_in.at[4], 3)
+    for a in range(4):
+        for k in range(2):
+            x = packed[across(a, IN0 + k), :]
+            xt[pl.ds(32 * a + 2 * k, 8, stride=4), :] = x
+            xt[pl.ds(32 * a + 2 * k + 1, 8, stride=4), :] = right(x, x)
+    cols = xt[0:128, :].T
+    s_in0[...] = cols[:64]
+    t_in0[...] = cols[:64].astype(bf)
+    put(s_in0, n_in0, 4)
+    put(t_in0, b_in0, 5)
+
+    def out_body(t, carry):
+        for a in range(4):
+            for p in range(2):
+                for h in range(2):
+                    s_out[h, t, pl.ds(16 * a + p, 8, stride=2), :] = packed[across(a, OUT + 4 * t + 2 * p + h), :]
+        for h in range(2):
+            t_out[h, t] = s_out[h, t].astype(bf)
+            put(s_out.at[h, t], n_out.at[t, :, pl.ds(128 * h, 128)], 6)
+            put(t_out.at[h, t], b_out.at[t, :, pl.ds(128 * h, 128)], 7)
+        return carry
+
+    lax.fori_loop(0, N_OUT, out_body, 0)
+    for h in range(2):
+        for a in range(4):
+            for p in range(4):
+                s_short[h, pl.ds(32 * a + p, 8, stride=4), :] = packed[across(a, SHORT + 2 * p + h), :]
+        t_short[h] = s_short[h].astype(bf)
+        put(s_short.at[h], n_short.at[:, pl.ds(128 * h, 128)], 8)
+        put(t_short.at[h], b_short.at[:, pl.ds(128 * h, 128)], 9)
+    for i in range(N_DEV):
+        xt[8 * i:8 * i + 8, :] = packed[i * ROWS + FC:i * ROWS + FC + 8, :]
+    for h in range(2):
+        cols = xt[128 * h:128 * h + 128, :].T
+        s_fc[:, 128 * h:128 * h + 128] = cols[:CLASSES]
+        t_fc[:, 128 * h:128 * h + 128] = cols[:CLASSES].astype(bf)
+    put(s_fc, n_fc, 10)
+    put(t_fc, b_fc, 11)
+
+    lane = lax.broadcasted_iota(jnp.int32, (8, LANES), 1)
+    for b in range(2):
+        def even(k):
+            return packed[pl.ds(16 * b * ROWS + BN + k, 8, stride=2 * ROWS), :]
+
+        def odd(k):
+            return packed[pl.ds((16 * b + 1) * ROWS + BN + k, 8, stride=2 * ROWS), :]
+
+        for k in range(3):
+            n_bn[pl.ds(56 * b + k, 8, stride=7), :] = even(k)
+            n_bn[pl.ds(56 * b + 4 + k, 8, stride=7), :] = odd(1 + k)
+        n_bn[pl.ds(56 * b + 3, 8, stride=7), :] = jnp.where(lane < 64, even(3), odd(0))
+    total = packed[across(0, BIAS), :]
+    for a in range(1, 4):
+        total = total + packed[across(a, BIAS), :]
+    n_bias[...] = jnp.sum(total, axis=0, keepdims=True)[0, :CLASSES]
+
     for rows, tile, ref, tensors in momentum_rows(v_mid, v_in, v_out):
         ref[tensors, tile] = v_own[rows, :]
     rank = lax.axis_index('dp')
@@ -657,104 +728,6 @@
     moved = [pltpu.make_async_copy(src, dst, sems.at[19 + k]) for k, (src, dst) in enumerate(zip(momenta, v_outs))]
     for copy in moved:
         copy.start()
-    fetches[1].wait()
-    lax.fori_loop(4, 16, mid_body, 0)
-    fetches[2].wait()
-    lax.fori_loop(16, N_MID, mid_body, 0)
-    fetches[3].wait()
-
-    def in_pair(first, second, row, other):
-        for a in range(4):
-            for k in range(4):
-                x = packed[across(a, row + k), :]
-                y = packed[across(a, other + k), :]
-                xt[pl.ds(64 * a + 2 * k, 8, stride=8), :] = left(x, y)
-                xt[pl.ds(64 * a + 2 * k + 1, 8, stride=8), :] = right(x, y)
-        for h in range(2):
-            cols = xt[128 * h:128 * h + 128, :].T
-            for u, t in enumerate((first, second)):
-                s_in[t, :, 128 * h:128 * h + 128] = cols[64 * u:64 * u + 64]
-                t_in[t, :, 128 * h:128 * h + 128] = cols[64 * u:64 * u + 64].astype(bf)
-        for t in (first, second):
-            put(s_in.at[t], n_in.at[t], 2)
-            put(t_in.at[t], b_in.at[t], 3)
-
-    def in_body(j, carry):
-        in_pair(2 * j + 5, 2 * j + 6, 184 + 8 * j, 188 + 8 * j)
-        return carry
-
-    lax.fori_loop(0, 6, in_body, 0)
-    in_pair(0, 1, in_row(0), in_row(1))
-    in_pair(2, 3, in_row(2), in_row(3))
-    for a in range(4):
-        for k in range(4):
-            x = packed[across(a, in_row(4) + k), :]
-            xt[pl.ds(64 * a + 2 * k, 8, stride=8), :] = x
-            xt[pl.ds(64 * a + 2 * k + 1, 8, stride=8), :] = right(x, x)
-    for h in range(2):
-        cols = xt[128 * h:128 * h + 128, :].T
-        s_in[4, :, 128 * h:128 * h + 128] = cols[:64]
-        t_in[4, :, 128 * h:128 * h + 128] = cols[:64].astype(bf)
-    put(s_in.at[4], n_in.at[4], 2)
-    put(t_in.at[4], b_in.at[4], 3)
-    for a in range(4):
-        for k in range(2):
-            x = packed[across(a, IN0 + k), :]
-            xt[pl.ds(32 * a + 2 * k, 8, stride=4), :] = x
-            xt[pl.ds(32 * a + 2 * k + 1, 8, stride=4), :] = right(x, x)
-    cols = xt[0:128, :].T
-    s_in0[...] = cols[:64]
-    t_in0[...] = cols[:64].astype(bf)
-    put(s_in0, n_in0, 4)
-    put(t_in0, b_in0, 5)
-
-    def out_body(t, carry):
-        for a in range(4):
-            for p in range(2):
-                for h in range(2):
-                    s_out[h, t, pl.ds(16 * a + p, 8, stride=2), :] = packed[across(a, OUT + 4 * t + 2 * p + h), :]
-        for h in range(2):
-            t_out[h, t] = s_out[h, t].astype(bf)
-            put(s_out.at[h, t], n_out.at[t, :, pl.ds(128 * h, 128)], 6)
-            put(t_out.at[h, t], b_out.at[t, :, pl.ds(128 * h, 128)], 7)
-        return carry
-
-    fetches[4].wait()
-    lax.fori_loop(0, N_OUT, out_body, 0)
-    fetches[5].wait()
-    for h in range(2):
-        for a in range(4):
-            for p in range(4):
-                s_short[h, pl.ds(32 * a + p, 8, stride=4), :] = packed[across(a, SHORT + 2 * p + h), :]
-        t_short[h] = s_short[h].astype(bf)
-        put(s_short.at[h], n_short.at[:, pl.ds(128 * h, 128)], 8)
-        put(t_short.at[h], b_short.at[:, pl.ds(128 * h, 128)], 9)
-    for i in range(N_DEV):
-        xt[8 * i:8 * i + 8, :] = packed[i * ROWS + FC:i * ROWS + FC + 8, :]
-    for h in range(2):
-        cols = xt[128 * h:128 * h + 128, :].T
-        s_fc[:, 128 * h:128 * h + 128] = cols[:CLASSES]
-        t_fc[:, 128 * h:128 * h + 128] = cols[:CLASSES].astype(bf)
-    put(s_fc, n_fc, 10)
-    put(t_fc, b_fc, 11)
-
-    lane = lax.broadcasted_iota(jnp.int32, (8, LANES), 1)
-    for b in range(2):
-        def even(k):
-            return packed[pl.ds(16 * b * ROWS + BN + k, 8, stride=2 * ROWS), :]
-
-        def odd(k):
-            return packed[pl.ds((16 * b + 1) * ROWS + BN + k, 8, stride=2 * ROWS), :]
-
-        for k in range(3):
-            n_bn[pl.ds(56 * b + k, 8, stride=7), :] = even(k)
-            n_bn[pl.ds(56 * b + 4 + k, 8, stride=7), :] = odd(1 + k)
-        n_bn[pl.ds(56 * b + 3, 8, stride=7), :] = jnp.where(lane < 64, even(3), odd(0))
-    total = packed[across(0, BIAS), :]
-    for a in range(1, 4):
-        total = total + packed[across(a, BIAS), :]
-    n_bias[...] = jnp.sum(total, axis=0, keepdims=True)[0, :CLASSES]
-
     last = []
     for k, (src, dst) in enumerate(((n_bn, bn_out), (n_bias, bias_out))):
         last.append(pltpu.make_async_copy(src, dst, sems.at[27 + k]))
@@ -774,7 +747,8 @@
 
 
 def unpack_weights(packed, v_own):
-    any_ = pl.BlockSpec(memory_space=pl.ANY)
+    hbm = pl.BlockSpec(memory_space=pltpu.HBM)
+    vm = pl.BlockSpec(memory_space=VMEM)
     bf = jnp.bfloat16
     kernels = ((N_MID, 576, 64), (N_IN, 64, 256), (64, 128), (N_OUT, 64, 256), (128, 256), (CLASSES, 256))
     shapes = [(s, F32) for s in kernels] + [((112, 128), F32), ((CLASSES,), F32)] + [(s, bf) for s in kernels]
@@ -783,11 +757,11 @@
     return pl.pallas_call(
         unpack_kernel,
         out_shape=[jax.ShapeDtypeStruct(s, d) for s, d in shapes],
-        in_specs=[any_, any_],
-        out_specs=[any_] * 22,
-        scratch_shapes=[VMEM(s, d) for s, d in shapes[6:8] + shapes[14:]] + [VMEM((N_DEV * ROWS, LANES), F32), VMEM((ROWS, LANES), F32)] + [VMEM(s, F32) for s in scratch] + [VMEM(s, bf) for s in scratch]
+        in_specs=[vm, vm],
+        out_specs=[hbm] * 22,
+        scratch_shapes=[VMEM(s, d) for s, d in shapes[6:8] + shapes[14:]] + [VMEM(s, F32) for s in scratch] + [VMEM(s, bf) for s in scratch]
         + [VMEM((256, 128), F32), pltpu.SemaphoreType.DMA((29,))],
-        compiler_params=pltpu.CompilerParams(vmem_limit_bytes=VMEM_LIMIT),
+        compiler_params=pltpu.CompilerParams(vmem_limit_bytes=UNPACK_VMEM),
     )(packed, v_own)
 
 

time: 74.2 us -> 69.6 us (0.938)
  Pallas kernels: 72.1 us -> 68 us
    pallas_call x1, Pallas kernels: 8.18 us -> 5.55 us  [unpack_weights(): pl.pallas_call(unpack_kernel, out_shape=[jax.ShapeDtypeStruct(s, d) for s...]
    pallas_call x1, Pallas kernels: 63.9 us -> 62.5 us  [exchange(): pl.pallas_call(exchange_kernel, out_shape=(jax.ShapeDtypeStruct((4, 2, 2,...]
where the time goes in v7:
time: 69.6 us; the launch traced here: 69.4 us
  Pallas kernels  68 us (98%)
  between operations  1.32 us (2%)
    pallas_call x1, Pallas kernels, exchange(): pl.pallas_call(exchange_kernel, out_shape=(jax.ShapeDtypeStruct((4, 2, 2,...  62.5 us
    pallas_call x1, Pallas kernels, unpack_weights(): pl.pallas_call(unpack_kernel, out_shape=[jax.ShapeDtypeStruct(s, d) for s...  5.55 us

profile of v7, /device:TPU:0, one launch (start us, length us, event | category | flops | bytes accessed | tf_op | source)
XLA Modules:
  0.0 69.4 jit_solution(14827147302621199925)
XLA Ops:
  1.3 62.5 %shard_map.408 = (f32[4,2,2,2,328,128]{5,4,3,2,1,0:T(8,128)S(1)}, f32[328,128]{1,0:T(8,128)S(1)}) custom-call(f32[1]{0:T(128)} %bitcast.31.lr, f32[18,576,64]{2,1,0:T(8,128)} %bitcast.33, f32[17,64,256]{2,1,0:T(8,128)} %bitcast.36, f32[64,128]{1,0:T(8,128)} %bitcast.43, f32[18,64,256]{2,1,0:T(8,128)} %bitcast.35, f32[128,256]{1,0:T(8,128)} %bitcast.39, ...), custom_call_target="tpu_custom_call" | custom-call | tf_op jit(solution)/shard_map/pallas_call | solution.py:574
  63.8 5.6 %shard_map.409 = (f32[18,576,64]{2,1,0:T(8,128)}, f32[17,64,256]{2,1,0:T(8,128)}, f32[64,128]{1,0:T(8,128)}, f32[18,64,256]{2,1,0:T(8,128)}, f32[128,256]{1,0:T(...) custom-call(f32[10496,128]{1,0:T(8,128)S(1)} %bitcast.32, ...), custom_call_target="tpu_custom_call" | custom-call | tf_op jit(solution)/shard_map/pallas_call | solution.py:757

commit v8 on v7

--- a/solution.py
+++ b/solution.py
@@ -18,20 +18,20 @@
 VMEM = pltpu.VMEM
 MESH = pl.DeviceIdType.MESH
 CHUNKS = (
-    (0, 40, 'x'), (40, 40, 'y'), (80, 40, 'x'), (120, 40, 'y'), (160, 24, 'y'),
-    (184, 24, 'x'), (208, 24, 'zx'), (232, 24, 'y'), (256, 24, 'x'), (280, 24, 'zx'),
-    (304, 24, 'y'),
+    (0, 40, 'y'), (40, 40, 'x'), (80, 40, 'x'), (120, 40, 'y'), (160, 24, 'zx'),
+    (184, 24, 'y'), (208, 24, 'zx'), (232, 24, 'y'), (256, 24, 'y'), (280, 24, 'x'),
+    (304, 24, 'x'),
 )
 STEPS = (
-    (1, 0), (8, 0), (9, 0), (7, 0), (1, 1), (8, 1), (2, 0), (9, 1), (6, 0), (2, 1), (4, 0), (8, 2), (1, 2), (6, 1),
-    (7, 1), (3, 0), (0, 0), (2, 2), (0, 1), (3, 1), (8, 3), (7, 2), (1, 3), (10, 0), (2, 3), (0, 2), (9, 2), (5, 0),
-    (3, 2), (4, 1), (7, 3), (8, 4), (10, 1), (5, 1), (0, 3), (1, 4), (9, 3), (3, 3), (4, 2), (2, 4), (5, 2), (6, 2),
-    (7, 4), (8, 5), (10, 2), (4, 3), (9, 4), (6, 3), (1, 5), (5, 3), (0, 4), (2, 5), (10, 3), (3, 4), (8, 6), (7, 5),
-    (6, 4), (9, 5), (1, 6), (4, 4), (0, 5), (5, 4), (3, 5), (2, 6), (10, 4), (7, 6), (9, 6), (6, 5), (8, 7), (5, 5),
-    (4, 5), (1, 7), (0, 6), (9, 7), (10, 5), (3, 6), (2, 7), (7, 7), (4, 6), (6, 6), (1, 8), (8, 8), (5, 6), (2, 8),
-    (10, 6), (9, 8), (7, 8), (6, 7), (3, 7), (0, 7), (4, 7), (2, 9), (10, 7), (6, 8), (5, 7), (3, 8), (0, 8), (8, 9),
-    (4, 8), (7, 9), (9, 9), (2, 10), (5, 8), (1, 9), (10, 8), (1, 10), (3, 9), (0, 9), (3, 10), (4, 9), (9, 10),
-    (5, 9), (6, 9), (7, 10), (8, 10), (10, 9), (5, 10), (6, 10), (0, 10), (4, 10), (10, 10),
+    (7, 0), (1, 0), (4, 0), (7, 1), (3, 0), (1, 1), (4, 1), (3, 1), (9, 0), (6, 0), (5, 0), (8, 0), (9, 1), (0, 0),
+    (7, 2), (1, 2), (6, 1), (10, 0), (3, 2), (0, 1), (10, 1), (9, 2), (1, 3), (4, 2), (5, 1), (3, 3), (0, 2), (2, 0),
+    (10, 2), (7, 3), (2, 1), (9, 3), (8, 1), (0, 3), (1, 4), (5, 2), (4, 3), (10, 3), (3, 4), (6, 2), (2, 2), (7, 4),
+    (8, 2), (9, 4), (4, 4), (1, 5), (5, 3), (6, 3), (3, 5), (2, 3), (10, 4), (0, 4), (7, 5), (8, 3), (4, 5), (9, 5),
+    (1, 6), (6, 4), (10, 5), (3, 6), (5, 4), (0, 5), (2, 4), (7, 6), (8, 4), (6, 5), (9, 6), (4, 6), (1, 7), (5, 5),
+    (2, 5), (10, 6), (3, 7), (8, 5), (0, 6), (7, 7), (4, 7), (6, 6), (1, 8), (9, 7), (5, 6), (2, 6), (3, 8), (7, 8),
+    (8, 6), (6, 7), (4, 8), (0, 7), (1, 9), (10, 7), (3, 9), (5, 7), (2, 7), (8, 7), (9, 8), (6, 8), (7, 9), (0, 8),
+    (7, 10), (10, 8), (2, 8), (5, 8), (4, 9), (8, 8), (10, 9), (9, 9), (0, 9), (5, 9), (3, 10), (2, 9), (1, 10),
+    (4, 10), (8, 9), (6, 9), (0, 10), (9, 10), (5, 10), (10, 10), (2, 10), (8, 10), (6, 10),
 )
 FIRST_NORMS = [step for step in STEPS if step[1] == 4][0]
 S_CORE, S_ONE, S_TWO, S_Z, A_Z, A_TWO, A_ONE, A_CORE, N_SEMS = 0, 2, 4, 6, 7, 8, 10, 12, 14
@@ -83,11 +83,11 @@
 def exchange_kernel(lr, g_mid, g_in, g_in0, g_out, g_short, g_bn, pooled, dlog_t,
                     w_mid, w_in, w_in0, w_out, w_short, w_fc, w_bn, w_bias,
                     v_mid, v_in, v_in0, v_out, v_short, v_fc, v_bn, v_bias,
-                    full, v_new,
+                    full, m_mid, m_in, m_in0, m_out, m_short, m_fc, m_bn, m_bias,
                     s_mid, s_in, s_in0, s_out, s_short, s_bn, s_x, s_d, xt, fct,
                     o_mid, o_in, o_in0, o_out, o_short, o_fc, o_bn, o_bias, ot,
                     p_mid, p_in, p_in0, p_out, p_short, p_fc, p_bn, p_bias,
-                    packed, w_own, v_own,
+                    packed, w_own, v_own, v_new,
                     got_core, acc, got_one, got_two, got_z, got_line, grad, layer_norms, norms,
                     sems, send, recv, n_send, n_recv):
     rank = lax.axis_index('dp')
@@ -370,6 +370,29 @@
     def arrived(c, *numbers):
         for k in numbers:
             wait(c, k, recv)
+
+    def store_momentum():
+        for rows, tile, ref, tensors in momentum_rows(m_mid, m_in, m_out):
+            ref[tensors, tile] = v_new[rows, :]
+        m_in0[...] = v_new[IN0:IN0 + 2, :]
+        m_short[...] = v_new[SHORT:SHORT + 8, :]
+        for q in range(7):
+            flat = jnp.zeros((1, LANES), F32)
+            for r in range(8):
+                d = CLASSES * r - LANES * q
+                if -CLASSES < d < LANES:
+                    row = pltpu.roll(v_new[FC + r:FC + r + 1, :], d % LANES, 1)
+                    flat = jnp.where((lane_row >= d) & (lane_row < d + CLASSES), row, flat)
+            size = min(LANES, 800 - LANES * q)
+            m_fc[pl.ds(LANES * q, size)] = flat[0, :size]
+        odd = lax.rem(rank, 2) == 1
+        for k in range(4):
+            here = v_new[BN + k:BN + k + 1, :]
+            after = v_new[BN + k + 1:BN + k + 2, :]
+            turned = jnp.where(lane_row < 64, pltpu.roll(here, 64, 1), pltpu.roll(after, 64, 1))
+            size = min(LANES, 448 - LANES * k)
+            m_bn[pl.ds(LANES * k, size)] = jnp.where(odd, turned, here)[0, :size]
+        m_bias[...] = pltpu.roll(v_new[BIAS:BIAS + 1, :], lax.rem(N_DEV - rank, N_DEV) * 4, 1)[0, :4]
 
     def tell(k, row, peer):
         pltpu.make_async_remote_copy(src_ref=row, dst_ref=row, send_sem=n_send.at[k], recv_sem=n_recv.at[k],
@@ -551,6 +574,8 @@
     for c, stage in STEPS:
         if stage == 4 and (c, stage) == FIRST_NORMS:
             own_pieces()
+        if (c, stage) == STEPS[-3]:
+            store_momentum()
         step(c, stage)
     for c, k in sent:
         wait(c, k, send)
@@ -571,30 +596,32 @@
                  (count, 8, 1, LANES), (count, 4, 1, LANES)]
     dma = pltpu.SemaphoreType.DMA
     placed = [pltpu.with_memory_space_constraint(operand, pltpu.HBM) for operand in operands[1:]]
-    full, v_new = pl.pallas_call(
+    momenta = own[-8:]
+    full, *momenta = pl.pallas_call(
         exchange_kernel,
-        out_shape=(jax.ShapeDtypeStruct((4, 2, 2, 2) + rows, F32), jax.ShapeDtypeStruct(rows, F32)),
+        out_shape=[jax.ShapeDtypeStruct(s, F32) for s in [(4, 2, 2, 2) + rows] + momenta],
         in_specs=[pl.BlockSpec(memory_space=pltpu.SMEM)] + [hbm] * 24,
-        out_specs=(vm, vm),
+        out_specs=[vm] * 9,
         scratch_shapes=[VMEM(s, F32) for s in shapes]
         + [VMEM((1024, 256), bf), VMEM((CLASSES, 1024), bf), VMEM((256, 128), F32), VMEM((128, 256), F32)]
         + [VMEM(s, F32) for s in own]
-        + [VMEM((4, 2, 2, 2) + rows, F32), VMEM(rows, F32), VMEM(rows, F32)]
+        + [VMEM((4, 2, 2, 2) + rows, F32), VMEM(rows, F32), VMEM(rows, F32), VMEM(rows, F32)]
         + [VMEM(s, F32) for s in exchanged]
         + [dma((40,)), dma((count * N_SEMS,)), dma((count * N_SEMS,)), dma((2 * count,)), dma((2 * count,))],
         compiler_params=pltpu.CompilerParams(vmem_limit_bytes=EXCHANGE_VMEM, collective_id=0, has_side_effects=True),
     )(operands[0], *placed)
-    return full.reshape(N_DEV * ROWS, LANES), v_new
-
-
-def unpack_kernel(packed, v_own, n_mid, n_in, n_in0, n_out, n_short, n_fc, bn_out, bias_out,
-                  b_mid, b_in, b_in0, b_out, b_short, b_fc, *rest):
-    v_outs, rest = rest[:8], rest[8:]
-    n_bn, n_bias = rest[:2]
-    (v_mid, v_in, v_in0, v_out, v_short, v_fc, v_bn, v_bias), rest = rest[2:10], rest[10:]
+    return full.reshape(N_DEV * ROWS, LANES), momenta
+
+
+def unpack_kernel(packed, *rest):
+    momenta, rest = rest[:8], rest[8:]
+    (n_mid, n_in, n_in0, n_out, n_short, n_fc, bn_out, bias_out, b_mid, b_in, b_in0, b_out, b_short, b_fc) = rest[:14]
+    v_outs, (n_bn, n_bias), rest = rest[14:22], rest[22:24], rest[24:]
     (s_mid, s_in, s_out, s_short, s_in0, s_fc, t_mid, t_in, t_out, t_short, t_in0, t_fc, xt, sems) = rest
     bf = jnp.bfloat16
-    lane_row = lax.broadcasted_iota(jnp.int32, (1, LANES), 1)
+    moved = [pltpu.make_async_copy(src, dst, sems.at[19 + k]) for k, (src, dst) in enumerate(zip(momenta, v_outs))]
+    for copy in moved:
+        copy.start()
 
     def put(src, dst, k):
         pltpu.make_async_copy(src, dst, sems.at[k]).start()
@@ -702,32 +729,6 @@
         total = total + packed[across(a, BIAS), :]
     n_bias[...] = jnp.sum(total, axis=0, keepdims=True)[0, :CLASSES]
 
-    for rows, tile, ref, tensors in momentum_rows(v_mid, v_in, v_out):
-        ref[tensors, tile] = v_own[rows, :]
-    rank = lax.axis_index('dp')
-    v_in0[...] = v_own[IN0:IN0 + 2, :]
-    v_short[...] = v_own[SHORT:SHORT + 8, :]
-    for q in range(7):
-        flat = jnp.zeros((1, LANES), F32)
-        for r in range(8):
-            d = CLASSES * r - LANES * q
-            if -CLASSES < d < LANES:
-                row = pltpu.roll(v_own[FC + r:FC + r + 1, :], d % LANES, 1)
-                flat = jnp.where((lane_row >= d) & (lane_row < d + CLASSES), row, flat)
-        size = min(LANES, 800 - LANES * q)
-        v_fc[pl.ds(LANES * q, size)] = flat[0, :size]
-    odd = lax.rem(rank, 2) == 1
-    for k in range(4):
-        here = v_own[BN + k:BN + k + 1, :]
-        after = v_own[BN + k + 1:BN + k + 2, :]
-        turned = jnp.where(lane_row < 64, pltpu.roll(here, 64, 1), pltpu.roll(after, 64, 1))
-        size = min(LANES, 448 - LANES * k)
-        v_bn[pl.ds(LANES * k, size)] = jnp.where(odd, turned, here)[0, :size]
-    v_bias[...] = pltpu.roll(v_own[BIAS:BIAS + 1, :], lax.rem(N_DEV - rank, N_DEV) * 4, 1)[0, :4]
-    momenta = (v_mid, v_in, v_in0, v_out, v_short, v_fc, v_bn, v_bias)
-    moved = [pltpu.make_async_copy(src, dst, sems.at[19 + k]) for k, (src, dst) in enumerate(zip(momenta, v_outs))]
-    for copy in moved:
-        copy.start()
     last = []
     for k, (src, dst) in enumerate(((n_bn, bn_out), (n_bias, bias_out))):
         last.append(pltpu.make_async_copy(src, dst, sems.at[27 + k]))
@@ -746,7 +747,7 @@
         copy.wait()
 
 
-def unpack_weights(packed, v_own):
+def unpack_weights(packed, momenta):
     hbm = pl.BlockSpec(memory_space=pltpu.HBM)
     vm = pl.BlockSpec(memory_space=VMEM)
     bf = jnp.bfloat16
@@ -757,12 +758,12 @@
     return pl.pallas_call(
         unpack_kernel,
         out_shape=[jax.ShapeDtypeStruct(s, d) for s, d in shapes],
-        in_specs=[vm, vm],
+        in_specs=[vm] * 9,
         out_specs=[hbm] * 22,
-        scratch_shapes=[VMEM(s, d) for s, d in shapes[6:8] + shapes[14:]] + [VMEM(s, F32) for s in scratch] + [VMEM(s, bf) for s in scratch]
+        scratch_shapes=[VMEM(s, d) for s, d in shapes[6:8]] + [VMEM(s, F32) for s in scratch] + [VMEM(s, bf) for s in scratch]
         + [VMEM((256, 128), F32), pltpu.SemaphoreType.DMA((29,))],
         compiler_params=pltpu.CompilerParams(vmem_limit_bytes=UNPACK_VMEM),
-    )(packed, v_own)
+    )(packed, *momenta)
 
 
 def solution(mesh):

time: 69.6 us -> 71.1 us (1.022)
  Pallas kernels: 68 us -> 69.6 us
    pallas_call x1, Pallas kernels: 62.5 us -> 64.1 us  [exchange(): pl.pallas_call(exchange_kernel, out_shape=[jax.ShapeDtypeStruct(s, F32) f...]
where the time goes in v8:
time: 71.1 us; the launch traced here: 70.9 us
  Pallas kernels  69.6 us (98%)
  between operations  1.32 us (2%)
    pallas_call x1, Pallas kernels, exchange(): pl.pallas_call(exchange_kernel, out_shape=[jax.ShapeDtypeStruct(s, F32) f...  64.1 us
    pallas_call x1, Pallas kernels, unpack_weights(): pl.pallas_call(unpack_kernel, out_shape=[jax.ShapeDtypeStruct(s, d) for s...  5.49 us

profile of v8, /device:TPU:0, one launch (start us, length us, event | category | flops | bytes accessed | tf_op | source)
XLA Modules:
  0.0 70.9 jit_solution(14111868251374392797)
XLA Ops:
  1.3 64.1 %shard_map.408 = (f32[4,2,2,2,328,128]{5,4,3,2,1,0:T(8,128)S(1)}, f32[18,1152]{1,0:T(8,128)S(1)}, f32[17,512]{1,0:T(8,128)S(1)}, f32[2,128]{1,0:T(2,128)S(1)}, f...) custom-call(f32[1]{0:T(128)} %bitcast.31.lr, ...), custom_call_target="tpu_custom_call" | custom-call | tf_op jit(solution)/shard_map/pallas_call | solution.py:600
  65.4 5.5 %shard_map.409 = (f32[18,576,64]{2,1,0:T(8,128)}, f32[17,64,256]{2,1,0:T(8,128)}, f32[64,128]{1,0:T(8,128)}, f32[18,64,256]{2,1,0:T(8,128)}, f32[128,256]{1,0:T(...) custom-call(f32[10496,128]{1,0:T(8,128)S(1)} %bitcast.32, ...), custom_call_target="tpu_custom_call" | custom-call | tf_op jit(solution)/shard_map/pallas_call | solution.py:758

commit v9 on v8

--- a/solution.py
+++ b/solution.py
@@ -18,20 +18,20 @@
 VMEM = pltpu.VMEM
 MESH = pl.DeviceIdType.MESH
 CHUNKS = (
-    (0, 40, 'y'), (40, 40, 'x'), (80, 40, 'x'), (120, 40, 'y'), (160, 24, 'zx'),
-    (184, 24, 'y'), (208, 24, 'zx'), (232, 24, 'y'), (256, 24, 'y'), (280, 24, 'x'),
-    (304, 24, 'x'),
+    (0, 40, 'y'), (40, 40, 'zx'), (80, 40, 'y'), (120, 40, 'x'), (160, 24, 'x'),
+    (184, 48, 'y'), (232, 32, 'x'), (264, 24, 'x'), (288, 8, 'zx'), (296, 16, 'x'),
+    (312, 16, 'y'),
 )
 STEPS = (
-    (7, 0), (1, 0), (4, 0), (7, 1), (3, 0), (1, 1), (4, 1), (3, 1), (9, 0), (6, 0), (5, 0), (8, 0), (9, 1), (0, 0),
-    (7, 2), (1, 2), (6, 1), (10, 0), (3, 2), (0, 1), (10, 1), (9, 2), (1, 3), (4, 2), (5, 1), (3, 3), (0, 2), (2, 0),
-    (10, 2), (7, 3), (2, 1), (9, 3), (8, 1), (0, 3), (1, 4), (5, 2), (4, 3), (10, 3), (3, 4), (6, 2), (2, 2), (7, 4),
-    (8, 2), (9, 4), (4, 4), (1, 5), (5, 3), (6, 3), (3, 5), (2, 3), (10, 4), (0, 4), (7, 5), (8, 3), (4, 5), (9, 5),
-    (1, 6), (6, 4), (10, 5), (3, 6), (5, 4), (0, 5), (2, 4), (7, 6), (8, 4), (6, 5), (9, 6), (4, 6), (1, 7), (5, 5),
-    (2, 5), (10, 6), (3, 7), (8, 5), (0, 6), (7, 7), (4, 7), (6, 6), (1, 8), (9, 7), (5, 6), (2, 6), (3, 8), (7, 8),
-    (8, 6), (6, 7), (4, 8), (0, 7), (1, 9), (10, 7), (3, 9), (5, 7), (2, 7), (8, 7), (9, 8), (6, 8), (7, 9), (0, 8),
-    (7, 10), (10, 8), (2, 8), (5, 8), (4, 9), (8, 8), (10, 9), (9, 9), (0, 9), (5, 9), (3, 10), (2, 9), (1, 10),
-    (4, 10), (8, 9), (6, 9), (0, 10), (9, 10), (5, 10), (10, 10), (2, 10), (8, 10), (6, 10),
+    (5, 0), (6, 0), (1, 0), (5, 1), (6, 1), (3, 0), (7, 0), (1, 1), (2, 0), (3, 1), (0, 0), (6, 2), (5, 2), (8, 0),
+    (7, 1), (0, 1), (10, 0), (3, 2), (6, 3), (2, 1), (5, 3), (0, 2), (4, 0), (4, 1), (3, 3), (6, 4), (0, 3), (7, 2),
+    (1, 2), (8, 1), (2, 2), (4, 2), (9, 0), (10, 1), (5, 4), (9, 1), (7, 3), (1, 3), (3, 4), (6, 5), (4, 3), (10, 2),
+    (2, 3), (0, 4), (9, 2), (1, 4), (5, 5), (8, 2), (10, 3), (6, 6), (7, 4), (4, 4), (8, 3), (0, 5), (9, 3), (1, 5),
+    (3, 5), (5, 6), (2, 4), (8, 4), (10, 4), (4, 5), (7, 5), (0, 6), (9, 4), (6, 7), (2, 5), (3, 6), (1, 6), (5, 7),
+    (10, 5), (7, 6), (9, 5), (6, 8), (8, 5), (4, 6), (1, 7), (0, 7), (2, 6), (5, 8), (10, 6), (6, 9), (3, 7), (9, 6),
+    (1, 8), (8, 6), (4, 7), (7, 7), (2, 7), (8, 7), (3, 8), (0, 8), (5, 9), (9, 7), (5, 10), (6, 10), (2, 8), (10, 7),
+    (8, 8), (7, 8), (4, 8), (9, 8), (0, 9), (10, 8), (1, 9), (7, 9), (0, 10), (3, 9), (2, 9), (4, 9), (8, 9), (10, 9),
+    (9, 9), (4, 10), (7, 10), (1, 10), (3, 10), (2, 10), (10, 10), (8, 10), (9, 10),
 )
 FIRST_NORMS = [step for step in STEPS if step[1] == 4][0]
 S_CORE, S_ONE, S_TWO, S_Z, A_Z, A_TWO, A_ONE, A_CORE, N_SEMS = 0, 2, 4, 6, 7, 8, 10, 12, 14

time: 71.1 us -> 70.9 us (level)
  no operation moved by 1% of the time
where the time goes in v9:
time: 70.9 us; the launch traced here: 70.7 us
  Pallas kernels  69.3 us (98%)
  between operations  1.32 us (2%)
    pallas_call x1, Pallas kernels, exchange(): pl.pallas_call(exchange_kernel, out_shape=[jax.ShapeDtypeStruct(s, F32) f...  63.9 us
    pallas_call x1, Pallas kernels, unpack_weights(): pl.pallas_call(unpack_kernel, out_shape=[jax.ShapeDtypeStruct(s, d) for s...  5.49 us

profile of v9, /device:TPU:0, one launch (start us, length us, event | category | flops | bytes accessed | tf_op | source)
XLA Modules:
  0.0 70.7 jit_solution(11374735739657899469)
XLA Ops:
  1.3 63.9 %shard_map.408 = (f32[4,2,2,2,328,128]{5,4,3,2,1,0:T(8,128)S(1)}, f32[18,1152]{1,0:T(8,128)S(1)}, f32[17,512]{1,0:T(8,128)S(1)}, f32[2,128]{1,0:T(2,128)S(1)}, f...) custom-call(f32[1]{0:T(128)} %bitcast.31.lr, ...), custom_call_target="tpu_custom_call" | custom-call | tf_op jit(solution)/shard_map/pallas_call | solution.py:600
  65.2 5.5 %shard_map.409 = (f32[18,576,64]{2,1,0:T(8,128)}, f32[17,64,256]{2,1,0:T(8,128)}, f32[64,128]{1,0:T(8,128)}, f32[18,64,256]{2,1,0:T(8,128)}, f32[128,256]{1,0:T(...) custom-call(f32[10496,128]{1,0:T(8,128)S(1)} %bitcast.32, ...), custom_call_target="tpu_custom_call" | custom-call | tf_op jit(solution)/shard_map/pallas_call | solution.py:758
